TPU v7x, 32 devices: a whole 2x2x4 slice. The times are simulated.
32 devices in a mesh: wave: 4 (over x, core), band: 8 (over z, y).
Axes of the slice: x: 2, y: 2, z: 4, core: 2. Of those that a mesh axis runs over, the one named last changes fastest.
Arguments:
- control: float32 [256, 224, 192], P('band', 'wave'), may hold values from -6 to 6
- spectral_scale: float32 [256, 224, 192], P('band', 'wave'), may hold values from 0.3 to 3
- vertical_root: float32 [96, 96], replicated, may hold values from -0.625 to 0.625
- legendre: float32 [224, 448, 256], P('wave'), may hold values from -0.375 to 0.375
- zonal_number: int32 [224], replicated, may hold values from 0 to 223, each once
- courant: float32 [448, 96, 1024], P('band', None, 'wave'), may hold values from 0.05 to 0.9
- lidar_coef: float32 [12], replicated, may hold values from 0.2 to 1
- aod_coef: float32 [96], replicated, may hold values from 0.02 to 0.2
- obs_count: int32 [32, 32], P(('wave', 'band')), may hold values from 0 to 128, as said below
- obs_column: int32 [1024, 128], P(('wave', 'band')), may hold values from 0 to 14335
- obs_level: int32 [1024, 128], P(('wave', 'band')), may hold values from 0 to 7
- lidar_obs: float32 [1024, 128], P(('wave', 'band')), may hold values from -6 to 6
- aod_obs: float32 [1024, 128], P(('wave', 'band')), may hold values from -6 to 6
- obs_weight: float32 [1024, 128], P(('wave', 'band')), may hold values from 0.5 to 2
Outputs:
- gradient: float32 [256, 224, 192], P('band', 'wave')
- state_increment: float32 [448, 96, 1024], P('band', None, 'wave')
Inputs may be any that keep to these rules, and one draw needn't show every extreme that they name: `obs_count`: live slots from a device to an owner; in every draw one owner receives 128 from every device. `zonal_number`: each number of 0 to 223 once.
All inputs are finite; a program needn't handle non-finite values.
Results may differ from a plain program's by a relative error of at most 0.0003.
Values sent between devices are 32-bit elements; how exact they have to be, the bound alone decides.
A program may use at most 128 MiB of HBM per device.

v0:
```python
import math

import jax
import jax.numpy as jnp
from jax import lax
from jax.experimental import pallas as pl
from jax.experimental.pallas import tpu as pltpu
from jax.sharding import PartitionSpec as P

MW = 224
LEV = 8
BINS = 12
STEPS = 4


highest = lax.Precision.HIGHEST
high = lax.Precision.HIGH


def trig_tables(numbers, lon_first, lon_count, lon_total, factor):
    longitudes = lon_first + jnp.arange(lon_count, dtype=jnp.int32)
    phases = numbers[:, None] * longitudes[None, :] % lon_total
    angles = phases.astype(jnp.float32) * (2.0 * math.pi / lon_total)
    return (jnp.cos(angles) * factor, jnp.sin(angles) * factor)


def settle_kernel(bins, tracer_ref, courant_ref, proj_ref, out_ref, model_ref):
    tracer = tracer_ref[0]
    courant = courant_ref[0]
    row = lax.broadcasted_iota(jnp.int32, tracer.shape, 0)
    for repeat in range(STEPS):
        outflow = courant * tracer
        inflow = jnp.where(row >= bins, pltpu.roll(outflow, bins, 0), 0.0)
        tracer = tracer - outflow + inflow
    out_ref[0] = tracer
    model_ref[0] = jnp.dot(proj_ref[...], tracer, precision=highest, preferred_element_type=jnp.float32)


def settle_adjoint_kernel(bins, resid_ref, courant_ref, proj_ref, out_ref):
    courant = courant_ref[0]
    adjoint = jnp.dot(proj_ref[...], resid_ref[0], precision=highest, preferred_element_type=jnp.float32)
    channels = adjoint.shape[0]
    row = lax.broadcasted_iota(jnp.int32, adjoint.shape, 0)
    for repeat in range(STEPS):
        below = jnp.where(row < channels - bins, pltpu.roll(adjoint, channels - bins, 0), 0.0)
        adjoint = adjoint + courant * (below - adjoint)
    out_ref[0] = adjoint


def per_lat(rows, cols):
    return pl.BlockSpec((1, rows, cols), lambda t: (t, 0, 0))


def whole(rows, cols):
    return pl.BlockSpec((rows, cols), lambda t: (0, 0))


def settle_forward(tracer, courant, proj, bins):
    lats, channels, lons = tracer.shape
    rows = proj.shape[0]
    return pl.pallas_call(
        lambda *refs: settle_kernel(bins, *refs),
        grid=(lats,),
        in_specs=[per_lat(channels, lons), per_lat(channels, lons), whole(rows, channels)],
        out_specs=[per_lat(channels, lons), per_lat(rows, lons)],
        out_shape=[
            jax.ShapeDtypeStruct((lats, channels, lons), jnp.float32),
            jax.ShapeDtypeStruct((lats, rows, lons), jnp.float32),
        ],
        name="settle_forward",
    )(tracer, courant, proj)


def settle_backward(resid, courant, proj_t, bins):
    lats, channels, lons = courant.shape
    rows = proj_t.shape[1]
    return pl.pallas_call(
        lambda *refs: settle_adjoint_kernel(bins, *refs),
        grid=(lats,),
        in_specs=[per_lat(rows, lons), per_lat(channels, lons), whole(channels, rows)],
        out_specs=per_lat(channels, lons),
        out_shape=jax.ShapeDtypeStruct((lats, channels, lons), jnp.float32),
        name="settle_backward",
    )(resid, courant, proj_t)


def synthesis_sum(cosine, sine_table, parts):
    return jnp.einsum("mo,mtc->tco", cosine, parts[..., 0], precision=high) - jnp.einsum(
        "mo,mtc->tco", sine_table, parts[..., 1], precision=high
    )


def analysis(cosine, sine_table, field):
    real_adj = jnp.einsum("mo,tco->mtc", cosine, field, precision=high)
    imag_adj = -jnp.einsum("mo,tco->mtc", sine_table, field, precision=high)
    stacked = jnp.stack([real_adj, imag_adj], axis=-1)
    return stacked.reshape(stacked.shape[0], stacked.shape[1], -1)


def body(
    control,
    spectral_scale,
    vertical_root,
    legendre,
    zonal_number,
    courant,
    lidar_coef,
    aod_coef,
    obs_count,
    obs_column,
    obs_level,
    lidar_obs,
    aod_obs,
    obs_weight,
):
    modes_here, waves_here, width = control.shape
    channels = width // 2
    wave_count = lax.axis_size("wave")
    band_count = lax.axis_size("band")
    lat_here = legendre.shape[1] // band_count
    lon_here = courant.shape[2]
    lon_total = lon_here * wave_count
    lon_first = lax.axis_index("wave") * lon_here
    factor = MW ** (-0.5)
    slot_count = obs_column.shape[1]
    live = jnp.arange(slot_count, dtype=jnp.int32)[None, :] < obs_count.reshape(-1, 1)
    packet = jnp.stack(
        [
            obs_column.astype(jnp.float32),
            obs_level.astype(jnp.float32),
            lidar_obs,
            aod_obs,
            jnp.where(live, obs_weight, 0.0),
        ],
        axis=1,
    )
    arrived = lax.all_to_all(packet, ("wave", "band"), split_axis=0, concat_axis=0, tiled=True)
    columns, levels, lidar_vals, aod_vals, weights = [arrived[:, i].reshape(-1) for i in range(5)]
    columns = columns.astype(jnp.int32)
    levels = levels.astype(jnp.int32)
    paired = control.reshape(modes_here, waves_here, channels, 2)
    mixed = jnp.einsum("nmcp,cd->nmdp", paired, vertical_root, precision=high).reshape(
        modes_here, waves_here, width
    )
    scaled = spectral_scale * mixed
    all_modes = lax.all_to_all(scaled, "band", split_axis=2, concat_axis=0, tiled=True)
    every_lat = jnp.einsum("mln,nmc->mlc", legendre, all_modes, precision=high)
    spectral = lax.all_to_all(every_lat, "band", split_axis=1, concat_axis=2, tiled=True)
    shard_piece = lax.all_gather(spectral, "wave", axis=0, tiled=True)
    numbers = zonal_number
    cosine, sine_table = trig_tables(numbers, lon_first, lon_here, lon_total, factor)
    parts = shard_piece.reshape(shard_piece.shape[0], lat_here, channels, 2)
    tracer = synthesis_sum(cosine, sine_table, parts)
    bins = lidar_coef.shape[0]
    levels_here = channels // bins
    proj_rows = -(-(levels_here + 1) // 8) * 8
    level_of = jnp.arange(channels, dtype=jnp.int32) // bins
    in_level = jnp.arange(levels_here, dtype=jnp.int32)[:, None] == level_of[None, :]
    proj = jnp.concatenate(
        [
            jnp.where(in_level, jnp.tile(lidar_coef, levels_here)[None, :], 0.0),
            aod_coef[None, :],
            jnp.zeros((proj_rows - levels_here - 1, channels), jnp.float32),
        ],
        axis=0,
    )
    tracer, model = settle_forward(tracer, courant, proj, bins)
    lat_index = columns // lon_here
    lon_hot = (columns % lon_here)[:, None] == jnp.arange(lon_here, dtype=jnp.int32)[None, :]
    lat_hot = (lat_index[:, None] == jnp.arange(lat_here, dtype=jnp.int32)[None, :]).astype(jnp.float32)
    cell = lat_index * levels_here + levels
    cell_hot = (
        cell[:, None] == jnp.arange(lat_here * levels_here, dtype=jnp.int32)[None, :]
    ).astype(jnp.float32)
    lidar_field = model[:, :levels_here].reshape(lat_here * levels_here, lon_here)
    aod_field = model[:, levels_here]
    lidar_rows = jnp.dot(cell_hot, lidar_field, precision=highest)
    aod_rows = jnp.dot(lat_hot, aod_field, precision=highest)
    lidar_model = jnp.sum(jnp.where(lon_hot, lidar_rows, 0.0), axis=1)
    aod_model = jnp.sum(jnp.where(lon_hot, aod_rows, 0.0), axis=1)
    lidar_resid = weights * (lidar_model - lidar_vals)
    aod_resid = weights * (aod_model - aod_vals)
    lidar_sum = lax.dot_general(
        cell_hot, jnp.where(lon_hot, lidar_resid[:, None], 0.0), (((0,), (0,)), ((), ())), precision=highest
    )
    aod_sum = lax.dot_general(
        lat_hot, jnp.where(lon_hot, aod_resid[:, None], 0.0), (((0,), (0,)), ((), ())), precision=highest
    )
    resid = jnp.concatenate(
        [
            lidar_sum.reshape(lat_here, levels_here, lon_here),
            aod_sum[:, None, :],
            jnp.zeros((lat_here, proj_rows - levels_here - 1, lon_here), jnp.float32),
        ],
        axis=1,
    )
    adjoint = settle_backward(resid, courant, proj.T, bins)
    numbers = zonal_number
    cosine, sine_table = trig_tables(numbers, lon_first, lon_here, lon_total, factor)
    spectral_adj = lax.psum_scatter(
        analysis(cosine, sine_table, adjoint), "wave", scatter_dimension=0, tiled=True
    )
    all_lats = lax.all_to_all(spectral_adj, "band", split_axis=2, concat_axis=1, tiled=True)
    mode_block = jnp.einsum("mtn,mtc->nmc", legendre, all_lats, precision=high)
    scaled_adj = lax.all_to_all(mode_block, "band", split_axis=0, concat_axis=2, tiled=True)
    mixed_adj = (spectral_scale * scaled_adj).reshape(modes_here, waves_here, channels, 2)
    control_adj = jnp.einsum("nmdp,cd->nmcp", mixed_adj, vertical_root, precision=high).reshape(
        modes_here, waves_here, width
    )
    return (control + control_adj, tracer)


def solution(mesh):
    return jax.shard_map(
        body,
        mesh=mesh,
        in_specs=(
            P("band", "wave", None),
            P("band", "wave", None),
            P(),
            P("wave", None, None),
            P(),
            P("band", None, "wave"),
            P(),
            P(),
            P(("wave", "band"), None),
            P(("wave", "band"), None),
            P(("wave", "band"), None),
            P(("wave", "band"), None),
            P(("wave", "band"), None),
            P(("wave", "band"), None),
        ),
        out_specs=(P("band", "wave", None), P("band", None, "wave")),
        check_vma=False,
    )
```

profile of v0, /device:TPU:0, one launch (start us, length us, event | category | flops | bytes accessed | tf_op | source)
XLA Modules:
  0.0 775.0 jit_solution(4632066076831188701)
XLA Ops:
  7.2 3.1 copy.152
  10.4 5.9 fusion.25
  16.3 4.7 copy.129
  20.9 3.8 copy.130
  24.7 3.6 bitcast_multiply_fusion
  28.3 4.5 reshape.131
  32.8 40.9 %all_to_all.77 = f32[8,1,43008]{2,1,0:T(1,128)S(1)} all-to-all(f32[8,1,43008]{2,1,0:T(1,128)} %reshape.131), channel_id=1, replica_groups=mesh['wave'=4,'band'=8] {'band'}, dimensions={0} | all-to-all | bytes 2752512 | tf_op jit(solution)/shard_map/all_to_all | solution.py:146
  73.7 0.5 broadcast.172
  74.2 5.4 reduce
  79.6 4.2 reshape.132
  83.7 3.5 copy.132
  87.2 3.2 copy.133
  90.4 17.4 %convolution_bitcast_fusion.1 = f32[56,448,24]{1,2,0:T(8,128)S(1)} fusion(f32[256,56,24]{0,2,1:T(8,128)} %copy.133, f32[56,448,256]{2,1,0:T(8,128)} %param.17), kind=kOutput, calls=%fused_computation.32 | convolution fusion | flops 924844032 | bytes 29474816 | tf_op jit(solution)/shard_map/mln,nmc->mlc/dot_general | solution.py:147
  107.8 4.0 copy.134
  111.9 9.4 %reshape.133 = f32[8,1,75264]{2,1,0:T(1,128)} reshape(f32[448,24,56]{2,1,0:T(8,128)} %bitcast.105) | data formatting | bytes 4816896
  121.2 59.0 %all_to_all.78 = f32[8,1,75264]{2,1,0:T(1,128)S(1)} all-to-all(f32[8,1,75264]{2,1,0:T(1,128)} %reshape.133), channel_id=1, replica_groups=mesh['wave'=4,'band'=8] {'band'}, dimensions={0} | all-to-all | bytes 4816896 | tf_op jit(solution)/shard_map/all_to_all | solution.py:148
  180.3 8.4 %reduce.1 = f32[8,75264]{1,0:T(8,128)} reduce(f32[8,1,75264]{2,1,0:T(1,128)S(1)} %all_to_all.78, f32[]{:T(128)} %broadcast.172), dimensions={1}, to_apply=%all_to_all.60.reduce_sub_computation | reduce | bytes 4816900 | tf_op jit(solution)/shard_map/all_to_all | solution.py:148
  188.7 9.1 %reshape.134 = f32[448,24,56]{2,1,0:T(8,128)} reshape(f32[8,75264]{1,0:T(8,128)} %reduce.1) | data formatting | bytes 4816896
  197.8 6.6 copy.135
  204.5 6.3 copy.136
  211.0 0.8 stack.32
  211.7 2.8 all-to-all-start
  214.8 0.7 copy.140
  215.6 6.8 all-to-all-done
  222.4 70.3 %all-gather.2.cloned.1.call-done = f32[224,56,192]{2,1,0:T(8,128)} async-done(((f32[56,56,192]{2,1,0:T(8,128)}), f32[224,56,192]{2,1,0:T(8,128)}) %all-gather.2.cloned.1.call-update) | async-done | bytes 9633808 | tf_op jit(solution)/shard_map/all_gather | solution.py:149
  292.7 14.6 %copy.137 = f32[224,56,192]{0,1,2:T(8,128)} copy(f32[224,56,192]{2,1,0:T(8,128)} %all-gather.2.cloned.1.call-done) | data formatting | bytes 19267584 | tf_op jit(solution)/shard_map/all_gather | solution.py:149
  307.4 5.0 fusion.85
  312.3 4.7 fusion.2
  317.0 7.1 fusion.16.refs_0_
  324.2 34.8 %settle_forward.1 = (f32[56,96,256]{2,1,0:T(8,128)}, f32[56,16,256]{2,1,0:T(8,128)}) custom-call(f32[56,96,256]{2,1,0:T(8,128)} %fusion.16.refs_0_, f32[56,96,256]{2,1,0:T(8,128)} %refs_1_.3, f32[16,96]{1,0:T(8,128)} %copy-done.5), custom_call_target="tpu_custom_call" | custom-call | tf_op jit(solution)/shard_map/settle_forward/pallas_call | solution.py:61
  359.0 1.0 slice.34
  360.0 6.9 fusion.24
  366.9 2.1 fusion.23
  369.1 2.7 fusion.7
  371.8 5.8 fusion.31
  377.6 1.1 maximum_maximum_fusion.refs_0_
  378.8 36.5 %settle_backward.1 = f32[56,96,256]{2,1,0:T(8,128)} custom-call(f32[56,16,256]{2,1,0:T(8,128)} %maximum_maximum_fusion.refs_0_, f32[56,96,256]{2,1,0:T(8,128)} %refs_1_.3, f32[96,16]{1,0:T(8,128)} %bitcast.114), custom_call_target="tpu_custom_call" | custom-call | tf_op jit(solution)/shard_map/settle_backward/pallas_call | solution.py:77
  415.3 8.4 %negate_bitcast_fusion = f32[224,56,96,1]{0,2,1,3:T(8,128)} fusion(f32[56,96,256]{2,1,0:T(8,128)} %settle_backward.1, s32[256]{0:T(256)S(1)} %iota_add_fusion, s32[224]{0:T(256)S(1)} %copy-done.6), kind=kOutput, calls=%fused_computation.8 | convolution fusion | flops 1851752448 | bytes 10323840 | tf_op jit(solution)/shard_map/mo,tco->mtc/dot_general | solution.py:95
  423.7 5.6 convolution_bitcast_fusion
  429.3 5.9 pad_maximum_fusion
  435.2 10.6 %copy.141 = f32[224,56,96,2]{0,1,3,2:T(8,128)} copy(f32[224,56,96,2]{0,2,1,3:T(8,128)S(1)} %pad_maximum_fusion) | data formatting | bytes 19267584 | tf_op jit(solution)/shard_map/stack | solution.py:96
  445.8 15.3 %copy.142 = f32[224,56,192]{2,1,0:T(8,128)} copy(f32[224,56,192]{0,1,2:T(8,128)} %bitcast.100) | data formatting | bytes 19267584 | tf_op jit(solution)/shard_map/reshape | solution.py:97
  461.2 101.5 %reduce-scatter.2.cloned.1.call-done = f32[56,56,192]{2,1,0:T(8,128)} async-done(((f32[224,56,192]{2,1,0:T(8,128)}), f32[56,56,192]{2,1,0:T(8,128)}) %reduce-scatter.2.cloned.1.call-update) | async-done | bytes 2408464 | tf_op jit(solution)/shard_map/reduce_scatter | solution.py:200
  562.7 6.2 copy.143
  568.9 9.4 %reshape.135 = f32[8,1,75264]{2,1,0:T(1,128)} reshape(f32[192,56,56]{2,1,0:T(8,128)} %bitcast.106) | data formatting | bytes 4816896
  578.3 61.0 %all_to_all.79 = f32[8,1,75264]{2,1,0:T(1,128)S(1)} all-to-all(f32[8,1,75264]{2,1,0:T(1,128)} %reshape.135), channel_id=1, replica_groups=mesh['wave'=4,'band'=8] {'band'}, dimensions={0} | all-to-all | bytes 4816896 | tf_op jit(solution)/shard_map/all_to_all | solution.py:203
  639.3 8.4 %reduce.2 = f32[8,75264]{1,0:T(8,128)} reduce(f32[8,1,75264]{2,1,0:T(1,128)S(1)} %all_to_all.79, f32[]{:T(128)} %broadcast.172), dimensions={1}, to_apply=%all_to_all.64.reduce_sub_computation | reduce | bytes 4816900 | tf_op jit(solution)/shard_map/all_to_all | solution.py:203
  647.7 9.1 %reshape.136 = f32[192,56,56]{2,1,0:T(8,128)} reshape(f32[8,75264]{1,0:T(8,128)} %reduce.2) | data formatting | bytes 4816896
  656.8 8.4 %copy.145 = f32[56,8,56,24]{2,1,3,0:T(8,128)} copy(f32[56,8,56,24]{2,0,3,1:T(8,128)} %bitcast.104) | data formatting | bytes 4816896 | tf_op jit(solution)/shard_map/all_to_all | solution.py:203
  665.2 4.0 all_to_all.67
  669.1 12.6 %convolution_bitcast_fusion.2 = f32[256,56,24]{0,2,1:T(8,128)} fusion(f32[56,448,24]{1,2,0:T(8,128)S(1)} %all_to_all.67, f32[56,448,256]{2,1,0:T(8,128)} %param.17), kind=kOutput, calls=%fused_computation.37 | convolution fusion | flops 924844032 | bytes 29474816 | tf_op jit(solution)/shard_map/mtn,mtc->nmc/dot_general | solution.py:204
  681.8 2.2 copy.146
  684.0 4.5 reshape.137
  688.5 36.5 %all_to_all.80 = f32[8,1,43008]{2,1,0:T(1,128)S(1)} all-to-all(f32[8,1,43008]{2,1,0:T(1,128)} %reshape.137), channel_id=1, replica_groups=mesh['wave'=4,'band'=8] {'band'}, dimensions={0} | all-to-all | bytes 2752512 | tf_op jit(solution)/shard_map/all_to_all | solution.py:205
  725.0 5.4 reduce.3
  730.4 4.2 reshape.138
  734.6 2.0 copy.147
  736.6 3.6 copy.148
  740.3 3.0 mul.74
  743.2 4.1 copy.149
  747.3 7.9 %fusion.28 = f32[32,56,96,2]{2,1,3,0:T(8,128)} fusion(f32[32,56,96,2]{1,0,3,2:T(8,128)} %bitcast.112, f32[96,96]{1,0:T(8,128)S(1)} %copy-done), kind=kOutput, calls=%fused_computation.36 | convolution fusion | flops 198180864 | bytes 2789376 | tf_op jit(solution)/shard_map/nmdp,cd->nmcp/dot_general | solution.py:207
  755.2 4.7 copy.151
  759.8 4.3 bitcast_add_fusion
  764.1 3.8 copy.153
  (49 shorter events, 0.7 us)
Async XLA Ops:
  7.2 3.2 copy-start
  7.2 285.6 %all-gather.2.cloned.1.call-start = ((), (), s32[]{:S(2)}) async-start(), calls=%async_computation.6 | async-start | bytes 16056320 | tf_op jit(solution)/shard_map/all_gather | solution.py:149
  10.4 10.6 %copy-start.2 = (f32[32,56,192]{1,0,2:T(8,128)}, f32[32,56,192]{1,0,2:T(8,128)S(1)}, u32[]{:S(2)}) copy-start(f32[32,56,192]{1,0,2:T(8,128)S(1)} %copy.152) | copy-start | bytes 4128772
  204.4 6.4 copy-start.7
  204.4 6.4 copy-start.8
  204.4 6.4 copy-start.9
  204.4 6.4 copy-start.12
  204.4 6.5 copy-start.10
  204.4 6.5 copy-start.11
  204.5 10.1 %copy-start.13 = (f32[12]{0:T(128)S(1)}, f32[12]{0:T(128)}, u32[]{:S(2)}) copy-start(f32[12]{0:T(128)} %param.20) | copy-start | bytes 148
  204.5 10.3 %copy-start.14 = (f32[96]{0:T(128)S(1)}, f32[96]{0:T(128)}, u32[]{:S(2)}) copy-start(f32[96]{0:T(128)} %param.21) | copy-start | bytes 1156
  211.7 10.6 %all-to-all-start = ((f32[32,5,128]{2,1,0:T(8,128)}), f32[32,5,128]{2,1,0:T(8,128)S(1)}, u32[]{:S(2)}, u32[]{:S(2)}) async-start(f32[32,5,128]{2,1,0:T(8,128)} %stack.32), calls=%async_computation | async-start | bytes 262144 | tf_op jit(solution)/shard_map/all_to_all | solution.py:137
  214.5 348.2 %reduce-scatter.2.cloned.1.call-start = ((), (), s32[]{:S(2)}) async-start(), calls=%async_computation.7 | async-start | bytes 16056320 | tf_op jit(solution)/shard_map/reduce_scatter | solution.py:200
  214.8 92.5 %copy-start.5 = (f32[16,96]{1,0:T(8,128)}, f32[16,96]{1,0:T(8,128)S(1)}, u32[]{:S(2)}) copy-start(f32[16,96]{1,0:T(8,128)S(1)} %maximum_maximum_fusion.1.refs_2_) | copy-start | bytes 18436
  307.4 5.0 copy-start.6
  415.3 8.4 %copy-start.1 = (f32[56,96,256]{2,1,0:T(8,128)S(1)}, f32[56,96,256]{2,1,0:T(8,128)}, u32[]{:S(2)}) copy-start(f32[56,96,256]{2,1,0:T(8,128)} %settle_backward.1) | copy-start | bytes 16515076
  736.6 3.7 copy-start.4
  747.3 12.5 %copy-start.3 = (f32[32,56,192]{1,0,2:T(8,128)S(1)}, f32[32,56,192]{1,0,2:T(8,128)}, u32[]{:S(2)}) copy-start(f32[32,56,192]{1,0,2:T(8,128)} %copy-done.2) | copy-start | bytes 4128772
Sparse Core Ops, SparseCore 0:
  210.9 81.7 all-gather.1
  461.3 101.3 reduce-scatter.1
where the time goes:
time: 787 us; the launch traced here: 775 us
  blocking collectives  197 us (25%)
  waiting for transfers between devices  179 us (23%)
  local copies, waits for them, and re-layouts  177 us (22%)
  matrix products  87.1 us (11%)
  Pallas kernels  71.3 us (9%)
  other arithmetic  45.7 us (6%)
  between operations  14.6 us (2%)
    reduce_scatter x1, waiting for transfers between devices, body(): lax.psum_scatter(analysis(cosine, sine_table, adjoint), 'wave', scatter_d...  101 us
    all_gather x1, waiting for transfers between devices, body(): shard_piece = lax.all_gather(spectral, 'wave', axis=0, tiled=True)  70.3 us
    unnamed x41, local copies, waits for them, and re-layouts  65.1 us
    all_to_all x1, blocking collectives, body(): lax.all_to_all(spectral_adj, 'band', split_axis=2, concat_axis=1, tiled=T...  61 us
    all_to_all x1, blocking collectives, body(): lax.all_to_all(every_lat, 'band', split_axis=1, concat_axis=2, tiled=True)  59 us
    all_to_all x1, blocking collectives, body(): lax.all_to_all(scaled, 'band', split_axis=2, concat_axis=0, tiled=True)  40.9 us
    pallas_call x1, Pallas kernels, settle_backward(): pl.pallas_call(lambda *refs: settle_adjoint_kernel(bins, *refs), grid=(la...  36.5 us
    all_to_all x1, blocking collectives, body(): lax.all_to_all(mode_block, 'band', split_axis=0, concat_axis=2, tiled=True)  36.5 us
  transfers between devices with their start and end apart: 3, of which 3 were waited for; matrix products, arithmetic and copies ran while one was open for 0% of the time, Pallas kernels for 0%

commit v1 on v0

--- a/solution.py
+++ b/solution.py
@@ -210,26 +210,715 @@
     return (control + control_adj, tracer)
 
 
+LANES = 128
+MESH_ID = pl.DeviceIdType.MESH
+bf16 = jnp.bfloat16
+f32 = jnp.float32
+VMEM_LIMIT = 63 * 1024 * 1024
+
+
+def split2(x):
+    hi = x.astype(bf16)
+    return hi, (x - hi.astype(f32)).astype(bf16)
+
+
+def split3(x):
+    hi, lo = split2(x)
+    rest = x - hi.astype(f32)
+    return hi, lo, (rest - lo.astype(f32)).astype(bf16)
+
+
+def product(a, b, dims=((1,), (0,))):
+    def one(x, y):
+        return lax.dot_general(x, y, (dims, ((), ())), preferred_element_type=f32)
+
+    return one(a[1], b[0]) + one(a[0], b[1]) + one(a[0], b[0])
+
+
+def lane_of(shape):
+    return lax.broadcasted_iota(jnp.int32, shape, len(shape) - 1)
+
+
+def packed_order(channels, transposed):
+    half = LANES // 2
+    width = 2 * channels
+    shape = (2 * LANES, width) if transposed else (width, 2 * LANES)
+    source = lax.broadcasted_iota(jnp.int32, shape, 1 if transposed else 0)
+    target = lax.broadcasted_iota(jnp.int32, shape, 0 if transposed else 1)
+    channel = source // 2
+    place = jnp.where(channel < half, channel, channel + half) + (source % 2) * half
+    return jnp.where(place == target, 1.0, 0.0).astype(bf16)
+
+
+def select_product(x, matrix):
+    return sum(
+        lax.dot_general(piece, matrix, (((1,), (0,)), ((), ())), preferred_element_type=f32)
+        for piece in reversed(split3(x))
+    )
+
+
+class Sizes:
+    def __init__(self, modes, waves, width, lats, bands, wave_count):
+        self.modes, self.waves, self.width, self.lats = modes, waves, width, lats
+        self.bands, self.wave_count = bands, wave_count
+        self.own = waves // bands
+        self.pairs = lats // 2
+        self.rows = -(-(3 * self.pairs) // 8) * 8
+        self.in_rows = modes + modes // 2
+        self.slots = waves * wave_count
+
+
+def first_kernel(z, control_ref, scale_ref, root_ref, leg_ref, out_ref, s_a, s_b, send_u, recv_v, leg, y_a, y_b, send_y,
+                 leg_sem, a1_send, a1_recv, a2_send, a2_recv, x_send, x_recv, c_send, c_recv):
+    w, b = lax.axis_index("wave"), lax.axis_index("band")
+    partner = w + 1 - 2 * (w % 2)
+    across = (w + 2) % z.wave_count
+    relay = (partner + 2) % z.wave_count
+    half = LANES // 2
+    quarter = LANES // 4
+
+    def peer(d):
+        return (b + d) % z.bands
+
+    leg_copy = pltpu.make_async_copy(leg_ref.at[pl.ds(b * z.own, z.own)], leg, leg_sem)
+    leg_copy.start()
+    barrier = pltpu.get_barrier_semaphore()
+    for d in range(1, z.bands):
+        pl.semaphore_signal(barrier, inc=1, device_id={"wave": w, "band": peer(d)}, device_id_type=MESH_ID)
+    for other in (partner, across):
+        pl.semaphore_signal(barrier, inc=1, device_id={"wave": other, "band": b}, device_id_type=MESH_ID)
+
+    root = split2(root_ref[...])
+    order = packed_order(z.width // 2, False)
+    group = 8
+
+    def vertical(i, carry):
+        x = control_ref[pl.ds(i * group, group)].reshape(group * z.waves, z.width)
+        scale = scale_ref[pl.ds(i * group, group)].reshape(group * z.waves, z.width)
+        placed = select_product(scale * product(split2(x), root), order)
+        at = pl.ds(pl.multiple_of(i * group * z.waves, 8), group * z.waves)
+        s_a[at, :] = placed[:, :LANES]
+        s_b[at, :] = placed[:, LANES:]
+        return carry
+
+    lax.fori_loop(0, z.modes // group, vertical, 0)
+
+    def pack(m, carry):
+        tall = s_b[pl.ds(m, z.modes, stride=z.waves), :]
+        low = z.modes // 2
+        send_u[m, : z.modes] = s_a[pl.ds(m, z.modes, stride=z.waves), :]
+        send_u[m, z.modes :] = tall[:low] + pltpu.roll(tall[low:], quarter, 1)
+        return carry
+
+    lax.fori_loop(0, z.waves, pack, 0)
+    pl.semaphore_wait(barrier, z.bands + 1)
+
+    def first_copy(d):
+        return pltpu.make_async_remote_copy(
+            send_u.at[pl.ds(peer(d) * z.own, z.own)], recv_v.at[b], a1_send.at[d], a1_recv.at[d],
+            device_id={"wave": w, "band": peer(d)}, device_id_type=MESH_ID)
+
+    first_own = pltpu.make_async_copy(send_u.at[pl.ds(b * z.own, z.own)], recv_v.at[b], a1_send.at[0])
+    for d in range(1, z.bands):
+        first_copy(d).start()
+    first_own.start()
+    leg_copy.wait()
+    first_own.wait()
+    for d in range(1, z.bands):
+        first_copy(d).wait_recv()
+
+    def second_copy(p, d):
+        return pltpu.make_async_remote_copy(
+            send_y.at[p, peer(d)], out_ref.at[w, b, p], a2_send.at[p, d], a2_recv.at[p, d],
+            device_id={"wave": w, "band": peer(d)}, device_id_type=MESH_ID)
+
+    def second_own(p):
+        return pltpu.make_async_copy(send_y.at[p, b], out_ref.at[w, b, p], a2_send.at[p, 0])
+
+    def across_copy(p):
+        return pltpu.make_async_remote_copy(
+            out_ref.at[w, :, p], out_ref.at[w, :, p], x_send.at[p], x_recv.at[p],
+            device_id={"wave": across, "band": b}, device_id_type=MESH_ID)
+
+    def core_copy(p, which):
+        block = w if which == 0 else across
+        return pltpu.make_async_remote_copy(
+            out_ref.at[block, :, p], out_ref.at[block, :, p], c_send.at[p, which], c_recv.at[p, which],
+            device_id={"wave": partner, "band": b}, device_id_type=MESH_ID)
+
+    def transform(p):
+        tops, tails = [], []
+        for s in range(z.bands):
+            tail = recv_v[s, p, z.modes :]
+            keep = lane_of(tail.shape) % half < quarter
+            tops.append(recv_v[s, p, : z.modes])
+            tails.append(jnp.where(keep, tail, 0.0))
+            tails.append(jnp.where(keep, pltpu.roll(tail, LANES - quarter, 1), 0.0))
+        x = jnp.concatenate([jnp.concatenate(tops, 0), jnp.concatenate(tails, 0)], 1)
+        y = product(split2(leg[p]), split2(x))
+        y_a[...] = y[:, :LANES]
+        y_b[...] = y[:, LANES:]
+        for s in range(z.bands):
+            at = s * z.lats
+            one = y_a[at : at + z.pairs]
+            two = y_a[at + z.pairs : at + z.lats]
+            left = lane_of(one.shape) < half
+            send_y[p, s, z.rows - 8 :] = jnp.zeros((8, LANES), f32)
+            send_y[p, s, : z.pairs] = jnp.where(left, one, pltpu.roll(two, half, 1))
+            send_y[p, s, z.pairs : 2 * z.pairs] = jnp.where(left, pltpu.roll(one, half, 1), two)
+            send_y[p, s, 2 * z.pairs : 3 * z.pairs] = y_b[at : at + z.pairs] + pltpu.roll(
+                y_b[at + z.pairs : at + z.lats], quarter, 1)
+
+    def phase(p, carry):
+        @pl.when(p < z.own)
+        def _():
+            transform(p)
+            for d in range(1, z.bands):
+                second_copy(p, d).start()
+            second_own(p).start()
+
+        @pl.when((p >= 1) & (p <= z.own))
+        def _():
+            for d in range(1, z.bands):
+                second_copy(p - 1, d).wait_recv()
+            second_own(p - 1).wait()
+            across_copy(p - 1).start()
+            core_copy(p - 1, 0).start()
+
+        @pl.when(p >= 2)
+        def _():
+            across_copy(p - 2).wait_recv()
+            core_copy(p - 2, 1).start()
+
+        return carry
+
+    lax.fori_loop(0, z.own + 2, phase, 0)
+    for d in range(1, z.bands):
+        first_copy(d).wait_send()
+
+    def drain(p, carry):
+        for d in range(1, z.bands):
+            second_copy(p, d).wait_send()
+        across_copy(p).wait_send()
+        for which in range(2):
+            core_copy(p, which).wait()
+        return carry
+
+    lax.fori_loop(0, z.own, drain, 0)
+
+
+def transform_forward(z, control, scale, root, legendre):
+    whole_in = pl.BlockSpec(memory_space=pltpu.VMEM)
+    anywhere = pl.BlockSpec(memory_space=pl.ANY)
+    dma = pltpu.SemaphoreType.DMA
+    lats_all = z.lats * z.bands
+    return pl.pallas_call(
+        lambda *refs: first_kernel(z, *refs),
+        in_specs=[whole_in, whole_in, whole_in, anywhere],
+        out_specs=anywhere,
+        out_shape=jax.ShapeDtypeStruct((z.wave_count, z.bands, z.own, z.rows, LANES), f32),
+        scratch_shapes=[
+            pltpu.VMEM((z.modes * z.waves, LANES), f32),
+            pltpu.VMEM((z.modes * z.waves, LANES), f32),
+            pltpu.VMEM((z.waves, z.in_rows, LANES), f32),
+            pltpu.VMEM((z.bands, z.own, z.in_rows, LANES), f32),
+            pltpu.VMEM((z.own, lats_all, z.modes * z.bands), f32),
+            pltpu.VMEM((lats_all, LANES), f32),
+            pltpu.VMEM((lats_all, LANES), f32),
+            pltpu.VMEM((z.own, z.bands, z.rows, LANES), f32),
+            dma(()), dma((z.bands,)), dma((z.bands,)), dma((z.own, z.bands)), dma((z.own, z.bands)),
+            dma((z.own,)), dma((z.own,)), dma((z.own, 2)), dma((z.own, 2)),
+        ],
+        compiler_params=pltpu.CompilerParams(collective_id=0, has_side_effects=True, vmem_limit_bytes=VMEM_LIMIT),
+        name="transform_forward",
+    )(control, scale, root, legendre)
+
+
+def synthesis_kernel(z, bins, slabs_ref, cos_ref, sin_ref, courant_ref, proj_ref, out_ref, model_ref, c_hi, c_lo, n_hi, n_lo):
+    i = pl.program_id(0)
+    half = LANES // 2
+
+    @pl.when(i == 0)
+    def _():
+        c_hi[...], c_lo[...] = split2(cos_ref[...])
+        n_hi[...], n_lo[...] = split2(-sin_ref[...])
+
+    def slab(row):
+        return slabs_ref[pl.ds(row, z.slots, stride=z.rows), :]
+
+    tail = slab(2 * z.pairs + i)
+    real = jnp.concatenate([slab(i), tail], 1)
+    imag = jnp.concatenate([slab(z.pairs + i), pltpu.roll(tail, half, 1)], 1)
+    over_waves = ((0,), (0,))
+    field = product(split2(real), (c_hi[...], c_lo[...]), over_waves) + product(
+        split2(imag), (n_hi[...], n_lo[...]), over_waves)
+    channels = z.width // 2
+    rest = channels - half
+    proj = split2(proj_ref[...])
+    for which in range(2):
+        tracer = jnp.concatenate(
+            [field[which * half : (which + 1) * half],
+             field[LANES + which * (half // 2) : LANES + which * (half // 2) + rest]], 0)
+        courant = courant_ref[which, 0]
+        row = lax.broadcasted_iota(jnp.int32, tracer.shape, 0)
+        for repeat in range(STEPS):
+            outflow = courant * tracer
+            inflow = jnp.where(row >= bins, pltpu.roll(outflow, bins, 0), 0.0)
+            tracer = tracer - outflow + inflow
+        out_ref[which, 0] = tracer
+        model_ref[which, 0] = product(proj, split2(tracer))
+
+
+def paired(rows, cols):
+    return pl.BlockSpec((2, 1, rows, cols), lambda i: (0, i, 0, 0))
+
+
+def synthesis_settle(z, slabs, cosine, sine, courant, proj, bins):
+    lats, channels, lons = courant.shape
+    rows = proj.shape[0]
+    tracer, model = pl.pallas_call(
+        lambda *refs: synthesis_kernel(z, bins, *refs),
+        grid=(z.pairs,),
+        in_specs=[whole(z.slots * z.rows, LANES), whole(z.slots, lons), whole(z.slots, lons), paired(channels, lons),
+                  whole(rows, channels)],
+        out_specs=[paired(channels, lons), paired(rows, lons)],
+        out_shape=[
+            jax.ShapeDtypeStruct((2, z.pairs, channels, lons), f32),
+            jax.ShapeDtypeStruct((2, z.pairs, rows, lons), f32),
+        ],
+        scratch_shapes=[pltpu.VMEM((z.slots, lons), bf16)] * 4,
+        compiler_params=pltpu.CompilerParams(vmem_limit_bytes=VMEM_LIMIT),
+        name="synthesis_settle",
+    )(slabs.reshape(z.slots * z.rows, LANES), cosine, sine, courant.reshape(2, z.pairs, channels, lons), proj)
+    return tracer.reshape(lats, channels, lons), model.reshape(lats, rows, lons)
+
+
+def analysis_kernel(z, bins, resid_ref, courant_ref, proj_ref, cos_ref, sin_ref, out_ref, c_hi, c_lo, n_hi, n_lo):
+    i = pl.program_id(0)
+    half = LANES // 2
+
+    @pl.when(i == 0)
+    def _():
+        c_hi[...], c_lo[...] = split2(cos_ref[...])
+        n_hi[...], n_lo[...] = split2(-sin_ref[...])
+
+    proj = split2(proj_ref[...])
+    fields = []
+    for which in range(2):
+        courant = courant_ref[which, 0]
+        adjoint = product(proj, split2(resid_ref[which, 0]))
+        channels = adjoint.shape[0]
+        row = lax.broadcasted_iota(jnp.int32, adjoint.shape, 0)
+        for repeat in range(STEPS):
+            below = jnp.where(row < channels - bins, pltpu.roll(adjoint, channels - bins, 0), 0.0)
+            adjoint = adjoint + courant * (below - adjoint)
+        fields.append(adjoint)
+    gap = jnp.zeros((half // 2 - (channels - half), fields[0].shape[1]), f32)
+    pieces = [field[:half] for field in fields]
+    for field in fields:
+        pieces.append(field[half:])
+        if gap.shape[0]:
+            pieces.append(gap)
+    pieces.append(jnp.zeros((half, fields[0].shape[1]), f32))
+    both = split2(jnp.concatenate(pieces, 0))
+    over_lons = ((1,), (1,))
+    real = product((c_hi[...], c_lo[...]), both, over_lons)
+    imag = product((n_hi[...], n_lo[...]), both, over_lons)
+
+    @pl.when(i == 0)
+    def _():
+        for spare in range(3 * z.pairs, z.rows):
+            out_ref[pl.ds(spare, z.slots, stride=z.rows), :] = jnp.zeros((z.slots, LANES), f32)
+
+    out_ref[pl.ds(i, z.slots, stride=z.rows), :] = real[:, :LANES]
+    out_ref[pl.ds(z.pairs + i, z.slots, stride=z.rows), :] = imag[:, :LANES]
+    out_ref[pl.ds(2 * z.pairs + i, z.slots, stride=z.rows), :] = real[:, LANES:] + pltpu.roll(imag[:, LANES:], half, 1)
+
+
+def settle_analysis(z, resid, courant, proj_t, cosine, sine, bins):
+    lats, channels, lons = courant.shape
+    rows = proj_t.shape[1]
+    out = pl.pallas_call(
+        lambda *refs: analysis_kernel(z, bins, *refs),
+        grid=(z.pairs,),
+        in_specs=[paired(rows, lons), paired(channels, lons), whole(channels, rows), whole(z.slots, lons),
+                  whole(z.slots, lons)],
+        out_specs=whole(z.slots * z.rows, LANES),
+        out_shape=jax.ShapeDtypeStruct((z.slots * z.rows, LANES), f32),
+        scratch_shapes=[pltpu.VMEM((z.slots, lons), bf16)] * 4,
+        compiler_params=pltpu.CompilerParams(vmem_limit_bytes=VMEM_LIMIT),
+        name="settle_analysis",
+    )(resid.reshape(2, z.pairs, rows, lons), courant.reshape(2, z.pairs, channels, lons), proj_t, cosine, sine)
+    return out.reshape(z.wave_count, z.bands, z.own, z.rows, LANES)
+
+
+def second_kernel(z, part_ref, leg_ref, out_ref, part, r1, r2, v3, leg, z_all, send_u,
+                  leg_sem, q_sem, c_send, c_recv, x_send, x_recv, a3_send, a3_recv, a4_send, a4_recv):
+    w, b = lax.axis_index("wave"), lax.axis_index("band")
+    partner = w + 1 - 2 * (w % 2)
+    across = (w + 2) % z.wave_count
+    relay = (partner + 2) % z.wave_count
+    half = LANES // 2
+    quarter = LANES // 4
+
+    def peer(d):
+        return (b + d) % z.bands
+
+    def target(q):
+        return (b + 1 + q) % z.bands
+
+    leg_copy = pltpu.make_async_copy(leg_ref.at[pl.ds(b * z.own, z.own)], leg, leg_sem)
+    barrier = pltpu.get_barrier_semaphore()
+    for d in range(1, z.bands):
+        pl.semaphore_signal(barrier, inc=1, device_id={"wave": w, "band": peer(d)}, device_id_type=MESH_ID)
+    for other in (partner, across):
+        pl.semaphore_signal(barrier, inc=1, device_id={"wave": other, "band": b}, device_id_type=MESH_ID)
+
+    def local_copy(q, which):
+        block = w if which == 0 else across
+        return pltpu.make_async_copy(part_ref.at[block, target(q)], part.at[q, which], q_sem.at[q, which])
+
+    def core_copy(q, which):
+        block = partner if which == 0 else relay
+        return pltpu.make_async_remote_copy(
+            part_ref.at[block, target(q)], r1.at[q, which], c_send.at[q, which], c_recv.at[q, which],
+            device_id={"wave": partner, "band": b}, device_id_type=MESH_ID)
+
+    def across_copy(q):
+        return pltpu.make_async_remote_copy(
+            part.at[q, 1], r2.at[q], x_send.at[q], x_recv.at[q],
+            device_id={"wave": across, "band": b}, device_id_type=MESH_ID)
+
+    def third_copy(q):
+        return pltpu.make_async_remote_copy(
+            part.at[q, 0], v3.at[b], a3_send.at[q], a3_recv.at[q],
+            device_id={"wave": w, "band": target(q)}, device_id_type=MESH_ID)
+
+    pl.semaphore_wait(barrier, z.bands + 1)
+
+    def begin(q, carry):
+        for which in (1, 0):
+            core_copy(q, which).start()
+            local_copy(q, which).start()
+        return carry
+
+    lax.fori_loop(0, z.bands, begin, 0)
+    leg_copy.start()
+
+    def stage(q, carry):
+        @pl.when(q < z.bands)
+        def _():
+            local_copy(q, 1).wait()
+            core_copy(q, 1).wait_recv()
+
+            def add(p, inner):
+                part[q, 1, p] = part[q, 1, p] + r1[q, 1, p]
+                return inner
+
+            lax.fori_loop(0, z.own, add, 0)
+            across_copy(q).start()
+
+        @pl.when(q >= 1)
+        def _():
+            k = q - 1
+            local_copy(k, 0).wait()
+            core_copy(k, 0).wait_recv()
+            across_copy(k).wait_recv()
+
+            def add(p, inner):
+                part[k, 0, p] = part[k, 0, p] + r1[k, 0, p] + r2[k, p]
+                return inner
+
+            lax.fori_loop(0, z.own, add, 0)
+
+            @pl.when(k < z.bands - 1)
+            def _():
+                third_copy(k).start()
+
+        return carry
+
+    lax.fori_loop(0, z.bands + 1, stage, 0)
+    own_copy = pltpu.make_async_copy(part.at[z.bands - 1, 0], v3.at[b], a3_send.at[z.bands - 1])
+    own_copy.start()
+    leg_copy.wait()
+    own_copy.wait()
+    for q in range(z.bands - 1):
+        third_copy(q).wait_recv()
+
+    def fourth_copy(p, d):
+        return pltpu.make_async_remote_copy(
+            send_u.at[p, peer(d)], out_ref.at[b, p], a4_send.at[p, d], a4_recv.at[p, d],
+            device_id={"wave": w, "band": peer(d)}, device_id_type=MESH_ID)
+
+    def fourth_own(p):
+        return pltpu.make_async_copy(send_u.at[p, b], out_ref.at[b, p], a4_send.at[p, 0])
+
+    def transform(p, carry):
+        for s in range(z.bands):
+            at = s * z.lats
+            real = v3[s, p, : z.pairs]
+            imag = v3[s, p, z.pairs : 2 * z.pairs]
+            tail = v3[s, p, 2 * z.pairs : 3 * z.pairs]
+            lane = lane_of(real.shape)
+            keep = lane % half < quarter
+            z_all[at : at + z.pairs, :LANES] = jnp.where(lane < half, real, pltpu.roll(imag, half, 1))
+            z_all[at + z.pairs : at + z.lats, :LANES] = jnp.where(lane < half, pltpu.roll(real, half, 1), imag)
+            z_all[at : at + z.pairs, LANES:] = jnp.where(keep, tail, 0.0)
+            z_all[at + z.pairs : at + z.lats, LANES:] = jnp.where(keep, pltpu.roll(tail, LANES - quarter, 1), 0.0)
+        y = product(split2(leg[p]), split2(z_all[...]), ((0,), (0,)))
+        for s in range(z.bands):
+            rows = y[s * z.modes : (s + 1) * z.modes]
+            low = z.modes // 2
+            send_u[p, s, : z.modes] = rows[:, :LANES]
+            send_u[p, s, z.modes :] = rows[:low, LANES:] + pltpu.roll(rows[low:, LANES:], quarter, 1)
+        for d in range(1, z.bands):
+            fourth_copy(p, d).start()
+        fourth_own(p).start()
+        return carry
+
+    lax.fori_loop(0, z.own, transform, 0)
+
+    def drain_sums(q, carry):
+        across_copy(q).wait_send()
+        for which in range(2):
+            core_copy(q, which).wait_send()
+        return carry
+
+    lax.fori_loop(0, z.bands, drain_sums, 0)
+    for q in range(z.bands - 1):
+        third_copy(q).wait_send()
+
+    def drain(p, carry):
+        for d in range(1, z.bands):
+            fourth_copy(p, d).wait()
+        fourth_own(p).wait()
+        return carry
+
+    lax.fori_loop(0, z.own, drain, 0)
+
+
+def transform_backward(z, part, legendre):
+    anywhere = pl.BlockSpec(memory_space=pl.ANY)
+    dma = pltpu.SemaphoreType.DMA
+    lats_all = z.lats * z.bands
+    slab = (z.own, z.rows, LANES)
+    return pl.pallas_call(
+        lambda *refs: second_kernel(z, *refs),
+        in_specs=[anywhere, anywhere],
+        out_specs=anywhere,
+        out_shape=jax.ShapeDtypeStruct((z.bands, z.own, z.in_rows, LANES), f32),
+        scratch_shapes=[
+            pltpu.VMEM((z.bands, 2) + slab, f32),
+            pltpu.VMEM((z.bands, 2) + slab, f32),
+            pltpu.VMEM((z.bands,) + slab, f32),
+            pltpu.VMEM((z.bands,) + slab, f32),
+            pltpu.VMEM((z.own, lats_all, z.modes * z.bands), f32),
+            pltpu.VMEM((lats_all, 2 * LANES), f32),
+            pltpu.VMEM((z.own, z.bands, z.in_rows, LANES), f32),
+            dma(()), dma((z.bands, 2)), dma((z.bands, 2)), dma((z.bands, 2)), dma((z.bands,)), dma((z.bands,)),
+            dma((z.bands,)), dma((z.bands,)), dma((z.own, z.bands)), dma((z.own, z.bands)),
+        ],
+        compiler_params=pltpu.CompilerParams(collective_id=1, has_side_effects=True, vmem_limit_bytes=VMEM_LIMIT),
+        name="transform_backward",
+    )(part, legendre)
+
+
+def last_kernel(z, slabs_ref, control_ref, scale_ref, root_ref, out_ref, s_a, s_b):
+    half = LANES // 2
+    quarter = LANES // 4
+
+    def unpack(m, carry):
+        tail = slabs_ref[m, z.modes :]
+        keep = lane_of(tail.shape) % half < quarter
+        both = jnp.concatenate(
+            [jnp.where(keep, tail, 0.0), jnp.where(keep, pltpu.roll(tail, LANES - quarter, 1), 0.0)], 0)
+        s_a[pl.ds(m, z.modes, stride=z.waves), :] = slabs_ref[m, : z.modes]
+        s_b[pl.ds(m, z.modes, stride=z.waves), :] = both
+        return carry
+
+    lax.fori_loop(0, z.waves, unpack, 0)
+    root = split2(root_ref[...])
+    order = packed_order(z.width // 2, True)
+    group = 8
+
+    def vertical(i, carry):
+        at = pl.ds(pl.multiple_of(i * group * z.waves, 8), group * z.waves)
+        placed = jnp.concatenate([s_a[at, :], s_b[at, :]], 1)
+        scale = scale_ref[pl.ds(i * group, group)].reshape(group * z.waves, z.width)
+        mixed = product(split2(scale * select_product(placed, order)), root)
+        out_ref[pl.ds(i * group, group)] = control_ref[pl.ds(i * group, group)] + mixed.reshape(
+            group, z.waves, z.width)
+        return carry
+
+    lax.fori_loop(0, z.modes // group, vertical, 0)
+
+
+def finish(z, slabs, control, scale, root_t):
+    whole_in = pl.BlockSpec(memory_space=pltpu.VMEM)
+    return pl.pallas_call(
+        lambda *refs: last_kernel(z, *refs),
+        in_specs=[whole_in] * 4,
+        out_specs=whole_in,
+        out_shape=jax.ShapeDtypeStruct(control.shape, f32),
+        scratch_shapes=[pltpu.VMEM((z.modes * z.waves, LANES), f32)] * 2,
+        compiler_params=pltpu.CompilerParams(vmem_limit_bytes=VMEM_LIMIT),
+        name="finish",
+    )(slabs.reshape(z.waves, z.in_rows, LANES), control, scale, root_t)
+
+
+def observation_sums(z, tracer_shape, model, arrived, lidar_coef, levels_here, proj_rows):
+    lat_here, lon_here = tracer_shape
+    columns, levels, lidar_vals, aod_vals, weights = [arrived[:, i].reshape(-1) for i in range(5)]
+    columns = columns.astype(jnp.int32)
+    levels = levels.astype(jnp.int32)
+    lat_index = columns // lon_here
+    lon_hot = (columns % lon_here)[:, None] == jnp.arange(lon_here, dtype=jnp.int32)[None, :]
+    lat_hot = (lat_index[:, None] == jnp.arange(lat_here, dtype=jnp.int32)[None, :]).astype(jnp.float32)
+    cell = lat_index * levels_here + levels
+    cell_hot = (
+        cell[:, None] == jnp.arange(lat_here * levels_here, dtype=jnp.int32)[None, :]
+    ).astype(jnp.float32)
+    lidar_field = model[:, :levels_here].reshape(lat_here * levels_here, lon_here)
+    aod_field = model[:, levels_here]
+    lidar_rows = jnp.dot(cell_hot, lidar_field, precision=highest)
+    aod_rows = jnp.dot(lat_hot, aod_field, precision=highest)
+    lidar_model = jnp.sum(jnp.where(lon_hot, lidar_rows, 0.0), axis=1)
+    aod_model = jnp.sum(jnp.where(lon_hot, aod_rows, 0.0), axis=1)
+    lidar_resid = weights * (lidar_model - lidar_vals)
+    aod_resid = weights * (aod_model - aod_vals)
+    lidar_sum = lax.dot_general(
+        cell_hot, jnp.where(lon_hot, lidar_resid[:, None], 0.0), (((0,), (0,)), ((), ())), precision=highest
+    )
+    aod_sum = lax.dot_general(
+        lat_hot, jnp.where(lon_hot, aod_resid[:, None], 0.0), (((0,), (0,)), ((), ())), precision=highest
+    )
+    return jnp.concatenate(
+        [
+            lidar_sum.reshape(lat_here, levels_here, lon_here),
+            aod_sum[:, None, :],
+            jnp.zeros((lat_here, proj_rows - levels_here - 1, lon_here), jnp.float32),
+        ],
+        axis=1,
+    )
+
+
+def observation_packet(obs_count, obs_column, obs_level, lidar_obs, aod_obs, obs_weight):
+    slot_count = obs_column.shape[1]
+    live = jnp.arange(slot_count, dtype=jnp.int32)[None, :] < obs_count.reshape(-1, 1)
+    packet = jnp.stack(
+        [
+            obs_column.astype(jnp.float32),
+            obs_level.astype(jnp.float32),
+            lidar_obs,
+            aod_obs,
+            jnp.where(live, obs_weight, 0.0),
+        ],
+        axis=1,
+    )
+    return lax.all_to_all(packet, ("wave", "band"), split_axis=0, concat_axis=0, tiled=True)
+
+
+def projection(lidar_coef, aod_coef):
+    bins = lidar_coef.shape[0]
+    channels = aod_coef.shape[0]
+    levels_here = channels // bins
+    proj_rows = -(-(levels_here + 1) // 8) * 8
+    level_of = jnp.arange(channels, dtype=jnp.int32) // bins
+    in_level = jnp.arange(levels_here, dtype=jnp.int32)[:, None] == level_of[None, :]
+    return jnp.concatenate(
+        [
+            jnp.where(in_level, jnp.tile(lidar_coef, levels_here)[None, :], 0.0),
+            aod_coef[None, :],
+            jnp.zeros((proj_rows - levels_here - 1, channels), jnp.float32),
+        ],
+        axis=0,
+    )
+
+
+def interleaved(root):
+    channels = root.shape[0]
+    wide = root[:, None, :, None] * jnp.eye(2, dtype=jnp.float32)[None, :, None, :]
+    return wide.reshape(2 * channels, 2 * channels)
+
+
+def fast_body(
+    control,
+    spectral_scale,
+    vertical_root,
+    legendre,
+    zonal_number,
+    courant,
+    lidar_coef,
+    aod_coef,
+    obs_count,
+    obs_column,
+    obs_level,
+    lidar_obs,
+    aod_obs,
+    obs_weight,
+):
+    modes_here, waves_here, width = control.shape
+    wave_count = lax.axis_size("wave")
+    lats_here, channels, lon_here = courant.shape
+    z = Sizes(modes_here, waves_here, width, lats_here, lax.axis_size("band"), wave_count)
+    lon_first = lax.axis_index("wave") * lon_here
+    factor = zonal_number.shape[0] ** (-0.5)
+    bins = lidar_coef.shape[0]
+    levels_here = channels // bins
+    arrived = observation_packet(obs_count, obs_column, obs_level, lidar_obs, aod_obs, obs_weight)
+    cosine, sine = trig_tables(zonal_number, lon_first, lon_here, lon_here * wave_count, factor)
+    proj = projection(lidar_coef, aod_coef)
+    slabs = transform_forward(z, control, spectral_scale, interleaved(vertical_root), legendre)
+    tracer, model = synthesis_settle(z, slabs, cosine, sine, courant, proj, bins)
+    resid = observation_sums(z, (lats_here, lon_here), model, arrived, lidar_coef, levels_here, proj.shape[0])
+    part = settle_analysis(z, resid, courant, proj.T, cosine, sine, bins)
+    back = transform_backward(z, part, legendre)
+    return finish(z, back, control, spectral_scale, interleaved(vertical_root.T)), tracer
+
+
+def fits(mesh, control, courant):
+    bands, waves = mesh.shape["band"], mesh.shape["wave"]
+    modes_here, waves_here = control[0] // bands, control[1] // waves
+    lats_here, channels = courant[0] // bands, courant[1]
+    return (
+        waves == 4
+        and waves_here % bands == 0
+        and waves_here % 8 == 0
+        and modes_here % 16 == 0
+        and lats_here % 8 == 0
+        and LANES // 2 < channels <= LANES * 3 // 4
+        and (channels - LANES // 2) % 8 == 0
+        and courant[2] // waves % LANES == 0
+    )
+
+
+SPECS = (
+    P("band", "wave", None),
+    P("band", "wave", None),
+    P(),
+    P("wave", None, None),
+    P(),
+    P("band", None, "wave"),
+    P(),
+    P(),
+    P(("wave", "band"), None),
+    P(("wave", "band"), None),
+    P(("wave", "band"), None),
+    P(("wave", "band"), None),
+    P(("wave", "band"), None),
+    P(("wave", "band"), None),
+)
+
+
 def solution(mesh):
-    return jax.shard_map(
-        body,
-        mesh=mesh,
-        in_specs=(
-            P("band", "wave", None),
-            P("band", "wave", None),
-            P(),
-            P("wave", None, None),
-            P(),
-            P("band", None, "wave"),
-            P(),
-            P(),
-            P(("wave", "band"), None),
-            P(("wave", "band"), None),
-            P(("wave", "band"), None),
-            P(("wave", "band"), None),
-            P(("wave", "band"), None),
-            P(("wave", "band"), None),
-        ),
-        out_specs=(P("band", "wave", None), P("band", None, "wave")),
-        check_vma=False,
-    )
+    def program(*args):
+        chosen = fast_body if fits(mesh, args[0].shape, args[5].shape) else body
+        return jax.shard_map(
+            chosen,
+            mesh=mesh,
+            in_specs=SPECS,
+            out_specs=(P("band", "wave", None), P("band", None, "wave")),
+            check_vma=False,
+        )(*args)
+
+    return program

time: 787 us -> 366 us (0.47)
  the two profiles are of different devices: /device:TPU:0 before, /device:TPU:26 now
where the time goes in v1:
time: 366 us; the launch traced here: 365 us
  Pallas kernels  305 us (83%)
  local copies, waits for them, and re-layouts  21.9 us (6%)
  matrix products  17.4 us (5%)
  other arithmetic  14 us (4%)
  starting transfers between devices  5.86 us (2%)
    pallas_call x1, Pallas kernels, transform_backward(): pl.pallas_call(lambda *refs: second_kernel(z, *refs), in_specs=[anywhere,...  122 us
    pallas_call x1, Pallas kernels, transform_forward(): pl.pallas_call(lambda *refs: first_kernel(z, *refs), in_specs=[whole_in,...  111 us
    pallas_call x1, Pallas kernels, settle_analysis(): pl.pallas_call(lambda *refs: analysis_kernel(z, bins, *refs), grid=(z.pai...  30.4 us
    pallas_call x1, Pallas kernels, synthesis_settle(): pl.pallas_call(lambda *refs: synthesis_kernel(z, bins, *refs), grid=(z.pa...  29.8 us
    mul x2, local copies, waits for them, and re-layouts, interleaved(): root[:, None, :, None] * jnp.eye(2, dtype=jnp.float32)[None, :, None, :]  16.9 us
    pallas_call x1, Pallas kernels, finish(): pl.pallas_call(lambda *refs: last_kernel(z, *refs), in_specs=[whole_in] *...  11.3 us
    mul x1, other arithmetic, interleaved(): root[:, None, :, None] * jnp.eye(2, dtype=jnp.float32)[None, :, None, :]  8.01 us
  transfers between devices with their start and end apart: 1, of which 0 were waited for; matrix products, arithmetic and copies ran while one was open for 8% of the time, Pallas kernels for 39%

profile of v1, /device:TPU:26, one launch (start us, length us, event | category | flops | bytes accessed | tf_op | source)
XLA Modules:
  0.0 364.5 jit_solution(4393203225209137815)
XLA Ops:
  0.6 0.7 convert_element_type.47
  1.4 0.7 convert_element_type.48
  2.1 0.8 fusion.25
  2.9 1.5 stack.23
  4.4 5.9 %all-to-all-start = ((f32[32,5,128]{2,1,0:T(8,128)}), f32[32,5,128]{2,1,0:T(8,128)S(1)}, u32[]{:S(2)}, u32[]{:S(2)}) async-start(f32[32,5,128]{2,1,0:T(8,128)} %stack.23), calls=%async_computation | async-start | bytes 262144 | tf_op jit(solution)/shard_map/all_to_all | solution.py:818
  10.3 0.7 tile.2
  10.9 0.1 broadcast_in_dim.67
  11.0 0.1 pad.5.clone
  11.1 0.7 maximum_maximum_fusion.1.refs_4_
  11.8 0.0 copy-start
  11.8 0.7 copy.24
  12.5 0.9 copy.25
  13.4 8.0 %broadcast_multiply_fusion = (f32[96,2,96,2]{3,2,1,0:T(8,128)}, f32[96,2,96,2]{3,2,1,0:T(8,128)}) fusion(f32[96,96]{1,0:T(8,128)S(1)} %copy.25, f32[2,2]{1,0:T(2,128)S(1)} %compare_convert_fusion, f32[96,96]{1,0:T(8,128)} %param.16), kind=kLoop, calls=%fused_computation.5 | loop fusion | flops 73728 | bytes 368656 | tf_op jit(solution)/shard_map/mul | solution.py:840
  21.4 0.0 copy-done
  21.4 8.5 %mul.101.refs_3_ = f32[192,192]{1,0:T(8,128)} reshape(f32[96,2,96,2]{3,2,1,0:T(8,128)} %get-tuple-element.18) | data formatting | bytes 294912 | tf_op jit(solution)/shard_map/mul | solution.py:840
  29.9 8.5 %mul.88.refs_2_ = f32[192,192]{1,0:T(8,128)} reshape(f32[96,2,96,2]{3,2,1,0:T(8,128)} %get-tuple-element.19) | data formatting | bytes 294912 | tf_op jit(solution)/shard_map/mul | solution.py:840
  38.3 0.0 copy-start.1
  38.3 111.1 %transform_forward.1 = f32[4,8,7,88,128]{4,3,2,1,0:T(8,128)} custom-call(f32[32,56,192]{2,1,0:T(8,128)} %refs_1_.5, f32[32,56,192]{2,1,0:T(8,128)} %refs_2_.1, f32[192,192]{1,0:T(8,128)} %mul.88.refs_2_, f32[56,448,256]{2,1,0:T(8,128)} %refs_1_.4), custom_call_target="tpu_custom_call" | custom-call | tf_op jit(solution)/shard_map/transform_forward/pallas_call | solution.py:415
  149.4 0.0 copy-done.1
  149.5 1.8 sine_multiply_fusion
  151.3 29.8 %synthesis_settle.1 = (f32[2,28,96,256]{3,2,1,0:T(8,128)}, f32[2,28,16,256]{3,2,1,0:T(8,128)}) custom-call(f32[19712,128]{1,0:T(8,128)} %bitcast.31, f32[224,256]{1,0:T(8,128)} %get-tuple-element.17.refs_1_.refs_3_, f32[224,256]{1,0:T(8,128)} %get-tuple-element.16.refs_2_.refs_4_, f32[2,28,96,256]{3,2,1,0:T(8,128)} %bitcast.33, f32[16,96]{1,0:T(8,128)} %copy-done), custom_call_target="tpu_custom_call" | custom-call | tf_op jit(solution)/shard_map/synthesis_settle/pallas_call | solution.py:479
  181.1 1.0 slice.33
  182.1 0.0 all-to-all-done
  182.1 0.1 fusion.31
  182.2 6.8 %fusion.17 = f32[4096]{0:T(1024)S(1)} fusion(s32[4096]{0:T(1024)S(1)} %get-tuple-element.13, s32[4096]{0:T(1024)S(1)} %get-tuple-element.14, f32[56,16,256]{2,1,0:T(8,128)} %bitcast.50), kind=kOutput, calls=%fused_computation.21 | convolution fusion | flops 5642121216 | bytes 507904 | tf_op jit(solution)/shard_map/dot_general | solution.py:783
  189.1 2.1 fusion.16
  191.2 2.7 fusion.5
  193.9 0.1 concatenate.13
  194.0 5.8 %fusion.3 = f32[448,256]{1,0:T(8,128)S(1)} fusion(s32[4096]{0:T(1024)S(1)} %get-tuple-element.13, f32[4096]{0:T(1024)S(1)} %get-tuple-element.11, s32[4096]{0:T(1024)S(1)} %get-tuple-element.14), kind=kOutput, calls=%fused_computation.7 | convolution fusion | flops 5642911744 | bytes 507904 | tf_op jit(solution)/shard_map/dot_general | solution.py:789
  199.8 1.1 maximum_maximum_fusion.refs_0_
  200.9 30.4 %settle_analysis.1 = f32[19712,128]{1,0:T(8,128)} custom-call(f32[2,28,16,256]{3,2,1,0:T(8,128)} %maximum_maximum_fusion.refs_0_, f32[2,28,96,256]{3,2,1,0:T(8,128)} %bitcast.34, f32[96,16]{1,0:T(8,128)} %bitcast.38, f32[224,256]{1,0:T(8,128)} %get-tuple-element.17.refs_1_.refs_3_, f32[224,256]{1,0:T(8,128)} %get-tuple-element.16.refs_2_.refs_4_), custom_call_target="tpu_custom_call" | custom-call | tf_op jit(solution)/shard_map/settle_analysis/pallas_call | solution.py:541
  231.3 122.0 %transform_backward.1 = f32[8,7,48,128]{3,2,1,0:T(8,128)} custom-call(f32[4,8,7,88,128]{4,3,2,1,0:T(8,128)} %bitcast.32, f32[56,448,256]{2,1,0:T(8,128)} %refs_1_.4), custom_call_target="tpu_custom_call" | custom-call | tf_op jit(solution)/shard_map/transform_backward/pallas_call | solution.py:705
  353.3 11.3 %finish.1 = f32[32,56,192]{2,1,0:T(8,128)} custom-call(f32[56,48,128]{2,1,0:T(8,128)} %bitcast.35, f32[32,56,192]{2,1,0:T(8,128)} %refs_1_.5, f32[32,56,192]{2,1,0:T(8,128)} %refs_2_.1, f32[192,192]{1,0:T(8,128)} %mul.101.refs_3_), custom_call_target="tpu_custom_call" | custom-call | tf_op jit(solution)/shard_map/finish/pallas_call | solution.py:758
  (7 shorter events, 0.1 us)
Async XLA Ops:
  4.4 177.8 %all-to-all-start = ((f32[32,5,128]{2,1,0:T(8,128)}), f32[32,5,128]{2,1,0:T(8,128)S(1)}, u32[]{:S(2)}, u32[]{:S(2)}) async-start(f32[32,5,128]{2,1,0:T(8,128)} %stack.23), calls=%async_computation | async-start | bytes 262144 | tf_op jit(solution)/shard_map/all_to_all | solution.py:818
  11.8 9.6 %copy-start = (f32[16,96]{1,0:T(8,128)}, f32[16,96]{1,0:T(8,128)S(1)}, u32[]{:S(2)}) copy-start(f32[16,96]{1,0:T(8,128)S(1)} %maximum_maximum_fusion.1.refs_4_) | copy-start | bytes 18436
  38.3 111.1 %copy-start.1 = (s32[224]{0:T(256)S(1)}, s32[224]{0:T(256)}, u32[]{:S(2)}) copy-start(s32[224]{0:T(256)} %param.18) | copy-start | bytes 2692

commit v2 on v1

--- a/solution.py
+++ b/solution.py
@@ -257,38 +257,80 @@
     )
 
 
+def interleaved(root):
+    channels = root.shape[0]
+    wide = 2 * channels
+    spread = (lax.broadcasted_iota(jnp.int32, (wide, channels), 0) // 2
+              == lax.broadcasted_iota(jnp.int32, (wide, channels), 1))
+    gather = (lax.broadcasted_iota(jnp.int32, (channels, wide), 1) // 2
+              == lax.broadcasted_iota(jnp.int32, (channels, wide), 0))
+    spread = jnp.where(spread, 1.0, 0.0).astype(bf16)
+    gather = jnp.where(gather, 1.0, 0.0).astype(bf16)
+    both = select_product(root, gather)
+    both = sum(jnp.dot(spread, piece, preferred_element_type=f32) for piece in reversed(split3(both)))
+    same = (lax.broadcasted_iota(jnp.int32, both.shape, 0) % 2) == (lax.broadcasted_iota(jnp.int32, both.shape, 1) % 2)
+    return jnp.where(same, both, 0.0)
+
+
 class Sizes:
     def __init__(self, modes, waves, width, lats, bands, wave_count):
         self.modes, self.waves, self.width, self.lats = modes, waves, width, lats
         self.bands, self.wave_count = bands, wave_count
-        self.own = waves // bands
+        self.group = bands // 2
+        self.own = waves // self.group
+        self.half_lats = lats * self.group
         self.pairs = lats // 2
         self.rows = -(-(3 * self.pairs) // 8) * 8
         self.in_rows = modes + modes // 2
         self.slots = waves * wave_count
 
 
+class Place:
+    def __init__(self, z):
+        self.w, self.b = lax.axis_index("wave"), lax.axis_index("band")
+        self.partner = self.w + 1 - 2 * (self.w % 2)
+        self.across = (self.w + 2) % z.wave_count
+        self.relay = (self.partner + 2) % z.wave_count
+        self.half, self.spot = self.b // z.group, self.b % z.group
+        self.z = z
+
+    def peer(self, d):
+        return (self.b + d) % self.z.bands
+
+    def near_spot(self, e):
+        return (self.spot + e) % self.z.group
+
+    def near(self, e):
+        return self.half * self.z.group + self.near_spot(e)
+
+    def greet(self):
+        barrier = pltpu.get_barrier_semaphore()
+        others = [(self.w, self.peer(d)) for d in range(1, self.z.bands)]
+        for wave, band in others + [(self.partner, self.b), (self.across, self.b)]:
+            pl.semaphore_signal(barrier, inc=1, device_id={"wave": wave, "band": band}, device_id_type=MESH_ID)
+        return barrier
+
+
+def remote(src, dst, send, recv, wave, band):
+    return pltpu.make_async_remote_copy(
+        src, dst, send, recv, device_id={"wave": wave, "band": band}, device_id_type=MESH_ID)
+
+
+AHEAD = 3
+
+
 def first_kernel(z, control_ref, scale_ref, root_ref, leg_ref, out_ref, s_a, s_b, send_u, recv_v, leg, y_a, y_b, send_y,
                  leg_sem, a1_send, a1_recv, a2_send, a2_recv, x_send, x_recv, c_send, c_recv):
-    w, b = lax.axis_index("wave"), lax.axis_index("band")
-    partner = w + 1 - 2 * (w % 2)
-    across = (w + 2) % z.wave_count
-    relay = (partner + 2) % z.wave_count
+    at_me = Place(z)
+    w, b = at_me.w, at_me.b
     half = LANES // 2
     quarter = LANES // 4
-
-    def peer(d):
-        return (b + d) % z.bands
-
-    leg_copy = pltpu.make_async_copy(leg_ref.at[pl.ds(b * z.own, z.own)], leg, leg_sem)
+    leg_copy = pltpu.make_async_copy(
+        leg_ref.at[pl.ds(at_me.spot * z.own, z.own), pl.ds(at_me.half * z.half_lats, z.half_lats)], leg, leg_sem)
     leg_copy.start()
-    barrier = pltpu.get_barrier_semaphore()
-    for d in range(1, z.bands):
-        pl.semaphore_signal(barrier, inc=1, device_id={"wave": w, "band": peer(d)}, device_id_type=MESH_ID)
-    for other in (partner, across):
-        pl.semaphore_signal(barrier, inc=1, device_id={"wave": other, "band": b}, device_id_type=MESH_ID)
-
-    root = split2(root_ref[...])
+    barrier = at_me.greet()
+
+    root = split2(interleaved(root_ref[...]))
     order = packed_order(z.width // 2, False)
     group = 8
 
@@ -303,84 +345,86 @@
 
     lax.fori_loop(0, z.modes // group, vertical, 0)
 
-    def pack(m, carry):
-        tall = s_b[pl.ds(m, z.modes, stride=z.waves), :]
+    def first_copy(c, d):
+        to = at_me.peer(d)
+        return remote(send_u.at[(to % z.group) * z.own + c], recv_v.at[b, c], a1_send.at[c, d], a1_recv.at[c, d], w, to)
+
+    def first_own(c):
+        return pltpu.make_async_copy(send_u.at[at_me.spot * z.own + c], recv_v.at[b, c], a1_send.at[c, 0])
+
+    def launch(c):
         low = z.modes // 2
-        send_u[m, : z.modes] = s_a[pl.ds(m, z.modes, stride=z.waves), :]
-        send_u[m, z.modes :] = tall[:low] + pltpu.roll(tall[low:], quarter, 1)
-        return carry
-
-    lax.fori_loop(0, z.waves, pack, 0)
-    pl.semaphore_wait(barrier, z.bands + 1)
-
-    def first_copy(d):
-        return pltpu.make_async_remote_copy(
-            send_u.at[pl.ds(peer(d) * z.own, z.own)], recv_v.at[b], a1_send.at[d], a1_recv.at[d],
-            device_id={"wave": w, "band": peer(d)}, device_id_type=MESH_ID)
-
-    first_own = pltpu.make_async_copy(send_u.at[pl.ds(b * z.own, z.own)], recv_v.at[b], a1_send.at[0])
-    for d in range(1, z.bands):
-        first_copy(d).start()
-    first_own.start()
-    leg_copy.wait()
-    first_own.wait()
-    for d in range(1, z.bands):
-        first_copy(d).wait_recv()
-
-    def second_copy(p, d):
-        return pltpu.make_async_remote_copy(
-            send_y.at[p, peer(d)], out_ref.at[w, b, p], a2_send.at[p, d], a2_recv.at[p, d],
-            device_id={"wave": w, "band": peer(d)}, device_id_type=MESH_ID)
-
-    def second_own(p):
-        return pltpu.make_async_copy(send_y.at[p, b], out_ref.at[w, b, p], a2_send.at[p, 0])
-
-    def across_copy(p):
-        return pltpu.make_async_remote_copy(
-            out_ref.at[w, :, p], out_ref.at[w, :, p], x_send.at[p], x_recv.at[p],
-            device_id={"wave": across, "band": b}, device_id_type=MESH_ID)
-
-    def core_copy(p, which):
-        block = w if which == 0 else across
-        return pltpu.make_async_remote_copy(
-            out_ref.at[block, :, p], out_ref.at[block, :, p], c_send.at[p, which], c_recv.at[p, which],
-            device_id={"wave": partner, "band": b}, device_id_type=MESH_ID)
-
-    def transform(p):
+        for spot in range(z.group):
+            m = spot * z.own + c
+            tall = s_b[pl.ds(m, z.modes, stride=z.waves), :]
+            send_u[m, : z.modes] = s_a[pl.ds(m, z.modes, stride=z.waves), :]
+            send_u[m, z.modes :] = tall[:low] + pltpu.roll(tall[low:], quarter, 1)
+        for d in range(1, z.bands):
+            first_copy(c, d).start()
+        first_own(c).start()
+
+    def second_copy(c, e):
+        return remote(send_y.at[c, at_me.near_spot(e)], out_ref.at[w, at_me.spot, c], a2_send.at[c, e], a2_recv.at[c, e],
+                      w, at_me.near(e))
+
+    def second_own(c):
+        return pltpu.make_async_copy(send_y.at[c, at_me.spot], out_ref.at[w, at_me.spot, c], a2_send.at[c, 0])
+
+    def across_copy(c):
+        return remote(out_ref.at[w, :, c], out_ref.at[w, :, c], x_send.at[c], x_recv.at[c], at_me.across, b)
+
+    def core_copy(c, which):
+        block = w if which == 0 else at_me.across
+        return remote(out_ref.at[block, :, c], out_ref.at[block, :, c], c_send.at[c, which], c_recv.at[c, which],
+                      at_me.partner, b)
+
+    def transform(c):
         tops, tails = [], []
         for s in range(z.bands):
-            tail = recv_v[s, p, z.modes :]
+            tail = recv_v[s, c, z.modes :]
             keep = lane_of(tail.shape) % half < quarter
-            tops.append(recv_v[s, p, : z.modes])
+            tops.append(recv_v[s, c, : z.modes])
             tails.append(jnp.where(keep, tail, 0.0))
             tails.append(jnp.where(keep, pltpu.roll(tail, LANES - quarter, 1), 0.0))
         x = jnp.concatenate([jnp.concatenate(tops, 0), jnp.concatenate(tails, 0)], 1)
-        y = product(split2(leg[p]), split2(x))
+        y = product(split2(leg[c]), split2(x))
         y_a[...] = y[:, :LANES]
         y_b[...] = y[:, LANES:]
-        for s in range(z.bands):
+        for s in range(z.group):
             at = s * z.lats
             one = y_a[at : at + z.pairs]
             two = y_a[at + z.pairs : at + z.lats]
             left = lane_of(one.shape) < half
-            send_y[p, s, z.rows - 8 :] = jnp.zeros((8, LANES), f32)
-            send_y[p, s, : z.pairs] = jnp.where(left, one, pltpu.roll(two, half, 1))
-            send_y[p, s, z.pairs : 2 * z.pairs] = jnp.where(left, pltpu.roll(one, half, 1), two)
-            send_y[p, s, 2 * z.pairs : 3 * z.pairs] = y_b[at : at + z.pairs] + pltpu.roll(
+            send_y[c, s, z.rows - 8 :] = jnp.zeros((8, LANES), f32)
+            send_y[c, s, : z.pairs] = jnp.where(left, one, pltpu.roll(two, half, 1))
+            send_y[c, s, z.pairs : 2 * z.pairs] = jnp.where(left, pltpu.roll(one, half, 1), two)
+            send_y[c, s, 2 * z.pairs : 3 * z.pairs] = y_b[at : at + z.pairs] + pltpu.roll(
                 y_b[at + z.pairs : at + z.lats], quarter, 1)
 
+    pl.semaphore_wait(barrier, z.bands + 1)
+    for c in range(min(AHEAD, z.own)):
+        launch(c)
+    leg_copy.wait()
+
     def phase(p, carry):
+        @pl.when(p + AHEAD < z.own)
+        def _():
+            launch(p + AHEAD)
+
         @pl.when(p < z.own)
         def _():
+            first_own(p).wait()
+            for d in range(1, z.bands):
+                first_copy(p, d).wait_recv()
             transform(p)
-            for d in range(1, z.bands):
-                second_copy(p, d).start()
+            for e in range(1, z.group):
+                second_copy(p, e).start()
             second_own(p).start()
 
         @pl.when((p >= 1) & (p <= z.own))
         def _():
-            for d in range(1, z.bands):
-                second_copy(p - 1, d).wait_recv()
+            for e in range(1, z.group):
+                second_copy(p - 1, e).wait_recv()
             second_own(p - 1).wait()
             across_copy(p - 1).start()
             core_copy(p - 1, 0).start()
@@ -393,15 +437,15 @@
         return carry
 
     lax.fori_loop(0, z.own + 2, phase, 0)
-    for d in range(1, z.bands):
-        first_copy(d).wait_send()
-
-    def drain(p, carry):
+
+    def drain(c, carry):
         for d in range(1, z.bands):
-            second_copy(p, d).wait_send()
-        across_copy(p).wait_send()
+            first_copy(c, d).wait_send()
+        for e in range(1, z.group):
+            second_copy(c, e).wait_send()
+        across_copy(c).wait_send()
         for which in range(2):
-            core_copy(p, which).wait()
+            core_copy(c, which).wait()
         return carry
 
     lax.fori_loop(0, z.own, drain, 0)
@@ -411,22 +455,21 @@
     whole_in = pl.BlockSpec(memory_space=pltpu.VMEM)
     anywhere = pl.BlockSpec(memory_space=pl.ANY)
     dma = pltpu.SemaphoreType.DMA
-    lats_all = z.lats * z.bands
     return pl.pallas_call(
         lambda *refs: first_kernel(z, *refs),
         in_specs=[whole_in, whole_in, whole_in, anywhere],
         out_specs=anywhere,
-        out_shape=jax.ShapeDtypeStruct((z.wave_count, z.bands, z.own, z.rows, LANES), f32),
+        out_shape=jax.ShapeDtypeStruct((z.wave_count, z.group, z.own, z.rows, LANES), f32),
         scratch_shapes=[
             pltpu.VMEM((z.modes * z.waves, LANES), f32),
             pltpu.VMEM((z.modes * z.waves, LANES), f32),
             pltpu.VMEM((z.waves, z.in_rows, LANES), f32),
             pltpu.VMEM((z.bands, z.own, z.in_rows, LANES), f32),
-            pltpu.VMEM((z.own, lats_all, z.modes * z.bands), f32),
-            pltpu.VMEM((lats_all, LANES), f32),
-            pltpu.VMEM((lats_all, LANES), f32),
-            pltpu.VMEM((z.own, z.bands, z.rows, LANES), f32),
-            dma(()), dma((z.bands,)), dma((z.bands,)), dma((z.own, z.bands)), dma((z.own, z.bands)),
+            pltpu.VMEM((z.own, z.half_lats, z.modes * z.bands), f32),
+            pltpu.VMEM((z.half_lats, LANES), f32),
+            pltpu.VMEM((z.half_lats, LANES), f32),
+            pltpu.VMEM((z.own, z.group, z.rows, LANES), f32),
+            dma(()), dma((z.own, z.bands)), dma((z.own, z.bands)), dma((z.own, z.group)), dma((z.own, z.group)),
             dma((z.own,)), dma((z.own,)), dma((z.own, 2)), dma((z.own, 2)),
         ],
         compiler_params=pltpu.CompilerParams(collective_id=0, has_side_effects=True, vmem_limit_bytes=VMEM_LIMIT),
@@ -549,149 +592,122 @@
         compiler_params=pltpu.CompilerParams(vmem_limit_bytes=VMEM_LIMIT),
         name="settle_analysis",
     )(resid.reshape(2, z.pairs, rows, lons), courant.reshape(2, z.pairs, channels, lons), proj_t, cosine, sine)
-    return out.reshape(z.wave_count, z.bands, z.own, z.rows, LANES)
+    return out.reshape(z.wave_count, z.group, z.own, z.rows, LANES)
 
 
 def second_kernel(z, part_ref, leg_ref, out_ref, part, r1, r2, v3, leg, z_all, send_u,
                   leg_sem, q_sem, c_send, c_recv, x_send, x_recv, a3_send, a3_recv, a4_send, a4_recv):
-    w, b = lax.axis_index("wave"), lax.axis_index("band")
-    partner = w + 1 - 2 * (w % 2)
-    across = (w + 2) % z.wave_count
-    relay = (partner + 2) % z.wave_count
+    at_me = Place(z)
+    w, b = at_me.w, at_me.b
     half = LANES // 2
     quarter = LANES // 4
-
-    def peer(d):
-        return (b + d) % z.bands
-
-    def target(q):
-        return (b + 1 + q) % z.bands
-
-    leg_copy = pltpu.make_async_copy(leg_ref.at[pl.ds(b * z.own, z.own)], leg, leg_sem)
-    barrier = pltpu.get_barrier_semaphore()
-    for d in range(1, z.bands):
-        pl.semaphore_signal(barrier, inc=1, device_id={"wave": w, "band": peer(d)}, device_id_type=MESH_ID)
-    for other in (partner, across):
-        pl.semaphore_signal(barrier, inc=1, device_id={"wave": other, "band": b}, device_id_type=MESH_ID)
-
-    def local_copy(q, which):
-        block = w if which == 0 else across
-        return pltpu.make_async_copy(part_ref.at[block, target(q)], part.at[q, which], q_sem.at[q, which])
-
-    def core_copy(q, which):
-        block = partner if which == 0 else relay
-        return pltpu.make_async_remote_copy(
-            part_ref.at[block, target(q)], r1.at[q, which], c_send.at[q, which], c_recv.at[q, which],
-            device_id={"wave": partner, "band": b}, device_id_type=MESH_ID)
-
-    def across_copy(q):
-        return pltpu.make_async_remote_copy(
-            part.at[q, 1], r2.at[q], x_send.at[q], x_recv.at[q],
-            device_id={"wave": across, "band": b}, device_id_type=MESH_ID)
-
-    def third_copy(q):
-        return pltpu.make_async_remote_copy(
-            part.at[q, 0], v3.at[b], a3_send.at[q], a3_recv.at[q],
-            device_id={"wave": w, "band": target(q)}, device_id_type=MESH_ID)
-
-    pl.semaphore_wait(barrier, z.bands + 1)
-
-    def begin(q, carry):
-        for which in (1, 0):
-            core_copy(q, which).start()
-            local_copy(q, which).start()
-        return carry
-
-    lax.fori_loop(0, z.bands, begin, 0)
-    leg_copy.start()
-
-    def stage(q, carry):
-        @pl.when(q < z.bands)
-        def _():
-            local_copy(q, 1).wait()
-            core_copy(q, 1).wait_recv()
-
-            def add(p, inner):
-                part[q, 1, p] = part[q, 1, p] + r1[q, 1, p]
-                return inner
-
-            lax.fori_loop(0, z.own, add, 0)
-            across_copy(q).start()
-
-        @pl.when(q >= 1)
-        def _():
-            k = q - 1
-            local_copy(k, 0).wait()
-            core_copy(k, 0).wait_recv()
-            across_copy(k).wait_recv()
-
-            def add(p, inner):
-                part[k, 0, p] = part[k, 0, p] + r1[k, 0, p] + r2[k, p]
-                return inner
-
-            lax.fori_loop(0, z.own, add, 0)
-
-            @pl.when(k < z.bands - 1)
-            def _():
-                third_copy(k).start()
-
-        return carry
-
-    lax.fori_loop(0, z.bands + 1, stage, 0)
-    own_copy = pltpu.make_async_copy(part.at[z.bands - 1, 0], v3.at[b], a3_send.at[z.bands - 1])
-    own_copy.start()
-    leg_copy.wait()
-    own_copy.wait()
-    for q in range(z.bands - 1):
-        third_copy(q).wait_recv()
-
-    def fourth_copy(p, d):
-        return pltpu.make_async_remote_copy(
-            send_u.at[p, peer(d)], out_ref.at[b, p], a4_send.at[p, d], a4_recv.at[p, d],
-            device_id={"wave": w, "band": peer(d)}, device_id_type=MESH_ID)
-
-    def fourth_own(p):
-        return pltpu.make_async_copy(send_u.at[p, b], out_ref.at[b, p], a4_send.at[p, 0])
-
-    def transform(p, carry):
-        for s in range(z.bands):
+    leg_copy = pltpu.make_async_copy(
+        leg_ref.at[pl.ds(at_me.spot * z.own, z.own), pl.ds(at_me.half * z.half_lats, z.half_lats)], leg, leg_sem)
+    barrier = at_me.greet()
+
+    def local_copy(c, which):
+        block = w if which == 0 else at_me.across
+        return pltpu.make_async_copy(part_ref.at[block, :, c], part.at[c, which], q_sem.at[c, which])
+
+    def core_copy(c, which):
+        block = at_me.partner if which == 0 else at_me.relay
+        return remote(part_ref.at[block, :, c], r1.at[c, which], c_send.at[c, which], c_recv.at[c, which], at_me.partner, b)
+
+    def across_copy(c):
+        return remote(part.at[c, 1], r2.at[c], x_send.at[c], x_recv.at[c], at_me.across, b)
+
+    def third_copy(c, e):
+        return remote(part.at[c, 0, at_me.near_spot(e)], v3.at[at_me.spot, c], a3_send.at[c, e], a3_recv.at[c, e],
+                      w, at_me.near(e))
+
+    def third_own(c):
+        return pltpu.make_async_copy(part.at[c, 0, at_me.spot], v3.at[at_me.spot, c], a3_send.at[c, 0])
+
+    def fourth_copy(c, d):
+        return remote(send_u.at[c, at_me.peer(d)], out_ref.at[at_me.half, at_me.spot, c], a4_send.at[c, d],
+                      a4_recv.at[c, d], w, at_me.peer(d))
+
+    def fourth_own(c):
+        return pltpu.make_async_copy(send_u.at[c, b], out_ref.at[at_me.half, at_me.spot, c], a4_send.at[c, 0])
+
+    def transform(c):
+        for s in range(z.group):
             at = s * z.lats
-            real = v3[s, p, : z.pairs]
-            imag = v3[s, p, z.pairs : 2 * z.pairs]
-            tail = v3[s, p, 2 * z.pairs : 3 * z.pairs]
+            real = v3[s, c, : z.pairs]
+            imag = v3[s, c, z.pairs : 2 * z.pairs]
+            tail = v3[s, c, 2 * z.pairs : 3 * z.pairs]
             lane = lane_of(real.shape)
             keep = lane % half < quarter
             z_all[at : at + z.pairs, :LANES] = jnp.where(lane < half, real, pltpu.roll(imag, half, 1))
             z_all[at + z.pairs : at + z.lats, :LANES] = jnp.where(lane < half, pltpu.roll(real, half, 1), imag)
             z_all[at : at + z.pairs, LANES:] = jnp.where(keep, tail, 0.0)
             z_all[at + z.pairs : at + z.lats, LANES:] = jnp.where(keep, pltpu.roll(tail, LANES - quarter, 1), 0.0)
-        y = product(split2(leg[p]), split2(z_all[...]), ((0,), (0,)))
+        y = product(split2(leg[c]), split2(z_all[...]), ((0,), (0,)))
+        low = z.modes // 2
         for s in range(z.bands):
             rows = y[s * z.modes : (s + 1) * z.modes]
-            low = z.modes // 2
-            send_u[p, s, : z.modes] = rows[:, :LANES]
-            send_u[p, s, z.modes :] = rows[:low, LANES:] + pltpu.roll(rows[low:, LANES:], quarter, 1)
+            send_u[c, s, : z.modes] = rows[:, :LANES]
+            send_u[c, s, z.modes :] = rows[:low, LANES:] + pltpu.roll(rows[low:, LANES:], quarter, 1)
+
+    pl.semaphore_wait(barrier, z.bands + 1)
+
+    def begin(c, carry):
+        for which in (1, 0):
+            core_copy(c, which).start()
+            local_copy(c, which).start()
+        return carry
+
+    lax.fori_loop(0, z.own, begin, 0)
+    leg_copy.start()
+
+    def phase(p, carry):
+        @pl.when(p < z.own)
+        def _():
+            local_copy(p, 1).wait()
+            core_copy(p, 1).wait_recv()
+            part[p, 1] = part[p, 1] + r1[p, 1]
+            across_copy(p).start()
+
+        @pl.when((p >= 1) & (p <= z.own))
+        def _():
+            c = p - 1
+            local_copy(c, 0).wait()
+            core_copy(c, 0).wait_recv()
+            part[c, 0] = part[c, 0] + r1[c, 0]
+            across_copy(c).wait_recv()
+            part[c, 0] = part[c, 0] + r2[c]
+            for e in range(1, z.group):
+                third_copy(c, e).start()
+            third_own(c).start()
+
+        @pl.when(p == 2)
+        def _():
+            leg_copy.wait()
+
+        @pl.when(p >= 2)
+        def _():
+            c = p - 2
+            third_own(c).wait()
+            for e in range(1, z.group):
+                third_copy(c, e).wait_recv()
+            transform(c)
+            for d in range(1, z.bands):
+                fourth_copy(c, d).start()
+            fourth_own(c).start()
+
+        return carry
+
+    lax.fori_loop(0, z.own + 2, phase, 0)
+
+    def drain(c, carry):
+        across_copy(c).wait_send()
+        for which in range(2):
+            core_copy(c, which).wait_send()
+        for e in range(1, z.group):
+            third_copy(c, e).wait_send()
         for d in range(1, z.bands):
-            fourth_copy(p, d).start()
-        fourth_own(p).start()
-        return carry
-
-    lax.fori_loop(0, z.own, transform, 0)
-
-    def drain_sums(q, carry):
-        across_copy(q).wait_send()
-        for which in range(2):
-            core_copy(q, which).wait_send()
-        return carry
-
-    lax.fori_loop(0, z.bands, drain_sums, 0)
-    for q in range(z.bands - 1):
-        third_copy(q).wait_send()
-
-    def drain(p, carry):
-        for d in range(1, z.bands):
-            fourth_copy(p, d).wait()
-        fourth_own(p).wait()
+            fourth_copy(c, d).wait()
+        fourth_own(c).wait()
         return carry
 
     lax.fori_loop(0, z.own, drain, 0)
@@ -700,23 +716,22 @@
 def transform_backward(z, part, legendre):
     anywhere = pl.BlockSpec(memory_space=pl.ANY)
     dma = pltpu.SemaphoreType.DMA
-    lats_all = z.lats * z.bands
-    slab = (z.own, z.rows, LANES)
+    slab = (z.rows, LANES)
     return pl.pallas_call(
         lambda *refs: second_kernel(z, *refs),
         in_specs=[anywhere, anywhere],
         out_specs=anywhere,
-        out_shape=jax.ShapeDtypeStruct((z.bands, z.own, z.in_rows, LANES), f32),
+        out_shape=jax.ShapeDtypeStruct((2, z.group, z.own, z.in_rows, LANES), f32),
         scratch_shapes=[
-            pltpu.VMEM((z.bands, 2) + slab, f32),
-            pltpu.VMEM((z.bands, 2) + slab, f32),
-            pltpu.VMEM((z.bands,) + slab, f32),
-            pltpu.VMEM((z.bands,) + slab, f32),
-            pltpu.VMEM((z.own, lats_all, z.modes * z.bands), f32),
-            pltpu.VMEM((lats_all, 2 * LANES), f32),
+            pltpu.VMEM((z.own, 2, z.group) + slab, f32),
+            pltpu.VMEM((z.own, 2, z.group) + slab, f32),
+            pltpu.VMEM((z.own, z.group) + slab, f32),
+            pltpu.VMEM((z.group, z.own) + slab, f32),
+            pltpu.VMEM((z.own, z.half_lats, z.modes * z.bands), f32),
+            pltpu.VMEM((z.half_lats, 2 * LANES), f32),
             pltpu.VMEM((z.own, z.bands, z.in_rows, LANES), f32),
-            dma(()), dma((z.bands, 2)), dma((z.bands, 2)), dma((z.bands, 2)), dma((z.bands,)), dma((z.bands,)),
-            dma((z.bands,)), dma((z.bands,)), dma((z.own, z.bands)), dma((z.own, z.bands)),
+            dma(()), dma((z.own, 2)), dma((z.own, 2)), dma((z.own, 2)), dma((z.own,)), dma((z.own,)),
+            dma((z.own, z.group)), dma((z.own, z.group)), dma((z.own, z.bands)), dma((z.own, z.bands)),
         ],
         compiler_params=pltpu.CompilerParams(collective_id=1, has_side_effects=True, vmem_limit_bytes=VMEM_LIMIT),
         name="transform_backward",
@@ -728,16 +743,17 @@
     quarter = LANES // 4
 
     def unpack(m, carry):
-        tail = slabs_ref[m, z.modes :]
+        slab = slabs_ref[0, m] + slabs_ref[1, m]
+        tail = slab[z.modes :]
         keep = lane_of(tail.shape) % half < quarter
         both = jnp.concatenate(
             [jnp.where(keep, tail, 0.0), jnp.where(keep, pltpu.roll(tail, LANES - quarter, 1), 0.0)], 0)
-        s_a[pl.ds(m, z.modes, stride=z.waves), :] = slabs_ref[m, : z.modes]
+        s_a[pl.ds(m, z.modes, stride=z.waves), :] = slab[: z.modes]
         s_b[pl.ds(m, z.modes, stride=z.waves), :] = both
         return carry
 
     lax.fori_loop(0, z.waves, unpack, 0)
-    root = split2(root_ref[...])
+    root = split2(interleaved(root_ref[...]))
     order = packed_order(z.width // 2, True)
     group = 8
 
@@ -745,7 +761,7 @@
         at = pl.ds(pl.multiple_of(i * group * z.waves, 8), group * z.waves)
         placed = jnp.concatenate([s_a[at, :], s_b[at, :]], 1)
         scale = scale_ref[pl.ds(i * group, group)].reshape(group * z.waves, z.width)
-        mixed = product(split2(scale * select_product(placed, order)), root)
+        mixed = product(split2(scale * select_product(placed, order)), root, ((1,), (1,)))
         out_ref[pl.ds(i * group, group)] = control_ref[pl.ds(i * group, group)] + mixed.reshape(
             group, z.waves, z.width)
         return carry
@@ -753,7 +769,7 @@
     lax.fori_loop(0, z.modes // group, vertical, 0)
 
 
-def finish(z, slabs, control, scale, root_t):
+def finish(z, slabs, control, scale, root):
     whole_in = pl.BlockSpec(memory_space=pltpu.VMEM)
     return pl.pallas_call(
         lambda *refs: last_kernel(z, *refs),
@@ -763,7 +779,7 @@
         scratch_shapes=[pltpu.VMEM((z.modes * z.waves, LANES), f32)] * 2,
         compiler_params=pltpu.CompilerParams(vmem_limit_bytes=VMEM_LIMIT),
         name="finish",
-    )(slabs.reshape(z.waves, z.in_rows, LANES), control, scale, root_t)
+    )(slabs.reshape(2, z.waves, z.in_rows, LANES), control, scale, root)
 
 
 def observation_sums(z, tracer_shape, model, arrived, lidar_coef, levels_here, proj_rows):
@@ -833,12 +849,6 @@
         ],
         axis=0,
     )
-
-
-def interleaved(root):
-    channels = root.shape[0]
-    wide = root[:, None, :, None] * jnp.eye(2, dtype=jnp.float32)[None, :, None, :]
-    return wide.reshape(2 * channels, 2 * channels)
 
 
 def fast_body(
@@ -868,12 +878,12 @@
     arrived = observation_packet(obs_count, obs_column, obs_level, lidar_obs, aod_obs, obs_weight)
     cosine, sine = trig_tables(zonal_number, lon_first, lon_here, lon_here * wave_count, factor)
     proj = projection(lidar_coef, aod_coef)
-    slabs = transform_forward(z, control, spectral_scale, interleaved(vertical_root), legendre)
+    slabs = transform_forward(z, control, spectral_scale, vertical_root, legendre)
     tracer, model = synthesis_settle(z, slabs, cosine, sine, courant, proj, bins)
     resid = observation_sums(z, (lats_here, lon_here), model, arrived, lidar_coef, levels_here, proj.shape[0])
     part = settle_analysis(z, resid, courant, proj.T, cosine, sine, bins)
     back = transform_backward(z, part, legendre)
-    return finish(z, back, control, spectral_scale, interleaved(vertical_root.T)), tracer
+    return finish(z, back, control, spectral_scale, vertical_root), tracer
 
 
 def fits(mesh, control, courant):
@@ -882,7 +892,8 @@
     lats_here, channels = courant[0] // bands, courant[1]
     return (
         waves == 4
-        and waves_here % bands == 0
+        and bands % 2 == 0
+        and waves_here % (bands // 2) == 0
         and waves_here % 8 == 0
         and modes_here % 16 == 0
         and lats_here % 8 == 0

time: 366 us -> 297 us (0.81)
  the two profiles are of different devices: /device:TPU:26 before, /device:TPU:0 now
where the time goes in v2:
time: 297 us; the launch traced here: 295 us
  Pallas kernels  259 us (87%)
  matrix products  17.4 us (6%)
  starting transfers between devices  7.33 us (2%)
  other arithmetic  6 us (2%)
  local copies, waits for them, and re-layouts  4.14 us (1%)
    pallas_call x1, Pallas kernels, transform_forward(): pl.pallas_call(lambda *refs: first_kernel(z, *refs), in_specs=[whole_in,...  97.3 us
    pallas_call x1, Pallas kernels, transform_backward(): pl.pallas_call(lambda *refs: second_kernel(z, *refs), in_specs=[anywhere,...  89.7 us
    pallas_call x1, Pallas kernels, settle_analysis(): pl.pallas_call(lambda *refs: analysis_kernel(z, bins, *refs), grid=(z.pai...  30.3 us
    pallas_call x1, Pallas kernels, synthesis_settle(): pl.pallas_call(lambda *refs: synthesis_kernel(z, bins, *refs), grid=(z.pa...  29.8 us
    pallas_call x1, Pallas kernels, finish(): pl.pallas_call(lambda *refs: last_kernel(z, *refs), in_specs=[whole_in] *...  12.2 us
    all_to_all x1, starting transfers between devices, observation_packet(): lax.all_to_all(packet, ('wave', 'band'), split_axis=0, concat_axis=0, til...  7.33 us
    dot_general x1, matrix products, observation_sums(): lidar_rows = jnp.dot(cell_hot, lidar_field, precision=highest)  6.84 us
  transfers between devices with their start and end apart: 1, of which 0 were waited for; matrix products, arithmetic and copies ran while one was open for 2% of the time, Pallas kernels for 43%

profile of v2, /device:TPU:0, one launch (start us, length us, event | category | flops | bytes accessed | tf_op | source)
XLA Modules:
  0.0 295.1 jit_solution(17816566328205456191)
XLA Ops:
  0.6 0.7 convert_element_type.37
  1.4 0.7 convert_element_type.38
  2.1 0.8 fusion.25
  2.9 1.5 stack.23
  4.4 7.3 %all-to-all-start = ((f32[32,5,128]{2,1,0:T(8,128)}), f32[32,5,128]{2,1,0:T(8,128)S(1)}, u32[]{:S(2)}, u32[]{:S(2)}) async-start(f32[32,5,128]{2,1,0:T(8,128)} %stack.23), calls=%async_computation | async-start | bytes 262144 | tf_op jit(solution)/shard_map/all_to_all | solution.py:834
  11.7 0.7 tile.2
  12.4 0.1 broadcast_in_dim.63
  12.5 0.1 pad.5.clone
  12.6 0.7 maximum_maximum_fusion.1.refs_4_
  13.3 0.0 copy-start
  13.3 0.7 copy.21
  14.0 0.0 copy-start.1
  14.0 97.3 %transform_forward.1 = f32[4,4,14,88,128]{4,3,2,1,0:T(8,128)} custom-call(f32[32,56,192]{2,1,0:T(8,128)} %refs_1_.5, f32[32,56,192]{2,1,0:T(8,128)} %refs_2_.3, f32[96,96]{1,0:T(8,128)} %refs_3_.3, f32[56,448,256]{2,1,0:T(8,128)} %refs_1_.4), custom_call_target="tpu_custom_call" | custom-call | tf_op jit(solution)/shard_map/transform_forward/pallas_call | solution.py:458
  111.3 0.0 copy-done
  111.3 0.0 copy-done.1
  111.3 1.8 sine_multiply_fusion
  113.2 29.8 %synthesis_settle.1 = (f32[2,28,96,256]{3,2,1,0:T(8,128)}, f32[2,28,16,256]{3,2,1,0:T(8,128)}) custom-call(f32[19712,128]{1,0:T(8,128)} %bitcast.26, f32[224,256]{1,0:T(8,128)} %get-tuple-element.17.refs_1_.refs_3_, f32[224,256]{1,0:T(8,128)} %get-tuple-element.16.refs_2_.refs_4_, f32[2,28,96,256]{3,2,1,0:T(8,128)} %bitcast.28, f32[16,96]{1,0:T(8,128)} %copy-done), custom_call_target="tpu_custom_call" | custom-call | tf_op jit(solution)/shard_map/synthesis_settle/pallas_call | solution.py:522
  143.0 1.0 slice.33
  144.0 0.0 all-to-all-done
  144.0 0.1 fusion.31
  144.1 6.8 %fusion.17 = f32[4096]{0:T(1024)S(1)} fusion(s32[4096]{0:T(1024)S(1)} %get-tuple-element.13, s32[4096]{0:T(1024)S(1)} %get-tuple-element.14, f32[56,16,256]{2,1,0:T(8,128)} %bitcast.44), kind=kOutput, calls=%fused_computation.19 | convolution fusion | flops 5642121216 | bytes 507904 | tf_op jit(solution)/shard_map/dot_general | solution.py:799
  151.0 2.1 fusion.16
  153.1 2.7 fusion.5
  155.8 0.1 concatenate.13
  155.9 5.8 %fusion.3 = f32[448,256]{1,0:T(8,128)S(1)} fusion(s32[4096]{0:T(1024)S(1)} %get-tuple-element.13, f32[4096]{0:T(1024)S(1)} %get-tuple-element.11, s32[4096]{0:T(1024)S(1)} %get-tuple-element.14), kind=kOutput, calls=%fused_computation.5 | convolution fusion | flops 5642911744 | bytes 507904 | tf_op jit(solution)/shard_map/dot_general | solution.py:805
  161.7 1.1 maximum_maximum_fusion.refs_0_
  162.8 30.3 %settle_analysis.1 = f32[19712,128]{1,0:T(8,128)} custom-call(f32[2,28,16,256]{3,2,1,0:T(8,128)} %maximum_maximum_fusion.refs_0_, f32[2,28,96,256]{3,2,1,0:T(8,128)} %bitcast.29, f32[96,16]{1,0:T(8,128)} %bitcast.32, f32[224,256]{1,0:T(8,128)} %get-tuple-element.17.refs_1_.refs_3_, f32[224,256]{1,0:T(8,128)} %get-tuple-element.16.refs_2_.refs_4_), custom_call_target="tpu_custom_call" | custom-call | tf_op jit(solution)/shard_map/settle_analysis/pallas_call | solution.py:584
  193.1 89.7 %transform_backward.1 = f32[2,4,14,48,128]{4,3,2,1,0:T(8,128)} custom-call(f32[4,4,14,88,128]{4,3,2,1,0:T(8,128)} %bitcast.27, f32[56,448,256]{2,1,0:T(8,128)} %refs_1_.4), custom_call_target="tpu_custom_call" | custom-call | tf_op jit(solution)/shard_map/transform_backward/pallas_call | solution.py:720
  282.9 12.2 %finish.1 = f32[32,56,192]{2,1,0:T(8,128)} custom-call(f32[2,56,48,128]{3,2,1,0:T(8,128)} %bitcast.30, f32[32,56,192]{2,1,0:T(8,128)} %refs_1_.5, f32[32,56,192]{2,1,0:T(8,128)} %refs_2_.3, f32[96,96]{1,0:T(8,128)} %refs_3_.3), custom_call_target="tpu_custom_call" | custom-call | tf_op jit(solution)/shard_map/finish/pallas_call | solution.py:774
  (6 shorter events, 0.1 us)
Async XLA Ops:
  4.4 139.7 %all-to-all-start = ((f32[32,5,128]{2,1,0:T(8,128)}), f32[32,5,128]{2,1,0:T(8,128)S(1)}, u32[]{:S(2)}, u32[]{:S(2)}) async-start(f32[32,5,128]{2,1,0:T(8,128)} %stack.23), calls=%async_computation | async-start | bytes 262144 | tf_op jit(solution)/shard_map/all_to_all | solution.py:834
  13.3 98.0 %copy-start = (f32[16,96]{1,0:T(8,128)}, f32[16,96]{1,0:T(8,128)S(1)}, u32[]{:S(2)}) copy-start(f32[16,96]{1,0:T(8,128)S(1)} %maximum_maximum_fusion.1.refs_4_) | copy-start | bytes 18436
  14.0 97.3 %copy-start.1 = (s32[224]{0:T(256)S(1)}, s32[224]{0:T(256)}, u32[]{:S(2)}) copy-start(s32[224]{0:T(256)} %param.18) | copy-start | bytes 2692

commit v3 on v2

--- a/solution.py
+++ b/solution.py
@@ -316,66 +316,111 @@
         src, dst, send, recv, device_id={"wave": wave, "band": band}, device_id_type=MESH_ID)
 
 
-AHEAD = 3
-
-
-def first_kernel(z, control_ref, scale_ref, root_ref, leg_ref, out_ref, s_a, s_b, send_u, recv_v, leg, y_a, y_b, send_y,
-                 leg_sem, a1_send, a1_recv, a2_send, a2_recv, x_send, x_recv, c_send, c_recv):
+AHEAD = 2
+LAG_SPREAD = 2
+LAG_ACROSS = 2
+GROUP_ROWS = 8
+
+
+def first_kernel(z, control_ref, scale_ref, root_ref, leg_ref, count_ref, column_ref, level_ref, lidar_ref, aod_ref,
+                 weight_ref, out_ref, seen_ref, control, scale, s_a, s_b, send_u, recv_v, leg, y_a, y_b, send_y, packet,
+                 leg_sem, in_sem, o_send, o_recv, a1_send, a1_recv, a2_send, a2_recv, x_send, x_recv, c_send, c_recv):
     at_me = Place(z)
     w, b = at_me.w, at_me.b
     half = LANES // 2
     quarter = LANES // 4
+    phases = GROUP_ROWS // z.group
+    groups = z.waves // GROUP_ROWS
+    devices = z.wave_count * z.bands
+    me = w * z.bands + b
+
+    def input_copy(i, which):
+        source, target = ((control_ref, control), (scale_ref, scale))[which]
+        return pltpu.make_async_copy(
+            source.at[:, pl.ds(i * GROUP_ROWS, GROUP_ROWS), :], target.at[i], in_sem.at[i, which])
+
+    for i in range(groups):
+        for which in range(2):
+            input_copy(i, which).start()
     leg_copy = pltpu.make_async_copy(
-        leg_ref.at[pl.ds(at_me.spot * z.own, z.own), pl.ds(at_me.half * z.half_lats, z.half_lats)], leg, leg_sem)
+        leg_ref.at[:, at_me.spot, pl.ds(at_me.half * z.half_lats, z.half_lats)], leg, leg_sem)
     leg_copy.start()
-    barrier = at_me.greet()
+    barrier = pltpu.get_barrier_semaphore()
+
+    def greet(e, carry):
+        to = (me + e) % devices
+        pl.semaphore_signal(barrier, inc=1, device_id={"wave": to // z.bands, "band": to % z.bands},
+                            device_id_type=MESH_ID)
+        return carry
+
+    lax.fori_loop(1, devices, greet, 0)
+
+    counts = jnp.broadcast_to(count_ref[...], (devices, devices))
+    diagonal = lax.broadcasted_iota(jnp.int32, counts.shape, 0) == lax.broadcasted_iota(jnp.int32, counts.shape, 1)
+    counts = jnp.sum(jnp.where(diagonal, counts, 0).astype(f32), axis=1, keepdims=True)
+    weights = weight_ref[...]
+    live = lax.broadcasted_iota(jnp.int32, weights.shape, 1).astype(f32) < counts
+    fields = (column_ref[...].astype(f32), level_ref[...].astype(f32), lidar_ref[...], aod_ref[...],
+              jnp.where(live, weights, 0.0))
+    for k in range(GROUP_ROWS):
+        value = fields[k] if k < len(fields) else jnp.zeros_like(weights)
+        packet[pl.ds(k, devices, stride=GROUP_ROWS), :] = value
+
+    def packet_copy(e):
+        to = (me + e) % devices
+        return remote(packet.at[pl.ds(to * GROUP_ROWS, GROUP_ROWS)], seen_ref.at[pl.ds(me * GROUP_ROWS, GROUP_ROWS)],
+                      o_send.at[e], o_recv.at[e], to // z.bands, to % z.bands)
+
+    packet_own = pltpu.make_async_copy(
+        packet.at[pl.ds(me * GROUP_ROWS, GROUP_ROWS)], seen_ref.at[pl.ds(me * GROUP_ROWS, GROUP_ROWS)], o_send.at[0])
 
     root = split2(interleaved(root_ref[...]))
     order = packed_order(z.width // 2, False)
-    group = 8
-
-    def vertical(i, carry):
-        x = control_ref[pl.ds(i * group, group)].reshape(group * z.waves, z.width)
-        scale = scale_ref[pl.ds(i * group, group)].reshape(group * z.waves, z.width)
-        placed = select_product(scale * product(split2(x), root), order)
-        at = pl.ds(pl.multiple_of(i * group * z.waves, 8), group * z.waves)
-        s_a[at, :] = placed[:, :LANES]
-        s_b[at, :] = placed[:, LANES:]
-        return carry
-
-    lax.fori_loop(0, z.modes // group, vertical, 0)
+
+    def vertical(i):
+        for which in range(2):
+            input_copy(i, which).wait()
+        x = control[i].reshape(z.modes * GROUP_ROWS, z.width)
+        y = scale[i].reshape(z.modes * GROUP_ROWS, z.width)
+        placed = select_product(y * product(split2(x), root), order)
+        s_a[...] = placed[:, :LANES]
+        s_b[...] = placed[:, LANES:]
 
     def first_copy(c, d):
         to = at_me.peer(d)
-        return remote(send_u.at[(to % z.group) * z.own + c], recv_v.at[b, c], a1_send.at[c, d], a1_recv.at[c, d], w, to)
+        return remote(send_u.at[c, to % z.group], recv_v.at[b, c], a1_send.at[c, d], a1_recv.at[c, d], w, to)
 
     def first_own(c):
-        return pltpu.make_async_copy(send_u.at[at_me.spot * z.own + c], recv_v.at[b, c], a1_send.at[c, 0])
+        return pltpu.make_async_copy(send_u.at[c, at_me.spot], recv_v.at[b, c], a1_send.at[c, 0])
 
     def launch(c):
+        @pl.when(c % phases == 0)
+        def _():
+            vertical(c // phases)
+
         low = z.modes // 2
         for spot in range(z.group):
-            m = spot * z.own + c
-            tall = s_b[pl.ds(m, z.modes, stride=z.waves), :]
-            send_u[m, : z.modes] = s_a[pl.ds(m, z.modes, stride=z.waves), :]
-            send_u[m, z.modes :] = tall[:low] + pltpu.roll(tall[low:], quarter, 1)
+            at = pl.ds(c % phases * z.group + spot, z.modes, stride=GROUP_ROWS)
+            tall = s_b[at, :]
+            send_u[c, spot, : z.modes] = s_a[at, :]
+            send_u[c, spot, z.modes :] = tall[:low] + pltpu.roll(tall[low:], quarter, 1)
         for d in range(1, z.bands):
             first_copy(c, d).start()
         first_own(c).start()
 
     def second_copy(c, e):
-        return remote(send_y.at[c, at_me.near_spot(e)], out_ref.at[w, at_me.spot, c], a2_send.at[c, e], a2_recv.at[c, e],
+        return remote(send_y.at[c, at_me.near_spot(e)], out_ref.at[w, c, at_me.spot], a2_send.at[c, e], a2_recv.at[c, e],
                       w, at_me.near(e))
 
     def second_own(c):
-        return pltpu.make_async_copy(send_y.at[c, at_me.spot], out_ref.at[w, at_me.spot, c], a2_send.at[c, 0])
+        return pltpu.make_async_copy(send_y.at[c, at_me.spot], out_ref.at[w, c, at_me.spot], a2_send.at[c, 0])
 
     def across_copy(c):
-        return remote(out_ref.at[w, :, c], out_ref.at[w, :, c], x_send.at[c], x_recv.at[c], at_me.across, b)
+        return remote(out_ref.at[w, c], out_ref.at[w, c], x_send.at[c], x_recv.at[c], at_me.across, b)
 
     def core_copy(c, which):
         block = w if which == 0 else at_me.across
-        return remote(out_ref.at[block, :, c], out_ref.at[block, :, c], c_send.at[c, which], c_recv.at[c, which],
+        return remote(out_ref.at[block, c], out_ref.at[block, c], c_send.at[c, which], c_recv.at[c, which],
                       at_me.partner, b)
 
     def transform(c):
@@ -401,9 +446,16 @@
             send_y[c, s, 2 * z.pairs : 3 * z.pairs] = y_b[at : at + z.pairs] + pltpu.roll(
                 y_b[at + z.pairs : at + z.lats], quarter, 1)
 
-    pl.semaphore_wait(barrier, z.bands + 1)
+    pl.semaphore_wait(barrier, devices - 1)
     for c in range(min(AHEAD, z.own)):
         launch(c)
+
+    def send_packet(e, carry):
+        packet_copy(e).start()
+        return carry
+
+    lax.fori_loop(1, devices, send_packet, 0)
+    packet_own.start()
     leg_copy.wait()
 
     def phase(p, carry):
@@ -421,22 +473,24 @@
                 second_copy(p, e).start()
             second_own(p).start()
 
-        @pl.when((p >= 1) & (p <= z.own))
+        @pl.when((p >= LAG_SPREAD) & (p < z.own + LAG_SPREAD))
         def _():
+            c = p - LAG_SPREAD
             for e in range(1, z.group):
-                second_copy(p - 1, e).wait_recv()
-            second_own(p - 1).wait()
-            across_copy(p - 1).start()
-            core_copy(p - 1, 0).start()
-
-        @pl.when(p >= 2)
+                second_copy(c, e).wait_recv()
+            second_own(c).wait()
+            across_copy(c).start()
+            core_copy(c, 0).start()
+
+        @pl.when(p >= LAG_SPREAD + LAG_ACROSS)
         def _():
-            across_copy(p - 2).wait_recv()
-            core_copy(p - 2, 1).start()
+            c = p - LAG_SPREAD - LAG_ACROSS
+            across_copy(c).wait_recv()
+            core_copy(c, 1).start()
 
         return carry
 
-    lax.fori_loop(0, z.own + 2, phase, 0)
+    lax.fori_loop(0, z.own + LAG_SPREAD + LAG_ACROSS, phase, 0)
 
     def drain(c, carry):
         for d in range(1, z.bands):
@@ -450,31 +504,48 @@
 
     lax.fori_loop(0, z.own, drain, 0)
 
-
-def transform_forward(z, control, scale, root, legendre):
-    whole_in = pl.BlockSpec(memory_space=pltpu.VMEM)
+    def drain_packet(e, carry):
+        packet_copy(e).wait()
+        return carry
+
+    lax.fori_loop(1, devices, drain_packet, 0)
+    packet_own.wait()
+
+
+def transform_forward(z, control, scale, root, legendre, observed):
+    in_vmem = pl.BlockSpec(memory_space=pltpu.VMEM)
     anywhere = pl.BlockSpec(memory_space=pl.ANY)
     dma = pltpu.SemaphoreType.DMA
+    devices = z.wave_count * z.bands
+    groups = z.waves // GROUP_ROWS
+    block = (groups, z.modes, GROUP_ROWS, z.width)
     return pl.pallas_call(
         lambda *refs: first_kernel(z, *refs),
-        in_specs=[whole_in, whole_in, whole_in, anywhere],
-        out_specs=anywhere,
-        out_shape=jax.ShapeDtypeStruct((z.wave_count, z.group, z.own, z.rows, LANES), f32),
+        in_specs=[anywhere, anywhere, in_vmem, anywhere] + [in_vmem] * 6,
+        out_specs=[anywhere, anywhere],
+        out_shape=[
+            jax.ShapeDtypeStruct((z.wave_count, z.own, z.group, z.rows, LANES), f32),
+            jax.ShapeDtypeStruct((devices * GROUP_ROWS, LANES), f32),
+        ],
         scratch_shapes=[
-            pltpu.VMEM((z.modes * z.waves, LANES), f32),
-            pltpu.VMEM((z.modes * z.waves, LANES), f32),
-            pltpu.VMEM((z.waves, z.in_rows, LANES), f32),
+            pltpu.VMEM(block, f32),
+            pltpu.VMEM(block, f32),
+            pltpu.VMEM((z.modes * GROUP_ROWS, LANES), f32),
+            pltpu.VMEM((z.modes * GROUP_ROWS, LANES), f32),
+            pltpu.VMEM((z.own, z.group, z.in_rows, LANES), f32),
             pltpu.VMEM((z.bands, z.own, z.in_rows, LANES), f32),
             pltpu.VMEM((z.own, z.half_lats, z.modes * z.bands), f32),
             pltpu.VMEM((z.half_lats, LANES), f32),
             pltpu.VMEM((z.half_lats, LANES), f32),
             pltpu.VMEM((z.own, z.group, z.rows, LANES), f32),
-            dma(()), dma((z.own, z.bands)), dma((z.own, z.bands)), dma((z.own, z.group)), dma((z.own, z.group)),
+            pltpu.VMEM((devices * GROUP_ROWS, LANES), f32),
+            dma(()), dma((groups, 2)), dma((devices,)), dma((devices,)),
+            dma((z.own, z.bands)), dma((z.own, z.bands)), dma((z.own, z.group)), dma((z.own, z.group)),
             dma((z.own,)), dma((z.own,)), dma((z.own, 2)), dma((z.own, 2)),
         ],
         compiler_params=pltpu.CompilerParams(collective_id=0, has_side_effects=True, vmem_limit_bytes=VMEM_LIMIT),
         name="transform_forward",
-    )(control, scale, root, legendre)
+    )(control, scale, root, legendre.reshape(z.own, z.group, *legendre.shape[1:]), *observed)
 
 
 def synthesis_kernel(z, bins, slabs_ref, cos_ref, sin_ref, courant_ref, proj_ref, out_ref, model_ref, c_hi, c_lo, n_hi, n_lo):
@@ -592,7 +663,7 @@
         compiler_params=pltpu.CompilerParams(vmem_limit_bytes=VMEM_LIMIT),
         name="settle_analysis",
     )(resid.reshape(2, z.pairs, rows, lons), courant.reshape(2, z.pairs, channels, lons), proj_t, cosine, sine)
-    return out.reshape(z.wave_count, z.group, z.own, z.rows, LANES)
+    return out.reshape(z.wave_count, z.own, z.group, z.rows, LANES)
 
 
 def second_kernel(z, part_ref, leg_ref, out_ref, part, r1, r2, v3, leg, z_all, send_u,
@@ -602,16 +673,16 @@
     half = LANES // 2
     quarter = LANES // 4
     leg_copy = pltpu.make_async_copy(
-        leg_ref.at[pl.ds(at_me.spot * z.own, z.own), pl.ds(at_me.half * z.half_lats, z.half_lats)], leg, leg_sem)
+        leg_ref.at[:, at_me.spot, pl.ds(at_me.half * z.half_lats, z.half_lats)], leg, leg_sem)
     barrier = at_me.greet()
 
     def local_copy(c, which):
         block = w if which == 0 else at_me.across
-        return pltpu.make_async_copy(part_ref.at[block, :, c], part.at[c, which], q_sem.at[c, which])
+        return pltpu.make_async_copy(part_ref.at[block, c], part.at[c, which], q_sem.at[c, which])
 
     def core_copy(c, which):
         block = at_me.partner if which == 0 else at_me.relay
-        return remote(part_ref.at[block, :, c], r1.at[c, which], c_send.at[c, which], c_recv.at[c, which], at_me.partner, b)
+        return remote(part_ref.at[block, c], r1.at[c, which], c_send.at[c, which], c_recv.at[c, which], at_me.partner, b)
 
     def across_copy(c):
         return remote(part.at[c, 1], r2.at[c], x_send.at[c], x_recv.at[c], at_me.across, b)
@@ -624,11 +695,11 @@
         return pltpu.make_async_copy(part.at[c, 0, at_me.spot], v3.at[at_me.spot, c], a3_send.at[c, 0])
 
     def fourth_copy(c, d):
-        return remote(send_u.at[c, at_me.peer(d)], out_ref.at[at_me.half, at_me.spot, c], a4_send.at[c, d],
+        return remote(send_u.at[c, at_me.peer(d)], out_ref.at[at_me.half, c, at_me.spot], a4_send.at[c, d],
                       a4_recv.at[c, d], w, at_me.peer(d))
 
     def fourth_own(c):
-        return pltpu.make_async_copy(send_u.at[c, b], out_ref.at[at_me.half, at_me.spot, c], a4_send.at[c, 0])
+        return pltpu.make_async_copy(send_u.at[c, b], out_ref.at[at_me.half, c, at_me.spot], a4_send.at[c, 0])
 
     def transform(c):
         for s in range(z.group):
@@ -668,9 +739,9 @@
             part[p, 1] = part[p, 1] + r1[p, 1]
             across_copy(p).start()
 
-        @pl.when((p >= 1) & (p <= z.own))
+        @pl.when((p >= LAG_ACROSS) & (p < z.own + LAG_ACROSS))
         def _():
-            c = p - 1
+            c = p - LAG_ACROSS
             local_copy(c, 0).wait()
             core_copy(c, 0).wait_recv()
             part[c, 0] = part[c, 0] + r1[c, 0]
@@ -680,13 +751,13 @@
                 third_copy(c, e).start()
             third_own(c).start()
 
-        @pl.when(p == 2)
+        @pl.when(p == LAG_ACROSS + LAG_SPREAD)
         def _():
             leg_copy.wait()
 
-        @pl.when(p >= 2)
+        @pl.when(p >= LAG_ACROSS + LAG_SPREAD)
         def _():
-            c = p - 2
+            c = p - LAG_ACROSS - LAG_SPREAD
             third_own(c).wait()
             for e in range(1, z.group):
                 third_copy(c, e).wait_recv()
@@ -697,7 +768,7 @@
 
         return carry
 
-    lax.fori_loop(0, z.own + 2, phase, 0)
+    lax.fori_loop(0, z.own + LAG_ACROSS + LAG_SPREAD, phase, 0)
 
     def drain(c, carry):
         across_copy(c).wait_send()
@@ -721,7 +792,7 @@
         lambda *refs: second_kernel(z, *refs),
         in_specs=[anywhere, anywhere],
         out_specs=anywhere,
-        out_shape=jax.ShapeDtypeStruct((2, z.group, z.own, z.in_rows, LANES), f32),
+        out_shape=jax.ShapeDtypeStruct((2, z.own, z.group, z.in_rows, LANES), f32),
         scratch_shapes=[
             pltpu.VMEM((z.own, 2, z.group) + slab, f32),
             pltpu.VMEM((z.own, 2, z.group) + slab, f32),
@@ -735,103 +806,111 @@
         ],
         compiler_params=pltpu.CompilerParams(collective_id=1, has_side_effects=True, vmem_limit_bytes=VMEM_LIMIT),
         name="transform_backward",
-    )(part, legendre)
-
-
-def last_kernel(z, slabs_ref, control_ref, scale_ref, root_ref, out_ref, s_a, s_b):
+    )(part, legendre.reshape(z.own, z.group, *legendre.shape[1:]))
+
+
+def last_kernel(z, slabs_ref, control_ref, scale_ref, root_ref, out_ref, s_a, s_b, r_hi, r_lo):
     half = LANES // 2
     quarter = LANES // 4
 
-    def unpack(m, carry):
+    @pl.when(pl.program_id(0) == 0)
+    def _():
+        r_hi[...], r_lo[...] = split2(interleaved(root_ref[...]))
+
+    for m in range(GROUP_ROWS):
         slab = slabs_ref[0, m] + slabs_ref[1, m]
         tail = slab[z.modes :]
         keep = lane_of(tail.shape) % half < quarter
         both = jnp.concatenate(
             [jnp.where(keep, tail, 0.0), jnp.where(keep, pltpu.roll(tail, LANES - quarter, 1), 0.0)], 0)
-        s_a[pl.ds(m, z.modes, stride=z.waves), :] = slab[: z.modes]
-        s_b[pl.ds(m, z.modes, stride=z.waves), :] = both
-        return carry
-
-    lax.fori_loop(0, z.waves, unpack, 0)
-    root = split2(interleaved(root_ref[...]))
+        s_a[pl.ds(m, z.modes, stride=GROUP_ROWS), :] = slab[: z.modes]
+        s_b[pl.ds(m, z.modes, stride=GROUP_ROWS), :] = both
     order = packed_order(z.width // 2, True)
-    group = 8
-
-    def vertical(i, carry):
-        at = pl.ds(pl.multiple_of(i * group * z.waves, 8), group * z.waves)
-        placed = jnp.concatenate([s_a[at, :], s_b[at, :]], 1)
-        scale = scale_ref[pl.ds(i * group, group)].reshape(group * z.waves, z.width)
-        mixed = product(split2(scale * select_product(placed, order)), root, ((1,), (1,)))
-        out_ref[pl.ds(i * group, group)] = control_ref[pl.ds(i * group, group)] + mixed.reshape(
-            group, z.waves, z.width)
-        return carry
-
-    lax.fori_loop(0, z.modes // group, vertical, 0)
+    placed = jnp.concatenate([s_a[...], s_b[...]], 1)
+    scale = scale_ref[...].reshape(z.modes * GROUP_ROWS, z.width)
+    mixed = product(split2(scale * select_product(placed, order)), (r_hi[...], r_lo[...]), ((1,), (1,)))
+    out_ref[...] = control_ref[...] + mixed.reshape(z.modes, GROUP_ROWS, z.width)
 
 
 def finish(z, slabs, control, scale, root):
-    whole_in = pl.BlockSpec(memory_space=pltpu.VMEM)
+    by_waves = pl.BlockSpec((z.modes, GROUP_ROWS, z.width), lambda i: (0, i, 0))
     return pl.pallas_call(
         lambda *refs: last_kernel(z, *refs),
-        in_specs=[whole_in] * 4,
-        out_specs=whole_in,
+        grid=(z.waves // GROUP_ROWS,),
+        in_specs=[
+            pl.BlockSpec((2, GROUP_ROWS, z.in_rows, LANES), lambda i: (0, i, 0, 0)),
+            by_waves, by_waves, whole(*root.shape),
+        ],
+        out_specs=by_waves,
         out_shape=jax.ShapeDtypeStruct(control.shape, f32),
-        scratch_shapes=[pltpu.VMEM((z.modes * z.waves, LANES), f32)] * 2,
+        scratch_shapes=[pltpu.VMEM((z.modes * GROUP_ROWS, LANES), f32)] * 2 + [pltpu.VMEM((z.width, z.width), bf16)] * 2,
         compiler_params=pltpu.CompilerParams(vmem_limit_bytes=VMEM_LIMIT),
         name="finish",
     )(slabs.reshape(2, z.waves, z.in_rows, LANES), control, scale, root)
 
 
-def observation_sums(z, tracer_shape, model, arrived, lidar_coef, levels_here, proj_rows):
-    lat_here, lon_here = tracer_shape
-    columns, levels, lidar_vals, aod_vals, weights = [arrived[:, i].reshape(-1) for i in range(5)]
-    columns = columns.astype(jnp.int32)
-    levels = levels.astype(jnp.int32)
-    lat_index = columns // lon_here
-    lon_hot = (columns % lon_here)[:, None] == jnp.arange(lon_here, dtype=jnp.int32)[None, :]
-    lat_hot = (lat_index[:, None] == jnp.arange(lat_here, dtype=jnp.int32)[None, :]).astype(jnp.float32)
-    cell = lat_index * levels_here + levels
-    cell_hot = (
-        cell[:, None] == jnp.arange(lat_here * levels_here, dtype=jnp.int32)[None, :]
-    ).astype(jnp.float32)
-    lidar_field = model[:, :levels_here].reshape(lat_here * levels_here, lon_here)
-    aod_field = model[:, levels_here]
-    lidar_rows = jnp.dot(cell_hot, lidar_field, precision=highest)
-    aod_rows = jnp.dot(lat_hot, aod_field, precision=highest)
-    lidar_model = jnp.sum(jnp.where(lon_hot, lidar_rows, 0.0), axis=1)
-    aod_model = jnp.sum(jnp.where(lon_hot, aod_rows, 0.0), axis=1)
-    lidar_resid = weights * (lidar_model - lidar_vals)
-    aod_resid = weights * (aod_model - aod_vals)
-    lidar_sum = lax.dot_general(
-        cell_hot, jnp.where(lon_hot, lidar_resid[:, None], 0.0), (((0,), (0,)), ((), ())), precision=highest
-    )
-    aod_sum = lax.dot_general(
-        lat_hot, jnp.where(lon_hot, aod_resid[:, None], 0.0), (((0,), (0,)), ((), ())), precision=highest
-    )
-    return jnp.concatenate(
-        [
-            lidar_sum.reshape(lat_here, levels_here, lon_here),
-            aod_sum[:, None, :],
-            jnp.zeros((lat_here, proj_rows - levels_here - 1, lon_here), jnp.float32),
-        ],
-        axis=1,
-    )
-
-
-def observation_packet(obs_count, obs_column, obs_level, lidar_obs, aod_obs, obs_weight):
-    slot_count = obs_column.shape[1]
-    live = jnp.arange(slot_count, dtype=jnp.int32)[None, :] < obs_count.reshape(-1, 1)
-    packet = jnp.stack(
-        [
-            obs_column.astype(jnp.float32),
-            obs_level.astype(jnp.float32),
-            lidar_obs,
-            aod_obs,
-            jnp.where(live, obs_weight, 0.0),
-        ],
-        axis=1,
-    )
-    return lax.all_to_all(packet, ("wave", "band"), split_axis=0, concat_axis=0, tiled=True)
+OBS_ROWS = 4
+
+
+def observation_kernel(levels, model_ref, seen_ref, out_ref, lidar_acc, aod_acc):
+    lats, rows, lons = model_ref.shape
+    cells = lats * levels
+    devices = seen_ref.shape[0] // GROUP_ROWS
+    slots = OBS_ROWS * seen_ref.shape[1]
+
+    def halves(x):
+        return jnp.concatenate(split2(x.T), 0)
+
+    lidar_field = halves(model_ref[:, :levels, :].reshape(cells, lons))
+    aod_field = halves(jnp.sum(model_ref[:, levels:, :], axis=1))
+    lidar_acc[...] = jnp.zeros_like(lidar_acc)
+    aod_acc[...] = jnp.zeros_like(aod_acc)
+    over_slots = ((1,), (1,))
+
+    def step(i, carry):
+        def row(k):
+            first = i * OBS_ROWS * GROUP_ROWS + k
+            return jnp.concatenate([seen_ref[pl.ds(first + r * GROUP_ROWS, 1), :] for r in range(OBS_ROWS)], 1)
+
+        column = row(0).astype(jnp.int32)
+        lat = column // lons
+        lon_hot = lax.broadcasted_iota(jnp.int32, (lons, slots), 0) == column - lat * lons
+        cell = lat * levels + row(1).astype(jnp.int32)
+        cell_hot = jnp.where(lax.broadcasted_iota(jnp.int32, (cells, slots), 0) == cell, 1.0, 0.0).astype(bf16)
+        lat_hot = jnp.where(lax.broadcasted_iota(jnp.int32, (lats, slots), 0) == lat, 1.0, 0.0).astype(bf16)
+        weight = row(4)
+
+        def one(field, hot, observed, acc):
+            picked = jnp.dot(field, hot, preferred_element_type=f32)
+            picked = picked[:lons] + picked[lons:]
+            resid = weight * (jnp.sum(jnp.where(lon_hot, picked, 0.0), axis=0, keepdims=True) - observed)
+            hi, lo = (jnp.where(lon_hot, part.astype(f32), 0.0).astype(bf16) for part in split2(resid))
+            acc[...] += lax.dot_general(hot, hi, (over_slots, ((), ())), preferred_element_type=f32) + lax.dot_general(
+                hot, lo, (over_slots, ((), ())), preferred_element_type=f32)
+
+        one(lidar_field, cell_hot, row(2), lidar_acc)
+        one(aod_field, lat_hot, row(3), aod_acc)
+        return carry
+
+    lax.fori_loop(0, devices // OBS_ROWS, step, 0)
+    out_ref[:, :levels, :] = lidar_acc[...].reshape(lats, levels, lons)
+    spread = jnp.broadcast_to(aod_acc[...][:, None, :], (lats, rows - levels, lons))
+    first = lax.broadcasted_iota(jnp.int32, spread.shape, 1) == 0
+    out_ref[:, levels:, :] = jnp.where(first, spread, 0.0)
+
+
+def observation_sums(model, seen, levels):
+    in_vmem = pl.BlockSpec(memory_space=pltpu.VMEM)
+    lats, rows, lons = model.shape
+    return pl.pallas_call(
+        lambda *refs: observation_kernel(levels, *refs),
+        in_specs=[in_vmem, in_vmem],
+        out_specs=in_vmem,
+        out_shape=jax.ShapeDtypeStruct(model.shape, f32),
+        scratch_shapes=[pltpu.VMEM((lats * levels, lons), f32), pltpu.VMEM((lats, lons), f32)],
+        compiler_params=pltpu.CompilerParams(vmem_limit_bytes=VMEM_LIMIT),
+        name="observation_sums",
+    )(model, seen)
 
 
 def projection(lidar_coef, aod_coef):
@@ -875,18 +954,18 @@
     factor = zonal_number.shape[0] ** (-0.5)
     bins = lidar_coef.shape[0]
     levels_here = channels // bins
-    arrived = observation_packet(obs_count, obs_column, obs_level, lidar_obs, aod_obs, obs_weight)
     cosine, sine = trig_tables(zonal_number, lon_first, lon_here, lon_here * wave_count, factor)
     proj = projection(lidar_coef, aod_coef)
-    slabs = transform_forward(z, control, spectral_scale, vertical_root, legendre)
+    observed = (obs_count, obs_column, obs_level, lidar_obs, aod_obs, obs_weight)
+    slabs, seen = transform_forward(z, control, spectral_scale, vertical_root, legendre, observed)
     tracer, model = synthesis_settle(z, slabs, cosine, sine, courant, proj, bins)
-    resid = observation_sums(z, (lats_here, lon_here), model, arrived, lidar_coef, levels_here, proj.shape[0])
+    resid = observation_sums(model, seen, levels_here)
     part = settle_analysis(z, resid, courant, proj.T, cosine, sine, bins)
     back = transform_backward(z, part, legendre)
     return finish(z, back, control, spectral_scale, vertical_root), tracer
 
 
-def fits(mesh, control, courant):
+def fits(mesh, control, courant, columns, bins):
     bands, waves = mesh.shape["band"], mesh.shape["wave"]
     modes_here, waves_here = control[0] // bands, control[1] // waves
     lats_here, channels = courant[0] // bands, courant[1]
@@ -900,6 +979,10 @@
         and LANES // 2 < channels <= LANES * 3 // 4
         and (channels - LANES // 2) % 8 == 0
         and courant[2] // waves % LANES == 0
+        and GROUP_ROWS % (bands // 2) == 0
+        and columns[1] == LANES
+        and channels // bins == GROUP_ROWS
+        and bands * waves % OBS_ROWS == 0
     )
 
 
@@ -923,7 +1006,7 @@
 
 def solution(mesh):
     def program(*args):
-        chosen = fast_body if fits(mesh, args[0].shape, args[5].shape) else body
+        chosen = fast_body if fits(mesh, args[0].shape, args[5].shape, args[9].shape, args[6].shape[0]) else body
         return jax.shard_map(
             chosen,
             mesh=mesh,

time: 297 us -> 283 us (0.953)
  matrix products: 17.4 us -> 0 us
  Pallas kernels: 259 us -> 276 us
  starting transfers between devices: 7.33 us -> 0 us
    dot_general x4 -> x0, matrix products: 17.4 us -> none  [the longest x1 6.84 us: observation_sums(): lidar_rows = jnp.dot(cell_hot, lidar_field, precision=highest)]
    pallas_call x2 -> x3, Pallas kernels: 110 us -> 124 us  [the longest x1 99.2 us: transform_forward(): pl.pallas_call(lambda *refs: first_kernel(z, *refs), in_specs=[anywhere,...]
    all_to_all x1 -> x0, starting transfers between devices: 7.33 us -> none  [observation_packet(): lax.all_to_all(packet, ('wave', 'band'), split_axis=0, concat_axis=0, til...]
  transfers between devices with their start and end apart: 1 -> 0, of which waited for: 0 -> 0; matrix products, arithmetic and copies ran while one was open for 2% -> 0% of each run, Pallas kernels for 43% -> 0%
where the time goes in v3:
time: 283 us; the launch traced here: 281 us
  Pallas kernels  276 us (98%)
  other arithmetic  3.24 us (1%)
    pallas_call x1, Pallas kernels, transform_forward(): pl.pallas_call(lambda *refs: first_kernel(z, *refs), in_specs=[anywhere,...  99.2 us
    pallas_call x1, Pallas kernels, transform_backward(): pl.pallas_call(lambda *refs: second_kernel(z, *refs), in_specs=[anywhere,...  92.2 us
    pallas_call x1, Pallas kernels, settle_analysis(): pl.pallas_call(lambda *refs: analysis_kernel(z, bins, *refs), grid=(z.pai...  30.3 us
    pallas_call x1, Pallas kernels, synthesis_settle(): pl.pallas_call(lambda *refs: synthesis_kernel(z, bins, *refs), grid=(z.pa...  29.8 us
    pallas_call x1, Pallas kernels, observation_sums(): pl.pallas_call(lambda *refs: observation_kernel(levels, *refs), in_specs=...  15.6 us
    pallas_call x1, Pallas kernels, finish(): pl.pallas_call(lambda *refs: last_kernel(z, *refs), grid=(z.waves // GROU...  8.72 us

profile of v3, /device:TPU:0, one launch (start us, length us, event | category | flops | bytes accessed | tf_op | source)
XLA Modules:
  0.0 281.4 jit_solution(822452497062138387)
XLA Ops:
  0.7 0.1 pad.2.clone
  0.7 0.7 tile.2
  1.4 0.1 broadcast_in_dim.24
  1.5 0.7 maximum_maximum_fusion.refs_4_
  2.2 0.0 copy-start
  2.2 0.7 copy.18
  2.9 2.5 sine_multiply_fusion
  5.4 99.2 %transform_forward.1 = (f32[4,14,4,88,128]{4,3,2,1,0:T(8,128)}, f32[256,128]{1,0:T(8,128)}) custom-call(f32[32,56,192]{2,1,0:T(8,128)} %refs_1_.3, f32[32,56,192]{2,1,0:T(8,128)} %refs_2_.3, f32[96,96]{1,0:T(8,128)} %refs_3_.1, f32[14,4,448,256]{3,2,1,0:T(8,128)} %bitcast.10, s32[1,32]{1,0:T(1,128)} %refs_4_.1, s32[32,128]{1,0:T(8,128)} %refs_5_.1, ...), custom_call_target="tpu_custom_call" | custom-call | tf_op jit(solution)/shard_map/transform_forward/pallas_call | solution.py:522
  104.6 0.0 copy-done
  104.6 29.8 %synthesis_settle.1 = (f32[2,28,96,256]{3,2,1,0:T(8,128)}, f32[2,28,16,256]{3,2,1,0:T(8,128)}) custom-call(f32[19712,128]{1,0:T(8,128)} %bitcast.16, f32[224,256]{1,0:T(8,128)} %get-tuple-element.11.refs_1_.refs_3_, f32[224,256]{1,0:T(8,128)} %get-tuple-element.10.refs_2_.refs_4_, f32[2,28,96,256]{3,2,1,0:T(8,128)} %bitcast.13, f32[16,96]{1,0:T(8,128)} %copy-done), custom_call_target="tpu_custom_call" | custom-call | tf_op jit(solution)/shard_map/synthesis_settle/pallas_call | solution.py:593
  134.5 15.6 %observation_sums.1 = f32[56,16,256]{2,1,0:T(8,128)} custom-call(f32[56,16,256]{2,1,0:T(8,128)} %bitcast.18, f32[256,128]{1,0:T(8,128)} %get-tuple-element.8.refs_1_), custom_call_target="tpu_custom_call" | custom-call | tf_op jit(solution)/shard_map/observation_sums/pallas_call | solution.py:905
  150.1 30.3 %settle_analysis.1 = f32[19712,128]{1,0:T(8,128)} custom-call(f32[2,28,16,256]{3,2,1,0:T(8,128)} %bitcast.17, f32[2,28,96,256]{3,2,1,0:T(8,128)} %bitcast.14, f32[96,16]{1,0:T(8,128)} %bitcast.19, f32[224,256]{1,0:T(8,128)} %get-tuple-element.11.refs_1_.refs_3_, f32[224,256]{1,0:T(8,128)} %get-tuple-element.10.refs_2_.refs_4_), custom_call_target="tpu_custom_call" | custom-call | tf_op jit(solution)/shard_map/settle_analysis/pallas_call | solution.py:655
  180.4 92.2 %transform_backward.1 = f32[2,14,4,48,128]{4,3,2,1,0:T(8,128)} custom-call(f32[4,14,4,88,128]{4,3,2,1,0:T(8,128)} %bitcast.12, f32[14,4,448,256]{3,2,1,0:T(8,128)} %bitcast.11), custom_call_target="tpu_custom_call" | custom-call | tf_op jit(solution)/shard_map/transform_backward/pallas_call | solution.py:791
  272.6 8.7 %finish.1 = f32[32,56,192]{2,1,0:T(8,128)} custom-call(f32[2,56,48,128]{3,2,1,0:T(8,128)} %bitcast.15, f32[32,56,192]{2,1,0:T(8,128)} %refs_1_.3, f32[32,56,192]{2,1,0:T(8,128)} %refs_2_.3, f32[96,96]{1,0:T(8,128)} %refs_3_.1), custom_call_target="tpu_custom_call" | custom-call | tf_op jit(solution)/shard_map/finish/pallas_call | solution.py:837
  (4 shorter events, 0.0 us)
Async XLA Ops:
  2.2 102.4 %copy-start = (f32[16,96]{1,0:T(8,128)}, f32[16,96]{1,0:T(8,128)S(1)}, u32[]{:S(2)}) copy-start(f32[16,96]{1,0:T(8,128)S(1)} %maximum_maximum_fusion.refs_4_) | copy-start | bytes 18436

commit v4 on v3

--- a/solution.py
+++ b/solution.py
@@ -283,6 +283,7 @@
         self.rows = -(-(3 * self.pairs) // 8) * 8
         self.in_rows = modes + modes // 2
         self.slots = waves * wave_count
+        self.unroll = max(u for u in range(1, UNROLL + 1) if self.pairs % u == 0)
 
 
 class Place:
@@ -320,10 +321,11 @@
 LAG_SPREAD = 2
 LAG_ACROSS = 2
 GROUP_ROWS = 8
+UNROLL = 4
 
 
 def first_kernel(z, control_ref, scale_ref, root_ref, leg_ref, count_ref, column_ref, level_ref, lidar_ref, aod_ref,
-                 weight_ref, out_ref, seen_ref, control, scale, s_a, s_b, send_u, recv_v, leg, y_a, y_b, send_y, packet,
+                 weight_ref, number_ref, out_ref, seen_ref, cos_ref, sin_ref, control, scale, s_a, s_b, send_u, recv_v, leg, y_a, y_b, send_y, packet,
                  leg_sem, in_sem, o_send, o_recv, a1_send, a1_recv, a2_send, a2_recv, x_send, x_recv, c_send, c_recv):
     at_me = Place(z)
     w, b = at_me.w, at_me.b
@@ -456,6 +458,13 @@
 
     lax.fori_loop(1, devices, send_packet, 0)
     packet_own.start()
+    lons = cos_ref.shape[1]
+    lon_total = lons * z.wave_count
+    longitude = lax.broadcasted_iota(jnp.int32, cos_ref.shape, 1) + w * lons
+    angle = (number_ref[...] * longitude % lon_total).astype(f32) * (2.0 * math.pi / lon_total)
+    factor = z.slots ** (-0.5)
+    cos_ref[...] = jnp.cos(angle) * factor
+    sin_ref[...] = jnp.sin(angle) * factor
     leg_copy.wait()
 
     def phase(p, carry):
@@ -512,7 +521,7 @@
     packet_own.wait()
 
 
-def transform_forward(z, control, scale, root, legendre, observed):
+def transform_forward(z, control, scale, root, legendre, numbers, lons, observed):
     in_vmem = pl.BlockSpec(memory_space=pltpu.VMEM)
     anywhere = pl.BlockSpec(memory_space=pl.ANY)
     dma = pltpu.SemaphoreType.DMA
@@ -521,11 +530,13 @@
     block = (groups, z.modes, GROUP_ROWS, z.width)
     return pl.pallas_call(
         lambda *refs: first_kernel(z, *refs),
-        in_specs=[anywhere, anywhere, in_vmem, anywhere] + [in_vmem] * 6,
-        out_specs=[anywhere, anywhere],
+        in_specs=[anywhere, anywhere, in_vmem, anywhere] + [in_vmem] * 7,
+        out_specs=[anywhere, anywhere, in_vmem, in_vmem],
         out_shape=[
             jax.ShapeDtypeStruct((z.wave_count, z.own, z.group, z.rows, LANES), f32),
             jax.ShapeDtypeStruct((devices * GROUP_ROWS, LANES), f32),
+            jax.ShapeDtypeStruct((z.slots, lons), f32),
+            jax.ShapeDtypeStruct((z.slots, lons), f32),
         ],
         scratch_shapes=[
             pltpu.VMEM(block, f32),
@@ -545,154 +556,213 @@
         ],
         compiler_params=pltpu.CompilerParams(collective_id=0, has_side_effects=True, vmem_limit_bytes=VMEM_LIMIT),
         name="transform_forward",
-    )(control, scale, root, legendre.reshape(z.own, z.group, *legendre.shape[1:]), *observed)
-
-
-def synthesis_kernel(z, bins, slabs_ref, cos_ref, sin_ref, courant_ref, proj_ref, out_ref, model_ref, c_hi, c_lo, n_hi, n_lo):
-    i = pl.program_id(0)
+    )(control, scale, root, legendre.reshape(z.own, z.group, *legendre.shape[1:]), *observed,
+      numbers.reshape(-1, 1))
+
+
+def synthesis_kernel(z, bins, slabs_ref, cos_ref, sin_ref, courant_ref, lidar_ref, aod_ref, out_ref, model_ref,
+                     c_hi, c_lo, n_hi, n_lo, p_hi, p_lo):
     half = LANES // 2
 
-    @pl.when(i == 0)
+    @pl.when(pl.program_id(0) == 0)
     def _():
         c_hi[...], c_lo[...] = split2(cos_ref[...])
         n_hi[...], n_lo[...] = split2(-sin_ref[...])
+        p_hi[...], p_lo[...] = split2(
+            projection(lidar_ref[...], aod_ref[...], bins, aod_ref.shape[1] // bins, model_ref.shape[2]))
 
     def slab(row):
         return slabs_ref[pl.ds(row, z.slots, stride=z.rows), :]
 
-    tail = slab(2 * z.pairs + i)
-    real = jnp.concatenate([slab(i), tail], 1)
-    imag = jnp.concatenate([slab(z.pairs + i), pltpu.roll(tail, half, 1)], 1)
     over_waves = ((0,), (0,))
-    field = product(split2(real), (c_hi[...], c_lo[...]), over_waves) + product(
-        split2(imag), (n_hi[...], n_lo[...]), over_waves)
-    channels = z.width // 2
-    rest = channels - half
-    proj = split2(proj_ref[...])
-    for which in range(2):
-        tracer = jnp.concatenate(
-            [field[which * half : (which + 1) * half],
-             field[LANES + which * (half // 2) : LANES + which * (half // 2) + rest]], 0)
-        courant = courant_ref[which, 0]
-        row = lax.broadcasted_iota(jnp.int32, tracer.shape, 0)
-        for repeat in range(STEPS):
-            outflow = courant * tracer
-            inflow = jnp.where(row >= bins, pltpu.roll(outflow, bins, 0), 0.0)
-            tracer = tracer - outflow + inflow
-        out_ref[which, 0] = tracer
-        model_ref[which, 0] = product(proj, split2(tracer))
-
-
-def paired(rows, cols):
-    return pl.BlockSpec((2, 1, rows, cols), lambda i: (0, i, 0, 0))
-
-
-def synthesis_settle(z, slabs, cosine, sine, courant, proj, bins):
+    rest = z.width // 2 - half
+    for u in range(z.unroll):
+        i = pl.program_id(0) * z.unroll + u
+        tail = slab(2 * z.pairs + i)
+        real = jnp.concatenate([slab(i), tail], 1)
+        imag = jnp.concatenate([slab(z.pairs + i), pltpu.roll(tail, half, 1)], 1)
+        field = product(split2(real), (c_hi[...], c_lo[...]), over_waves) + product(
+            split2(imag), (n_hi[...], n_lo[...]), over_waves)
+        for which in range(2):
+            tracer = jnp.concatenate(
+                [field[which * half : (which + 1) * half],
+                 field[LANES + which * (half // 2) : LANES + which * (half // 2) + rest]], 0)
+            courant = courant_ref[which, u]
+            row = lax.broadcasted_iota(jnp.int32, tracer.shape, 0)
+            for repeat in range(STEPS):
+                outflow = courant * tracer
+                inflow = jnp.where(row >= bins, pltpu.roll(outflow, bins, 0), 0.0)
+                tracer = tracer - outflow + inflow
+            out_ref[which, u] = tracer
+            model_ref[which, u] = product((p_hi[...], p_lo[...]), split2(tracer))
+
+
+def paired(z, rows, cols):
+    return pl.BlockSpec((2, z.unroll, rows, cols), lambda i: (0, i, 0, 0))
+
+
+def synthesis_settle(z, slabs, cosine, sine, courant, lidar, aod):
     lats, channels, lons = courant.shape
-    rows = proj.shape[0]
+    bins = lidar.shape[1]
+    rows = -(-(channels // bins + 1) // 8) * 8
     tracer, model = pl.pallas_call(
         lambda *refs: synthesis_kernel(z, bins, *refs),
-        grid=(z.pairs,),
-        in_specs=[whole(z.slots * z.rows, LANES), whole(z.slots, lons), whole(z.slots, lons), paired(channels, lons),
-                  whole(rows, channels)],
-        out_specs=[paired(channels, lons), paired(rows, lons)],
+        grid=(z.pairs // z.unroll,),
+        in_specs=[whole(z.slots * z.rows, LANES), whole(z.slots, lons), whole(z.slots, lons), paired(z, channels, lons),
+                  whole(1, bins), whole(1, channels)],
+        out_specs=[paired(z, channels, lons), paired(z, rows, lons)],
         out_shape=[
             jax.ShapeDtypeStruct((2, z.pairs, channels, lons), f32),
             jax.ShapeDtypeStruct((2, z.pairs, rows, lons), f32),
         ],
-        scratch_shapes=[pltpu.VMEM((z.slots, lons), bf16)] * 4,
+        scratch_shapes=[pltpu.VMEM((z.slots, lons), bf16)] * 4 + [pltpu.VMEM((rows, channels), bf16)] * 2,
         compiler_params=pltpu.CompilerParams(vmem_limit_bytes=VMEM_LIMIT),
         name="synthesis_settle",
-    )(slabs.reshape(z.slots * z.rows, LANES), cosine, sine, courant.reshape(2, z.pairs, channels, lons), proj)
+    )(slabs.reshape(z.slots * z.rows, LANES), cosine, sine, courant.reshape(2, z.pairs, channels, lons), lidar, aod)
     return tracer.reshape(lats, channels, lons), model.reshape(lats, rows, lons)
 
 
-def analysis_kernel(z, bins, resid_ref, courant_ref, proj_ref, cos_ref, sin_ref, out_ref, c_hi, c_lo, n_hi, n_lo):
-    i = pl.program_id(0)
-    half = LANES // 2
-
-    @pl.when(i == 0)
-    def _():
-        c_hi[...], c_lo[...] = split2(cos_ref[...])
-        n_hi[...], n_lo[...] = split2(-sin_ref[...])
-
-    proj = split2(proj_ref[...])
-    fields = []
-    for which in range(2):
-        courant = courant_ref[which, 0]
-        adjoint = product(proj, split2(resid_ref[which, 0]))
-        channels = adjoint.shape[0]
-        row = lax.broadcasted_iota(jnp.int32, adjoint.shape, 0)
-        for repeat in range(STEPS):
-            below = jnp.where(row < channels - bins, pltpu.roll(adjoint, channels - bins, 0), 0.0)
-            adjoint = adjoint + courant * (below - adjoint)
-        fields.append(adjoint)
-    gap = jnp.zeros((half // 2 - (channels - half), fields[0].shape[1]), f32)
-    pieces = [field[:half] for field in fields]
-    for field in fields:
-        pieces.append(field[half:])
-        if gap.shape[0]:
-            pieces.append(gap)
-    pieces.append(jnp.zeros((half, fields[0].shape[1]), f32))
-    both = split2(jnp.concatenate(pieces, 0))
-    over_lons = ((1,), (1,))
-    real = product((c_hi[...], c_lo[...]), both, over_lons)
-    imag = product((n_hi[...], n_lo[...]), both, over_lons)
-
-    @pl.when(i == 0)
-    def _():
-        for spare in range(3 * z.pairs, z.rows):
-            out_ref[pl.ds(spare, z.slots, stride=z.rows), :] = jnp.zeros((z.slots, LANES), f32)
-
-    out_ref[pl.ds(i, z.slots, stride=z.rows), :] = real[:, :LANES]
-    out_ref[pl.ds(z.pairs + i, z.slots, stride=z.rows), :] = imag[:, :LANES]
-    out_ref[pl.ds(2 * z.pairs + i, z.slots, stride=z.rows), :] = real[:, LANES:] + pltpu.roll(imag[:, LANES:], half, 1)
-
-
-def settle_analysis(z, resid, courant, proj_t, cosine, sine, bins):
-    lats, channels, lons = courant.shape
-    rows = proj_t.shape[1]
-    out = pl.pallas_call(
-        lambda *refs: analysis_kernel(z, bins, *refs),
-        grid=(z.pairs,),
-        in_specs=[paired(rows, lons), paired(channels, lons), whole(channels, rows), whole(z.slots, lons),
-                  whole(z.slots, lons)],
-        out_specs=whole(z.slots * z.rows, LANES),
-        out_shape=jax.ShapeDtypeStruct((z.slots * z.rows, LANES), f32),
-        scratch_shapes=[pltpu.VMEM((z.slots, lons), bf16)] * 4,
-        compiler_params=pltpu.CompilerParams(vmem_limit_bytes=VMEM_LIMIT),
-        name="settle_analysis",
-    )(resid.reshape(2, z.pairs, rows, lons), courant.reshape(2, z.pairs, channels, lons), proj_t, cosine, sine)
-    return out.reshape(z.wave_count, z.own, z.group, z.rows, LANES)
-
-
-def second_kernel(z, part_ref, leg_ref, out_ref, part, r1, r2, v3, leg, z_all, send_u,
-                  leg_sem, q_sem, c_send, c_recv, x_send, x_recv, a3_send, a3_recv, a4_send, a4_recv):
+OBS_ROWS = 4
+
+
+def projection(lidar, aod, bins, levels, rows):
+    channels = aod.shape[1]
+    repeat = (lax.broadcasted_iota(jnp.int32, (bins, channels), 1) % bins
+              == lax.broadcasted_iota(jnp.int32, (bins, channels), 0))
+    repeat = jnp.where(repeat, 1.0, 0.0).astype(bf16)
+    tiled = select_product(jnp.broadcast_to(lidar, (8, bins)), repeat)[:1]
+    row = lax.broadcasted_iota(jnp.int32, (rows, channels), 0)
+    level = lax.broadcasted_iota(jnp.int32, (rows, channels), 1) // bins
+    return jnp.where((row < levels) & (level == row), tiled, jnp.where(row == levels, aod, 0.0))
+
+
+def observe(z, levels, model_ref, seen_ref, resid, lidar_acc, aod_acc):
+    lats, rows, lons = model_ref.shape
+    cells = lats * levels
+    devices = seen_ref.shape[0] // GROUP_ROWS
+    slots = OBS_ROWS * seen_ref.shape[1]
+
+    def halves(x):
+        return jnp.concatenate(split2(x.T), 0)
+
+    lidar_field = halves(model_ref[:, :levels, :].reshape(cells, lons))
+    aod_field = halves(jnp.sum(model_ref[:, levels:, :], axis=1))
+    lidar_acc[...] = jnp.zeros_like(lidar_acc)
+    aod_acc[...] = jnp.zeros_like(aod_acc)
+    over_slots = ((1,), (1,))
+
+    def step(i, carry):
+        def row(k):
+            first = i * OBS_ROWS * GROUP_ROWS + k
+            return jnp.concatenate([seen_ref[pl.ds(first + r * GROUP_ROWS, 1), :] for r in range(OBS_ROWS)], 1)
+
+        column = row(0).astype(jnp.int32)
+        lat = column // lons
+        lon_hot = lax.broadcasted_iota(jnp.int32, (lons, slots), 0) == column - lat * lons
+        cell = lat * levels + row(1).astype(jnp.int32)
+        cell_hot = jnp.where(lax.broadcasted_iota(jnp.int32, (cells, slots), 0) == cell, 1.0, 0.0).astype(bf16)
+        lat_hot = jnp.where(lax.broadcasted_iota(jnp.int32, (lats, slots), 0) == lat, 1.0, 0.0).astype(bf16)
+        weight = row(4)
+
+        def one(field, hot, observed, acc):
+            picked = jnp.dot(field, hot, preferred_element_type=f32)
+            picked = picked[:lons] + picked[lons:]
+            left = weight * (jnp.sum(jnp.where(lon_hot, picked, 0.0), axis=0, keepdims=True) - observed)
+            hi, lo = (jnp.where(lon_hot, part.astype(f32), 0.0).astype(bf16) for part in split2(left))
+            acc[...] += lax.dot_general(hot, hi, (over_slots, ((), ())), preferred_element_type=f32) + lax.dot_general(
+                hot, lo, (over_slots, ((), ())), preferred_element_type=f32)
+
+        one(lidar_field, cell_hot, row(2), lidar_acc)
+        one(aod_field, lat_hot, row(3), aod_acc)
+        return carry
+
+    lax.fori_loop(0, devices // OBS_ROWS, step, 0)
+    resid[:, :levels, :] = lidar_acc[...].reshape(lats, levels, lons)
+    spread = jnp.broadcast_to(aod_acc[...][:, None, :], (lats, rows - levels, lons))
+    first = lax.broadcasted_iota(jnp.int32, spread.shape, 1) == 0
+    resid[:, levels:, :] = jnp.where(first, spread, 0.0)
+
+
+def second_kernel(z, bins, model_ref, seen_ref, lidar_ref, aod_ref, cos_ref, sin_ref, courant_ref, leg_ref, out_ref,
+                  resid, lidar_acc, aod_acc, courant, q, c_hi, c_lo, n_hi, n_lo, p_hi, p_lo, r1, r2, v3, leg, z_all, send_u,
+                  leg_sem, k_sem, c_send, c_recv, x_send, x_recv, a3_send, a3_recv, a4_send, a4_recv):
     at_me = Place(z)
     w, b = at_me.w, at_me.b
     half = LANES // 2
     quarter = LANES // 4
+    channels = z.width // 2
+    levels = channels // bins
+    steps = z.pairs // z.unroll
+
+    def courant_copy(k):
+        at = pl.ds(k * z.unroll, z.unroll)
+        return pltpu.make_async_copy(courant_ref.at[:, at], courant.at[:, at], k_sem.at[k])
+
+    for k in range(steps):
+        courant_copy(k).start()
     leg_copy = pltpu.make_async_copy(
         leg_ref.at[:, at_me.spot, pl.ds(at_me.half * z.half_lats, z.half_lats)], leg, leg_sem)
+    leg_copy.start()
     barrier = at_me.greet()
 
-    def local_copy(c, which):
-        block = w if which == 0 else at_me.across
-        return pltpu.make_async_copy(part_ref.at[block, c], part.at[c, which], q_sem.at[c, which])
+    observe(z, levels, model_ref, seen_ref, resid, lidar_acc, aod_acc)
+
+    c_hi[...], c_lo[...] = split2(cos_ref[...])
+    n_hi[...], n_lo[...] = split2(-sin_ref[...])
+    p_hi[...], p_lo[...] = split2(projection(lidar_ref[...], aod_ref[...], bins, levels, resid.shape[1]))
+    for spare in range(3 * z.pairs, z.rows):
+        q[pl.ds(spare, z.slots, stride=z.rows), :] = jnp.zeros((z.slots, LANES), f32)
+    over_lons = ((1,), (1,))
+
+    def analyse(k, carry):
+        courant_copy(k).wait()
+        for u in range(z.unroll):
+            i = k * z.unroll + u
+            fields = []
+            for which in range(2):
+                number = courant[which, i]
+                adjoint = product((p_hi[...], p_lo[...]), split2(resid[which * z.pairs + i]), ((0,), (0,)))
+                row = lax.broadcasted_iota(jnp.int32, adjoint.shape, 0)
+                for repeat in range(STEPS):
+                    below = jnp.where(row < channels - bins, pltpu.roll(adjoint, channels - bins, 0), 0.0)
+                    adjoint = adjoint + number * (below - adjoint)
+                fields.append(adjoint)
+            gap = jnp.zeros((half // 2 - (channels - half), fields[0].shape[1]), f32)
+            pieces = [field[:half] for field in fields]
+            for field in fields:
+                pieces.append(field[half:])
+                if gap.shape[0]:
+                    pieces.append(gap)
+            pieces.append(jnp.zeros((half, fields[0].shape[1]), f32))
+            both = split2(jnp.concatenate(pieces, 0))
+            real = product((c_hi[...], c_lo[...]), both, over_lons)
+            imag = product((n_hi[...], n_lo[...]), both, over_lons)
+            q[pl.ds(i, z.slots, stride=z.rows), :] = real[:, :LANES]
+            q[pl.ds(z.pairs + i, z.slots, stride=z.rows), :] = imag[:, :LANES]
+            q[pl.ds(2 * z.pairs + i, z.slots, stride=z.rows), :] = real[:, LANES:] + pltpu.roll(imag[:, LANES:], half, 1)
+        return carry
+
+    lax.fori_loop(0, steps, analyse, 0)
+
+    def block(wave, c):
+        return pl.ds(pl.multiple_of((wave * z.own + c) * z.group * z.rows, 8), z.group * z.rows)
+
+    def slab(c, spot):
+        return pl.ds(pl.multiple_of(((w * z.own + c) * z.group + spot) * z.rows, 8), z.rows)
 
     def core_copy(c, which):
-        block = at_me.partner if which == 0 else at_me.relay
-        return remote(part_ref.at[block, c], r1.at[c, which], c_send.at[c, which], c_recv.at[c, which], at_me.partner, b)
+        wave = at_me.partner if which == 0 else at_me.relay
+        return remote(q.at[block(wave, c)], r1.at[c, which], c_send.at[c, which], c_recv.at[c, which], at_me.partner, b)
 
     def across_copy(c):
-        return remote(part.at[c, 1], r2.at[c], x_send.at[c], x_recv.at[c], at_me.across, b)
+        return remote(q.at[block(at_me.across, c)], r2.at[c], x_send.at[c], x_recv.at[c], at_me.across, b)
 
     def third_copy(c, e):
-        return remote(part.at[c, 0, at_me.near_spot(e)], v3.at[at_me.spot, c], a3_send.at[c, e], a3_recv.at[c, e],
+        return remote(q.at[slab(c, at_me.near_spot(e))], v3.at[at_me.spot, c], a3_send.at[c, e], a3_recv.at[c, e],
                       w, at_me.near(e))
 
     def third_own(c):
-        return pltpu.make_async_copy(part.at[c, 0, at_me.spot], v3.at[at_me.spot, c], a3_send.at[c, 0])
+        return pltpu.make_async_copy(q.at[slab(c, at_me.spot)], v3.at[at_me.spot, c], a3_send.at[c, 0])
 
     def fourth_copy(c, d):
         return remote(send_u.at[c, at_me.peer(d)], out_ref.at[at_me.half, c, at_me.spot], a4_send.at[c, d],
@@ -725,35 +795,29 @@
     def begin(c, carry):
         for which in (1, 0):
             core_copy(c, which).start()
-            local_copy(c, which).start()
         return carry
 
     lax.fori_loop(0, z.own, begin, 0)
-    leg_copy.start()
+    leg_copy.wait()
 
     def phase(p, carry):
         @pl.when(p < z.own)
         def _():
-            local_copy(p, 1).wait()
             core_copy(p, 1).wait_recv()
-            part[p, 1] = part[p, 1] + r1[p, 1]
+            at = block(at_me.across, p)
+            q[at, :] = q[at, :] + r1[p, 1]
             across_copy(p).start()
 
         @pl.when((p >= LAG_ACROSS) & (p < z.own + LAG_ACROSS))
         def _():
             c = p - LAG_ACROSS
-            local_copy(c, 0).wait()
             core_copy(c, 0).wait_recv()
-            part[c, 0] = part[c, 0] + r1[c, 0]
             across_copy(c).wait_recv()
-            part[c, 0] = part[c, 0] + r2[c]
+            at = block(w, c)
+            q[at, :] = q[at, :] + r1[c, 0] + r2[c]
             for e in range(1, z.group):
                 third_copy(c, e).start()
             third_own(c).start()
-
-        @pl.when(p == LAG_ACROSS + LAG_SPREAD)
-        def _():
-            leg_copy.wait()
 
         @pl.when(p >= LAG_ACROSS + LAG_SPREAD)
         def _():
@@ -784,29 +848,43 @@
     lax.fori_loop(0, z.own, drain, 0)
 
 
-def transform_backward(z, part, legendre):
+def transform_backward(z, bins, model, seen, lidar, aod, cosine, sine, courant, legendre):
     anywhere = pl.BlockSpec(memory_space=pl.ANY)
+    in_vmem = pl.BlockSpec(memory_space=pltpu.VMEM)
     dma = pltpu.SemaphoreType.DMA
+    lats, channels, lons = courant.shape
+    rows = model.shape[1]
+    levels = channels // bins
     slab = (z.rows, LANES)
+    chunk = (z.group * z.rows, LANES)
+    table = pltpu.VMEM((z.slots, lons), bf16)
     return pl.pallas_call(
-        lambda *refs: second_kernel(z, *refs),
-        in_specs=[anywhere, anywhere],
+        lambda *refs: second_kernel(z, bins, *refs),
+        in_specs=[in_vmem] * 6 + [anywhere, anywhere],
         out_specs=anywhere,
         out_shape=jax.ShapeDtypeStruct((2, z.own, z.group, z.in_rows, LANES), f32),
         scratch_shapes=[
-            pltpu.VMEM((z.own, 2, z.group) + slab, f32),
-            pltpu.VMEM((z.own, 2, z.group) + slab, f32),
-            pltpu.VMEM((z.own, z.group) + slab, f32),
+            pltpu.VMEM(model.shape, f32),
+            pltpu.VMEM((lats * levels, lons), f32),
+            pltpu.VMEM((lats, lons), f32),
+            pltpu.VMEM((2, z.pairs, channels, lons), f32),
+            pltpu.VMEM((z.slots * z.rows, LANES), f32),
+            table, table, table, table,
+            pltpu.VMEM((rows, channels), bf16),
+            pltpu.VMEM((rows, channels), bf16),
+            pltpu.VMEM((z.own, 2) + chunk, f32),
+            pltpu.VMEM((z.own,) + chunk, f32),
             pltpu.VMEM((z.group, z.own) + slab, f32),
             pltpu.VMEM((z.own, z.half_lats, z.modes * z.bands), f32),
             pltpu.VMEM((z.half_lats, 2 * LANES), f32),
             pltpu.VMEM((z.own, z.bands, z.in_rows, LANES), f32),
-            dma(()), dma((z.own, 2)), dma((z.own, 2)), dma((z.own, 2)), dma((z.own,)), dma((z.own,)),
+            dma(()), dma((z.pairs // z.unroll,)), dma((z.own, 2)), dma((z.own, 2)), dma((z.own,)), dma((z.own,)),
             dma((z.own, z.group)), dma((z.own, z.group)), dma((z.own, z.bands)), dma((z.own, z.bands)),
         ],
         compiler_params=pltpu.CompilerParams(collective_id=1, has_side_effects=True, vmem_limit_bytes=VMEM_LIMIT),
         name="transform_backward",
-    )(part, legendre.reshape(z.own, z.group, *legendre.shape[1:]))
+    )(model, seen, lidar, aod, cosine, sine, courant.reshape(2, z.pairs, channels, lons),
+      legendre.reshape(z.own, z.group, *legendre.shape[1:]))
 
 
 def last_kernel(z, slabs_ref, control_ref, scale_ref, root_ref, out_ref, s_a, s_b, r_hi, r_lo):
@@ -847,87 +925,6 @@
         compiler_params=pltpu.CompilerParams(vmem_limit_bytes=VMEM_LIMIT),
         name="finish",
     )(slabs.reshape(2, z.waves, z.in_rows, LANES), control, scale, root)
-
-
-OBS_ROWS = 4
-
-
-def observation_kernel(levels, model_ref, seen_ref, out_ref, lidar_acc, aod_acc):
-    lats, rows, lons = model_ref.shape
-    cells = lats * levels
-    devices = seen_ref.shape[0] // GROUP_ROWS
-    slots = OBS_ROWS * seen_ref.shape[1]
-
-    def halves(x):
-        return jnp.concatenate(split2(x.T), 0)
-
-    lidar_field = halves(model_ref[:, :levels, :].reshape(cells, lons))
-    aod_field = halves(jnp.sum(model_ref[:, levels:, :], axis=1))
-    lidar_acc[...] = jnp.zeros_like(lidar_acc)
-    aod_acc[...] = jnp.zeros_like(aod_acc)
-    over_slots = ((1,), (1,))
-
-    def step(i, carry):
-        def row(k):
-            first = i * OBS_ROWS * GROUP_ROWS + k
-            return jnp.concatenate([seen_ref[pl.ds(first + r * GROUP_ROWS, 1), :] for r in range(OBS_ROWS)], 1)
-
-        column = row(0).astype(jnp.int32)
-        lat = column // lons
-        lon_hot = lax.broadcasted_iota(jnp.int32, (lons, slots), 0) == column - lat * lons
-        cell = lat * levels + row(1).astype(jnp.int32)
-        cell_hot = jnp.where(lax.broadcasted_iota(jnp.int32, (cells, slots), 0) == cell, 1.0, 0.0).astype(bf16)
-        lat_hot = jnp.where(lax.broadcasted_iota(jnp.int32, (lats, slots), 0) == lat, 1.0, 0.0).astype(bf16)
-        weight = row(4)
-
-        def one(field, hot, observed, acc):
-            picked = jnp.dot(field, hot, preferred_element_type=f32)
-            picked = picked[:lons] + picked[lons:]
-            resid = weight * (jnp.sum(jnp.where(lon_hot, picked, 0.0), axis=0, keepdims=True) - observed)
-            hi, lo = (jnp.where(lon_hot, part.astype(f32), 0.0).astype(bf16) for part in split2(resid))
-            acc[...] += lax.dot_general(hot, hi, (over_slots, ((), ())), preferred_element_type=f32) + lax.dot_general(
-                hot, lo, (over_slots, ((), ())), preferred_element_type=f32)
-
-        one(lidar_field, cell_hot, row(2), lidar_acc)
-        one(aod_field, lat_hot, row(3), aod_acc)
-        return carry
-
-    lax.fori_loop(0, devices // OBS_ROWS, step, 0)
-    out_ref[:, :levels, :] = lidar_acc[...].reshape(lats, levels, lons)
-    spread = jnp.broadcast_to(aod_acc[...][:, None, :], (lats, rows - levels, lons))
-    first = lax.broadcasted_iota(jnp.int32, spread.shape, 1) == 0
-    out_ref[:, levels:, :] = jnp.where(first, spread, 0.0)
-
-
-def observation_sums(model, seen, levels):
-    in_vmem = pl.BlockSpec(memory_space=pltpu.VMEM)
-    lats, rows, lons = model.shape
-    return pl.pallas_call(
-        lambda *refs: observation_kernel(levels, *refs),
-        in_specs=[in_vmem, in_vmem],
-        out_specs=in_vmem,
-        out_shape=jax.ShapeDtypeStruct(model.shape, f32),
-        scratch_shapes=[pltpu.VMEM((lats * levels, lons), f32), pltpu.VMEM((lats, lons), f32)],
-        compiler_params=pltpu.CompilerParams(vmem_limit_bytes=VMEM_LIMIT),
-        name="observation_sums",
-    )(model, seen)
-
-
-def projection(lidar_coef, aod_coef):
-    bins = lidar_coef.shape[0]
-    channels = aod_coef.shape[0]
-    levels_here = channels // bins
-    proj_rows = -(-(levels_here + 1) // 8) * 8
-    level_of = jnp.arange(channels, dtype=jnp.int32) // bins
-    in_level = jnp.arange(levels_here, dtype=jnp.int32)[:, None] == level_of[None, :]
-    return jnp.concatenate(
-        [
-            jnp.where(in_level, jnp.tile(lidar_coef, levels_here)[None, :], 0.0),
-            aod_coef[None, :],
-            jnp.zeros((proj_rows - levels_here - 1, channels), jnp.float32),
-        ],
-        axis=0,
-    )
 
 
 def fast_body(
@@ -950,18 +947,13 @@
     wave_count = lax.axis_size("wave")
     lats_here, channels, lon_here = courant.shape
     z = Sizes(modes_here, waves_here, width, lats_here, lax.axis_size("band"), wave_count)
-    lon_first = lax.axis_index("wave") * lon_here
-    factor = zonal_number.shape[0] ** (-0.5)
     bins = lidar_coef.shape[0]
-    levels_here = channels // bins
-    cosine, sine = trig_tables(zonal_number, lon_first, lon_here, lon_here * wave_count, factor)
-    proj = projection(lidar_coef, aod_coef)
+    lidar, aod = lidar_coef.reshape(1, -1), aod_coef.reshape(1, -1)
     observed = (obs_count, obs_column, obs_level, lidar_obs, aod_obs, obs_weight)
-    slabs, seen = transform_forward(z, control, spectral_scale, vertical_root, legendre, observed)
-    tracer, model = synthesis_settle(z, slabs, cosine, sine, courant, proj, bins)
-    resid = observation_sums(model, seen, levels_here)
-    part = settle_analysis(z, resid, courant, proj.T, cosine, sine, bins)
-    back = transform_backward(z, part, legendre)
+    slabs, seen, cosine, sine = transform_forward(
+        z, control, spectral_scale, vertical_root, legendre, zonal_number, lon_here, observed)
+    tracer, model = synthesis_settle(z, slabs, cosine, sine, courant, lidar, aod)
+    back = transform_backward(z, bins, model, seen, lidar, aod, cosine, sine, courant, legendre)
     return finish(z, back, control, spectral_scale, vertical_root), tracer
 
 

time: 283 us -> 257 us (0.908)
  Pallas kernels: 276 us -> 255 us
  other arithmetic: 3.24 us -> 0 us
    pallas_call x3 -> x1, Pallas kernels: 138 us -> 122 us  [transform_backward(): pl.pallas_call(lambda *refs: second_kernel(z, bins, *refs), in_specs=[in_...]
    pallas_call x1, Pallas kernels: 29.8 us -> 24.6 us  [synthesis_settle(): pl.pallas_call(lambda *refs: synthesis_kernel(z, bins, *refs), grid=(z.pa...]
where the time goes in v4:
time: 257 us
  Pallas kernels  255 us (99%)
    pallas_call x1, Pallas kernels, transform_backward(): pl.pallas_call(lambda *refs: second_kernel(z, bins, *refs), in_specs=[in_...  122 us
    pallas_call x1, Pallas kernels, transform_forward(): pl.pallas_call(lambda *refs: first_kernel(z, *refs), in_specs=[anywhere,...  100 us
    pallas_call x1, Pallas kernels, synthesis_settle(): pl.pallas_call(lambda *refs: synthesis_kernel(z, bins, *refs), grid=(z.pa...  24.6 us
    pallas_call x1, Pallas kernels, finish(): pl.pallas_call(lambda *refs: last_kernel(z, *refs), grid=(z.waves // GROU...  8.72 us

profile of v4, /device:TPU:0, one launch (start us, length us, event | category | flops | bytes accessed | tf_op | source)
XLA Modules:
  0.0 257.2 jit_solution(15147119162639989380)
XLA Ops:
  0.6 1.5 copy.16.refs_10_
  2.1 100.0 %transform_forward.1 = (f32[4,14,4,88,128]{4,3,2,1,0:T(8,128)}, f32[256,128]{1,0:T(8,128)}, f32[224,256]{1,0:T(8,128)}, f32[224,256]{1,0:T(8,128)}) custom-call(f32[32,56,192]{2,1,0:T(8,128)} %refs_1_.3, f32[32,56,192]{2,1,0:T(8,128)} %refs_2_.3, f32[96,96]{1,0:T(8,128)} %refs_3_.1, f32[14,4,448,256]{3,2,1,0:T(8,128)} %bitcast.9, s32[1,32]{1,0:T(1,128)} %refs_4_.1, ...), custom_call_target="tpu_custom_call" | custom-call | tf_op jit(solution)/shard_map/transform_forward/pallas_call | solution.py:531
  102.1 24.6 %synthesis_settle.1 = (f32[2,28,96,256]{3,2,1,0:T(8,128)}, f32[2,28,16,256]{3,2,1,0:T(8,128)}) custom-call(f32[19712,128]{1,0:T(8,128)} %bitcast.14, f32[224,256]{1,0:T(8,128)} %get-tuple-element.9.refs_1_.refs_4_, f32[224,256]{1,0:T(8,128)} %get-tuple-element.10.refs_2_.refs_5_, f32[2,28,96,256]{3,2,1,0:T(8,128)} %bitcast.11, f32[1,12]{1,0:T(1,128)} %bitcast.16, ...), custom_call_target="tpu_custom_call" | custom-call | tf_op jit(solution)/shard_map/synthesis_settle/pallas_call | solution.py:608
  126.8 121.7 %transform_backward.1 = f32[2,14,4,48,128]{4,3,2,1,0:T(8,128)} custom-call(f32[56,16,256]{2,1,0:T(8,128)} %bitcast.15, f32[256,128]{1,0:T(8,128)} %get-tuple-element.12.refs_1_, f32[1,12]{1,0:T(1,128)} %bitcast.17, f32[1,96]{1,0:T(1,128)} %bitcast.19, f32[224,256]{1,0:T(8,128)} %get-tuple-element.9.refs_1_.refs_4_, ...), custom_call_target="tpu_custom_call" | custom-call | tf_op jit(solution)/shard_map/transform_backward/pallas_call | solution.py:861
  248.4 8.7 %finish.1 = f32[32,56,192]{2,1,0:T(8,128)} custom-call(f32[2,56,48,128]{3,2,1,0:T(8,128)} %bitcast.13, f32[32,56,192]{2,1,0:T(8,128)} %refs_1_.3, f32[32,56,192]{2,1,0:T(8,128)} %refs_2_.3, f32[96,96]{1,0:T(8,128)} %refs_3_.1), custom_call_target="tpu_custom_call" | custom-call | tf_op jit(solution)/shard_map/finish/pallas_call | solution.py:915

commit v5 on v4

--- a/solution.py
+++ b/solution.py
@@ -214,7 +214,8 @@
 MESH_ID = pl.DeviceIdType.MESH
 bf16 = jnp.bfloat16
 f32 = jnp.float32
-VMEM_LIMIT = 63 * 1024 * 1024
+VMEM_LIMIT = 42 * 1024 * 1024
+SMALL_LIMIT = 16 * 1024 * 1024
 
 
 def split2(x):
@@ -531,9 +532,9 @@
     return pl.pallas_call(
         lambda *refs: first_kernel(z, *refs),
         in_specs=[anywhere, anywhere, in_vmem, anywhere] + [in_vmem] * 7,
-        out_specs=[anywhere, anywhere, in_vmem, in_vmem],
+        out_specs=[in_vmem, anywhere, in_vmem, in_vmem],
         out_shape=[
-            jax.ShapeDtypeStruct((z.wave_count, z.own, z.group, z.rows, LANES), f32),
+            pltpu.VMEM((z.wave_count, z.own, z.group, z.rows, LANES), f32),
             jax.ShapeDtypeStruct((devices * GROUP_ROWS, LANES), f32),
             jax.ShapeDtypeStruct((z.slots, lons), f32),
             jax.ShapeDtypeStruct((z.slots, lons), f32),
@@ -608,7 +609,7 @@
     tracer, model = pl.pallas_call(
         lambda *refs: synthesis_kernel(z, bins, *refs),
         grid=(z.pairs // z.unroll,),
-        in_specs=[whole(z.slots * z.rows, LANES), whole(z.slots, lons), whole(z.slots, lons), paired(z, channels, lons),
+        in_specs=[pl.BlockSpec(memory_space=pltpu.VMEM), whole(z.slots, lons), whole(z.slots, lons), paired(z, channels, lons),
                   whole(1, bins), whole(1, channels)],
         out_specs=[paired(z, channels, lons), paired(z, rows, lons)],
         out_shape=[
@@ -616,7 +617,7 @@
             jax.ShapeDtypeStruct((2, z.pairs, rows, lons), f32),
         ],
         scratch_shapes=[pltpu.VMEM((z.slots, lons), bf16)] * 4 + [pltpu.VMEM((rows, channels), bf16)] * 2,
-        compiler_params=pltpu.CompilerParams(vmem_limit_bytes=VMEM_LIMIT),
+        compiler_params=pltpu.CompilerParams(vmem_limit_bytes=SMALL_LIMIT),
         name="synthesis_settle",
     )(slabs.reshape(z.slots * z.rows, LANES), cosine, sine, courant.reshape(2, z.pairs, channels, lons), lidar, aod)
     return tracer.reshape(lats, channels, lons), model.reshape(lats, rows, lons)

time: 257 us -> 252 us (0.981)
  Pallas kernels: 255 us -> 245 us
  local copies, waits for them, and re-layouts: 1.46 us -> 5.86 us
    unnamed x0 -> x26, local copies, waits for them, and re-layouts: none -> 5.06 us
    pallas_call x1, Pallas kernels: 24.6 us -> 20.9 us  [synthesis_settle(): pl.pallas_call(lambda *refs: synthesis_kernel(z, bins, *refs), grid=(z.pa...]
where the time goes in v5:
time: 252 us
  Pallas kernels  245 us (97%)
  local copies, waits for them, and re-layouts  5.86 us (2%)
    pallas_call x1, Pallas kernels, transform_backward(): pl.pallas_call(lambda *refs: second_kernel(z, bins, *refs), in_specs=[in_...  120 us
    pallas_call x1, Pallas kernels, transform_forward(): pl.pallas_call(lambda *refs: first_kernel(z, *refs), in_specs=[anywhere,...  97.6 us
    pallas_call x1, Pallas kernels, synthesis_settle(): pl.pallas_call(lambda *refs: synthesis_kernel(z, bins, *refs), grid=(z.pa...  20.9 us
    pallas_call x1, Pallas kernels, finish(): pl.pallas_call(lambda *refs: last_kernel(z, *refs), grid=(z.waves // GROU...  6.21 us
    unnamed x26, local copies, waits for them, and re-layouts  5.06 us

profile of v5, /device:TPU:0, one launch (start us, length us, event | category | flops | bytes accessed | tf_op | source)
XLA Modules:
  0.0 251.7 jit_solution(12001170322279632484)
XLA Ops:
  0.6 0.8 copy.16.refs_10_
  1.4 0.0 copy-start.3
  1.4 0.8 copy-done.3
  2.2 0.0 copy-start.5
  2.2 0.7 copy-done.5
  3.0 0.0 copy-start.6
  3.0 0.7 copy-done.6
  3.7 0.0 copy-start.7
  3.7 0.7 copy-done.7
  4.4 0.0 copy-start.8
  4.4 0.7 copy-done.8
  5.1 0.0 copy-start.9
  5.1 0.7 copy-done.9
  5.8 0.0 copy-start.12
  5.8 0.7 copy-done.12
  6.5 0.0 copy-start
  6.5 0.0 copy-start.10
  6.5 0.0 copy-start.11
  6.5 97.6 %transform_forward.1 = (f32[4,14,4,88,128]{4,3,2,1,0:T(8,128)S(1)}, f32[256,128]{1,0:T(8,128)S(1)}, f32[224,256]{1,0:T(8,128)S(1)}, f32[224,256]{1,0:T(8,128)S(1)}) custom-call(f32[32,56,192]{2,1,0:T(8,128)} %refs_1_.3, f32[32,56,192]{2,1,0:T(8,128)} %refs_2_.3, f32[96,96]{1,0:T(8,128)S(1)} %copy-done.3, f32[14,4,448,256]{3,2,1,0:T(8,128)} %bitcast.18, ...), custom_call_target="tpu_custom_call" | custom-call | tf_op jit(solution)/shard_map/transform_forward/pallas_call | solution.py:532
  104.1 0.0 copy-done
  104.1 0.0 copy-done.10
  104.1 0.0 copy-done.11
  104.1 20.9 %synthesis_settle.1 = (f32[2,28,96,256]{3,2,1,0:T(8,128)}, f32[2,28,16,256]{3,2,1,0:T(8,128)S(1)}) custom-call(f32[19712,128]{1,0:T(8,128)S(1)} %bitcast.12, f32[224,256]{1,0:T(8,128)S(1)} %get-tuple-element.9.refs_1_.refs_4_, f32[224,256]{1,0:T(8,128)S(1)} %get-tuple-element.10.refs_2_.refs_5_, f32[2,28,96,256]{3,2,1,0:T(8,128)S(1)} %bitcast.9, ...), custom_call_target="tpu_custom_call" | custom-call | tf_op jit(solution)/shard_map/synthesis_settle/pallas_call | solution.py:609
  125.0 0.0 copy-start.1
  125.0 0.0 copy-start.2
  125.0 0.0 copy-start.4
  125.0 120.5 %transform_backward.1 = f32[2,14,4,48,128]{4,3,2,1,0:T(8,128)S(1)} custom-call(f32[56,16,256]{2,1,0:T(8,128)S(1)} %bitcast.13, f32[256,128]{1,0:T(8,128)S(1)} %get-tuple-element.12.refs_1_, f32[1,12]{1,0:T(1,128)S(1)} %bitcast.15, f32[1,96]{1,0:T(1,128)S(1)} %bitcast.17, f32[224,256]{1,0:T(8,128)S(1)} %get-tuple-element.9.refs_1_.refs_4_, ...), custom_call_target="tpu_custom_call" | custom-call | tf_op jit(solution)/shard_map/transform_backward/pallas_call | solution.py:862
  245.5 0.0 copy-done.1
  245.5 0.0 copy-done.2
  245.5 0.0 copy-done.4
  245.5 6.2 %finish.1 = f32[32,56,192]{2,1,0:T(8,128)} custom-call(f32[2,56,48,128]{3,2,1,0:T(8,128)S(1)} %bitcast.11, f32[32,56,192]{2,1,0:T(8,128)S(1)} %copy-done.1, f32[32,56,192]{2,1,0:T(8,128)S(1)} %copy-done.2, f32[96,96]{1,0:T(8,128)S(1)} %copy-done.4), custom_call_target="tpu_custom_call" | custom-call | tf_op jit(solution)/shard_map/finish/pallas_call | solution.py:916
Async XLA Ops:
  1.4 0.8 copy-start.3
  2.2 0.7 copy-start.5
  3.0 0.7 copy-start.6
  3.7 0.7 copy-start.7
  4.4 0.7 copy-start.8
  5.1 0.7 copy-start.9
  5.8 0.7 copy-start.12
  6.5 97.6 %copy-start = (f32[56,96,256]{2,1,0:T(8,128)S(1)}, f32[56,96,256]{2,1,0:T(8,128)}, u32[]{:S(2)}) copy-start(f32[56,96,256]{2,1,0:T(8,128)} %param.19) | copy-start | bytes 16515076
  6.5 97.6 %copy-start.10 = (f32[12]{0:T(128)S(1)}, f32[12]{0:T(128)}, u32[]{:S(2)}) copy-start(f32[12]{0:T(128)} %param.20) | copy-start | bytes 148
  6.5 97.6 %copy-start.11 = (f32[96]{0:T(128)S(1)}, f32[96]{0:T(128)}, u32[]{:S(2)}) copy-start(f32[96]{0:T(128)} %param.21) | copy-start | bytes 1156
  125.0 120.5 %copy-start.1 = (f32[32,56,192]{2,1,0:T(8,128)S(1)}, f32[32,56,192]{2,1,0:T(8,128)}, u32[]{:S(2)}) copy-start(f32[32,56,192]{2,1,0:T(8,128)} %refs_1_.3) | copy-start | bytes 4128772
  125.0 120.5 %copy-start.2 = (f32[32,56,192]{2,1,0:T(8,128)S(1)}, f32[32,56,192]{2,1,0:T(8,128)}, u32[]{:S(2)}) copy-start(f32[32,56,192]{2,1,0:T(8,128)} %refs_2_.3) | copy-start | bytes 4128772
  125.0 120.5 %copy-start.4 = (f32[96,96]{1,0:T(8,128)S(1)}, f32[96,96]{1,0:T(8,128)}, u32[]{:S(2)}) copy-start(f32[96,96]{1,0:T(8,128)} %refs_3_.1) | copy-start | bytes 110596

commit v6 on v5

--- a/solution.py
+++ b/solution.py
@@ -322,11 +322,12 @@
 LAG_SPREAD = 2
 LAG_ACROSS = 2
 GROUP_ROWS = 8
-UNROLL = 4
-
-
-def first_kernel(z, control_ref, scale_ref, root_ref, leg_ref, count_ref, column_ref, level_ref, lidar_ref, aod_ref,
-                 weight_ref, number_ref, out_ref, seen_ref, cos_ref, sin_ref, control, scale, s_a, s_b, send_u, recv_v, leg, y_a, y_b, send_y, packet,
+UNROLL = 7
+
+
+def first_kernel(z, control_hbm, scale_hbm, root_hbm, leg_ref, count_hbm, column_hbm, level_hbm, lidar_hbm, aod_hbm,
+                 weight_hbm, number_hbm, out_ref, seen_ref, cos_ref, sin_ref,
+                 root_ref, count_ref, column_ref, level_ref, lidar_ref, aod_ref, weight_ref, number_ref, s_sem, control, scale, s_a, s_b, send_u, recv_v, leg, y_a, y_b, send_y, packet,
                  leg_sem, in_sem, o_send, o_recv, a1_send, a1_recv, a2_send, a2_recv, x_send, x_recv, c_send, c_recv):
     at_me = Place(z)
     w, b = at_me.w, at_me.b
@@ -338,11 +339,21 @@
     me = w * z.bands + b
 
     def input_copy(i, which):
-        source, target = ((control_ref, control), (scale_ref, scale))[which]
+        source, target = ((control_hbm, control), (scale_hbm, scale))[which]
         return pltpu.make_async_copy(
             source.at[:, pl.ds(i * GROUP_ROWS, GROUP_ROWS), :], target.at[i], in_sem.at[i, which])
 
-    for i in range(groups):
+    small = [
+        pltpu.make_async_copy(source, target, s_sem.at[n])
+        for n, (source, target) in enumerate((
+            (root_hbm, root_ref), (count_hbm, count_ref), (column_hbm, column_ref), (level_hbm, level_ref),
+            (lidar_hbm, lidar_ref), (aod_hbm, aod_ref), (weight_hbm, weight_ref), (number_hbm, number_ref)))
+    ]
+    for which in range(2):
+        input_copy(0, which).start()
+    for copy in small:
+        copy.start()
+    for i in range(1, groups):
         for which in range(2):
             input_copy(i, which).start()
     leg_copy = pltpu.make_async_copy(
@@ -358,6 +369,8 @@
 
     lax.fori_loop(1, devices, greet, 0)
 
+    for copy in small:
+        copy.wait()
     counts = jnp.broadcast_to(count_ref[...], (devices, devices))
     diagonal = lax.broadcasted_iota(jnp.int32, counts.shape, 0) == lax.broadcasted_iota(jnp.int32, counts.shape, 1)
     counts = jnp.sum(jnp.where(diagonal, counts, 0).astype(f32), axis=1, keepdims=True)
@@ -397,7 +410,7 @@
         return pltpu.make_async_copy(send_u.at[c, at_me.spot], recv_v.at[b, c], a1_send.at[c, 0])
 
     def launch(c):
-        @pl.when(c % phases == 0)
+        @pl.when((c % phases == 0) & (c >= phases))
         def _():
             vertical(c // phases)
 
@@ -449,6 +462,7 @@
             send_y[c, s, 2 * z.pairs : 3 * z.pairs] = y_b[at : at + z.pairs] + pltpu.roll(
                 y_b[at + z.pairs : at + z.lats], quarter, 1)
 
+    vertical(0)
     pl.semaphore_wait(barrier, devices - 1)
     for c in range(min(AHEAD, z.own)):
         launch(c)
@@ -462,7 +476,10 @@
     lons = cos_ref.shape[1]
     lon_total = lons * z.wave_count
     longitude = lax.broadcasted_iota(jnp.int32, cos_ref.shape, 1) + w * lons
-    angle = (number_ref[...] * longitude % lon_total).astype(f32) * (2.0 * math.pi / lon_total)
+    across_lanes = jnp.broadcast_to(number_ref[...].astype(f32), (z.slots, z.slots))
+    same = lax.broadcasted_iota(jnp.int32, across_lanes.shape, 0) == lane_of(across_lanes.shape)
+    number = jnp.sum(jnp.where(same, across_lanes, 0.0), axis=1, keepdims=True).astype(jnp.int32)
+    angle = (number * longitude % lon_total).astype(f32) * (2.0 * math.pi / lon_total)
     factor = z.slots ** (-0.5)
     cos_ref[...] = jnp.cos(angle) * factor
     sin_ref[...] = jnp.sin(angle) * factor
@@ -522,16 +539,23 @@
     packet_own.wait()
 
 
+def in_hbm(x):
+    return pltpu.with_memory_space_constraint(x, pltpu.MemorySpace.HBM)
+
+
 def transform_forward(z, control, scale, root, legendre, numbers, lons, observed):
     in_vmem = pl.BlockSpec(memory_space=pltpu.VMEM)
     anywhere = pl.BlockSpec(memory_space=pl.ANY)
     dma = pltpu.SemaphoreType.DMA
     devices = z.wave_count * z.bands
     groups = z.waves // GROUP_ROWS
+    numbers = numbers.reshape(1, -1)
+    control, scale, root, numbers = (in_hbm(x) for x in (control, scale, root, numbers))
+    observed = [in_hbm(x) for x in observed]
     block = (groups, z.modes, GROUP_ROWS, z.width)
     return pl.pallas_call(
         lambda *refs: first_kernel(z, *refs),
-        in_specs=[anywhere, anywhere, in_vmem, anywhere] + [in_vmem] * 7,
+        in_specs=[pl.BlockSpec(memory_space=pltpu.MemorySpace.HBM)] * 11,
         out_specs=[in_vmem, anywhere, in_vmem, in_vmem],
         out_shape=[
             pltpu.VMEM((z.wave_count, z.own, z.group, z.rows, LANES), f32),
@@ -539,7 +563,8 @@
             jax.ShapeDtypeStruct((z.slots, lons), f32),
             jax.ShapeDtypeStruct((z.slots, lons), f32),
         ],
-        scratch_shapes=[
+        scratch_shapes=[pltpu.VMEM(x.shape, x.dtype) for x in (root, *observed, numbers)] + [
+            dma((8,)),
             pltpu.VMEM(block, f32),
             pltpu.VMEM(block, f32),
             pltpu.VMEM((z.modes * GROUP_ROWS, LANES), f32),
@@ -557,8 +582,7 @@
         ],
         compiler_params=pltpu.CompilerParams(collective_id=0, has_side_effects=True, vmem_limit_bytes=VMEM_LIMIT),
         name="transform_forward",
-    )(control, scale, root, legendre.reshape(z.own, z.group, *legendre.shape[1:]), *observed,
-      numbers.reshape(-1, 1))
+    )(control, scale, root, legendre.reshape(z.own, z.group, *legendre.shape[1:]), *observed, numbers)
 
 
 def synthesis_kernel(z, bins, slabs_ref, cos_ref, sin_ref, courant_ref, lidar_ref, aod_ref, out_ref, model_ref,

time: 252 us -> 243 us (0.964)
  local copies, waits for them, and re-layouts: 5.86 us -> 0.02 us
  Pallas kernels: 245 us -> 242 us
    unnamed x26 -> x12, local copies, waits for them, and re-layouts: 5.06 us -> 0.02 us
where the time goes in v6:
time: 243 us; the launch traced here: 242 us
  Pallas kernels  242 us (100%)
    pallas_call x1, Pallas kernels, transform_backward(): pl.pallas_call(lambda *refs: second_kernel(z, bins, *refs), in_specs=[in_...  120 us
    pallas_call x1, Pallas kernels, transform_forward(): pl.pallas_call(lambda *refs: first_kernel(z, *refs), in_specs=[pl.BlockSp...  96.5 us
    pallas_call x1, Pallas kernels, synthesis_settle(): pl.pallas_call(lambda *refs: synthesis_kernel(z, bins, *refs), grid=(z.pa...  18.8 us
    pallas_call x1, Pallas kernels, finish(): pl.pallas_call(lambda *refs: last_kernel(z, *refs), grid=(z.waves // GROU...  6.21 us

profile of v6, /device:TPU:0, one launch (start us, length us, event | category | flops | bytes accessed | tf_op | source)
XLA Modules:
  0.0 242.4 jit_solution(12505220681999632427)
XLA Ops:
  0.6 0.0 copy-start
  0.6 0.0 copy-start.4
  0.7 0.0 copy-start.5
  0.7 96.5 %transform_forward.1 = (f32[4,14,4,88,128]{4,3,2,1,0:T(8,128)S(1)}, f32[256,128]{1,0:T(8,128)S(1)}, f32[224,256]{1,0:T(8,128)S(1)}, f32[224,256]{1,0:T(8,128)S(1)}) custom-call(f32[32,56,192]{2,1,0:T(8,128)} %refs_1_.3, f32[32,56,192]{2,1,0:T(8,128)} %refs_2_.3, f32[96,96]{1,0:T(8,128)} %refs_3_.1, f32[14,4,448,256]{3,2,1,0:T(8,128)} %bitcast.18, ...), custom_call_target="tpu_custom_call" | custom-call | tf_op jit(solution)/shard_map/transform_forward/pallas_call | solution.py:556
  97.2 0.0 copy-done
  97.2 0.0 copy-done.4
  97.2 0.0 copy-done.5
  97.2 18.8 %synthesis_settle.1 = (f32[2,28,96,256]{3,2,1,0:T(8,128)}, f32[2,28,16,256]{3,2,1,0:T(8,128)S(1)}) custom-call(f32[19712,128]{1,0:T(8,128)S(1)} %bitcast.12, f32[224,256]{1,0:T(8,128)S(1)} %get-tuple-element.9.refs_1_.refs_4_, f32[224,256]{1,0:T(8,128)S(1)} %get-tuple-element.10.refs_2_.refs_5_, f32[2,28,96,256]{3,2,1,0:T(8,128)S(1)} %bitcast.9, ...), custom_call_target="tpu_custom_call" | custom-call | tf_op jit(solution)/shard_map/synthesis_settle/pallas_call | solution.py:633
  116.0 0.0 copy-start.1
  116.0 0.0 copy-start.2
  116.0 0.0 copy-start.3
  116.0 120.2 %transform_backward.1 = f32[2,14,4,48,128]{4,3,2,1,0:T(8,128)S(1)} custom-call(f32[56,16,256]{2,1,0:T(8,128)S(1)} %bitcast.13, f32[256,128]{1,0:T(8,128)S(1)} %get-tuple-element.12.refs_1_, f32[1,12]{1,0:T(1,128)S(1)} %bitcast.15, f32[1,96]{1,0:T(1,128)S(1)} %bitcast.17, f32[224,256]{1,0:T(8,128)S(1)} %get-tuple-element.9.refs_1_.refs_4_, ...), custom_call_target="tpu_custom_call" | custom-call | tf_op jit(solution)/shard_map/transform_backward/pallas_call | solution.py:886
  236.2 0.0 copy-done.1
  236.2 0.0 copy-done.2
  236.2 0.0 copy-done.3
  236.2 6.2 %finish.1 = f32[32,56,192]{2,1,0:T(8,128)} custom-call(f32[2,56,48,128]{3,2,1,0:T(8,128)S(1)} %bitcast.11, f32[32,56,192]{2,1,0:T(8,128)S(1)} %copy-done.1, f32[32,56,192]{2,1,0:T(8,128)S(1)} %copy-done.2, f32[96,96]{1,0:T(8,128)S(1)} %copy-done.3), custom_call_target="tpu_custom_call" | custom-call | tf_op jit(solution)/shard_map/finish/pallas_call | solution.py:940
Async XLA Ops:
  0.6 96.5 %copy-start = (f32[56,96,256]{2,1,0:T(8,128)S(1)}, f32[56,96,256]{2,1,0:T(8,128)}, u32[]{:S(2)}) copy-start(f32[56,96,256]{2,1,0:T(8,128)} %param.19) | copy-start | bytes 16515076
  0.6 96.5 %copy-start.4 = (f32[12]{0:T(128)S(1)}, f32[12]{0:T(128)}, u32[]{:S(2)}) copy-start(f32[12]{0:T(128)} %param.20) | copy-start | bytes 148
  0.7 96.5 %copy-start.5 = (f32[96]{0:T(128)S(1)}, f32[96]{0:T(128)}, u32[]{:S(2)}) copy-start(f32[96]{0:T(128)} %param.21) | copy-start | bytes 1156
  116.0 120.2 %copy-start.1 = (f32[32,56,192]{2,1,0:T(8,128)S(1)}, f32[32,56,192]{2,1,0:T(8,128)}, u32[]{:S(2)}) copy-start(f32[32,56,192]{2,1,0:T(8,128)} %refs_1_.3) | copy-start | bytes 4128772
  116.0 120.2 %copy-start.2 = (f32[32,56,192]{2,1,0:T(8,128)S(1)}, f32[32,56,192]{2,1,0:T(8,128)}, u32[]{:S(2)}) copy-start(f32[32,56,192]{2,1,0:T(8,128)} %refs_2_.3) | copy-start | bytes 4128772
  116.0 120.2 %copy-start.3 = (f32[96,96]{1,0:T(8,128)S(1)}, f32[96,96]{1,0:T(8,128)}, u32[]{:S(2)}) copy-start(f32[96,96]{1,0:T(8,128)} %refs_3_.1) | copy-start | bytes 110596
